TPU v7x, 32 devices: a whole 2x2x4 slice. The times are simulated.
32 devices in a mesh: groups: 2 (over y), pair: 4 (over z), tp: 4 (over x, core).
Axes of the slice: x: 2, y: 2, z: 4, core: 2. Of those that a mesh axis runs over, the one named last changes fastest.
Arguments:
- prompt_keys: bfloat16 [8, 1536, 8, 128], P(('groups', 'pair'), None, 'tp'), parts along dimension 0, may hold values from -6 to 6
- prompt_values: bfloat16 [8, 1536, 8, 128], P(('groups', 'pair'), None, 'tp'), parts along dimension 0, may hold values from -6 to 6
- span_queries: bfloat16 [8, 512, 64, 128], P(('groups', 'pair'), None, 'tp'), parts along dimension 0, may hold values from -1024 to 1024
- span_keys: bfloat16 [8, 512, 8, 128], P(('groups', 'pair'), None, 'tp'), parts along dimension 0, may hold values from -6 to 6
- span_values: bfloat16 [8, 512, 8, 128], P(('groups', 'pair'), None, 'tp'), parts along dimension 0, may hold values from -6 to 6
- prefill_residual: bfloat16 [8, 512, 8192], P(('groups', 'pair'), None, 'tp'), parts along dimension 0, may hold values from -8 to 8
- decode_queries: bfloat16 [8, 2, 32, 64, 128], P(('groups', 'pair'), None, None, 'tp'), parts along dimension 0, may hold values from -1024 to 1024
- decode_keys: bfloat16 [8, 2, 32, 8, 128], P(('groups', 'pair'), None, None, 'tp'), parts along dimension 0, may hold values from -16 to 16
- decode_values: bfloat16 [8, 2, 32, 8, 128], P(('groups', 'pair'), None, None, 'tp'), parts along dimension 0, may hold values from -6 to 6
- decode_residual: bfloat16 [8, 2, 32, 8192], P(('groups', 'pair'), None, None, 'tp'), parts along dimension 0, may hold values from -8 to 8
- cursor: int32 [8, 32], P(('groups', 'pair')), parts along dimension 0, may hold values from 1024 to 2048
- norm_gain: bfloat16 [8192], P('tp'), may hold values from 0.25 to 1.75
Outputs:
- prefill_normed: bfloat16 [8, 512, 8192], P(('groups', 'pair'), None, 'tp'), parts along dimension 0
- handed_keys: bfloat16 [8, 2048, 8, 128], P(('groups', 'pair'), None, 'tp'), parts along dimension 0
- handed_values: bfloat16 [8, 2048, 8, 128], P(('groups', 'pair'), None, 'tp'), parts along dimension 0
- decode_normed: bfloat16 [8, 2, 32, 8192], P(('groups', 'pair'), None, None, 'tp'), parts along dimension 0
There are 2 independent parts, one for each index of `groups`. A program takes and returns all parts, laid end to end along the dimension named above; an argument that names none is the same for every part. Nothing has to cross between parts.
All inputs are finite; a program needn't handle non-finite values.
Results may differ from a plain program's by a relative error of at most 0.0034.
Values may be sent and summed in bfloat16 or wider, within the bound.
No kernel may reach another device: no remote copies, remote signals or barrier semaphores. Data moves between devices by JAX's collectives and lax.ppermute only.
A program may use at most 128 MiB of HBM per device.

v0:
```python
import jax
import jax.numpy as jnp
from jax import lax
from jax.sharding import PartitionSpec as P

D = 8192


epsilon = 1e-05


def from_behind(value, axis, steps):
    count = lax.axis_size(axis)
    pairs = [(source, (source + steps) % count) for source in range(count)]
    return lax.ppermute(value, axis, pairs)


def prefill_attention(queries, keys_one, values_one):
    span_len = queries.shape[0]
    query_heads = queries.shape[1]
    head_size = queries.shape[2]
    key_heads = keys_one.shape[1]
    positions = keys_one.shape[0]
    groups = query_heads // key_heads
    score_scale = head_size ** (-0.5)
    row_index = lax.broadcasted_iota(jnp.int32, (span_len, positions), 0) + (positions - span_len)
    col_index = lax.broadcasted_iota(jnp.int32, (span_len, positions), 1)
    visible = col_index <= row_index

    def one_head(head_index):
        query = lax.dynamic_index_in_dim(queries, head_index, 1, keepdims=False)
        key_head = lax.dynamic_index_in_dim(keys_one, head_index // groups, 1, keepdims=False)
        value_head = lax.dynamic_index_in_dim(values_one, head_index // groups, 1, keepdims=False)
        scores = (
            lax.dot_general(
                query, key_head, (((1,), (1,)), ((), ())), preferred_element_type=jnp.float32
            )
            * score_scale
        )
        scores = jnp.where(visible, scores, -jnp.inf)
        row_max = jnp.max(scores, axis=1, keepdims=True)
        scaled = jnp.exp(scores - row_max)
        denominator = jnp.sum(scaled, axis=1, keepdims=True)
        weights = scaled.astype(jnp.bfloat16)
        return jnp.dot(weights, value_head, preferred_element_type=jnp.float32) / denominator

    per_head = lax.map(one_head, jnp.arange(query_heads, dtype=jnp.int32))
    return jnp.transpose(per_head, (1, 0, 2)).reshape(span_len, query_heads * head_size)


def decode_attention(queries, own_keys, own_values, reach_count, keys_one, values_one):
    steps_count, row_count, query_heads, head_size = queries.shape
    key_heads = keys_one.shape[1]
    positions = keys_one.shape[0]
    groups = query_heads // key_heads
    score_scale = head_size ** (-0.5)
    grouped = queries.reshape(steps_count, row_count, key_heads, groups, head_size)
    far_scores = (
        jnp.einsum("trkgd,skd->trkgs", grouped, keys_one, preferred_element_type=jnp.float32)
        * score_scale
    )
    reach = lax.broadcasted_iota(jnp.int32, (row_count, positions), 1) < reach_count[:, None]
    far_scores = jnp.where(reach[None, :, None, None, :], far_scores, -jnp.inf)
    own_scores = (
        jnp.einsum("trkgd,urkd->trkgu", grouped, own_keys, preferred_element_type=jnp.float32)
        * score_scale
    )
    earlier = lax.broadcasted_iota(
        jnp.int32, (steps_count, steps_count), 1
    ) <= lax.broadcasted_iota(jnp.int32, (steps_count, steps_count), 0)
    own_scores = jnp.where(earlier[:, None, None, None, :], own_scores, -jnp.inf)
    row_max = jnp.maximum(jnp.max(far_scores, axis=4), jnp.max(own_scores, axis=4))[..., None]
    far_expon = jnp.exp(far_scores - row_max)
    own_expon = jnp.exp(own_scores - row_max)
    denominator = jnp.sum(far_expon, axis=4) + jnp.sum(own_expon, axis=4)
    attended = jnp.einsum(
        "trkgs,skd->trkgd",
        far_expon.astype(jnp.bfloat16),
        values_one,
        preferred_element_type=jnp.float32,
    )
    attended = attended + jnp.einsum(
        "trkgu,urkd->trkgd",
        own_expon.astype(jnp.bfloat16),
        own_values,
        preferred_element_type=jnp.float32,
    )
    attended = attended / denominator[..., None]
    return attended.reshape(steps_count, row_count, query_heads * head_size)


def local(
    prompt_keys,
    prompt_values,
    span_queries,
    span_keys,
    span_values,
    prefill_residual,
    decode_queries,
    decode_keys,
    decode_values,
    decode_residual,
    cursor,
    norm_gain,
):
    halfway = lax.axis_size("pair") // 2
    keys_all = jnp.concatenate([prompt_keys, span_keys], axis=1)
    values_all = jnp.concatenate([prompt_values, span_values], axis=1)
    handed_keys, handed_values = from_behind((keys_all, values_all), "pair", halfway)
    gain_wide = norm_gain.astype(jnp.float32)
    attended = prefill_attention(span_queries[0], keys_all[0], values_all[0])
    prefill_hidden = attended + prefill_residual[0].astype(jnp.float32)
    prefill_squares = lax.psum(jnp.sum(prefill_hidden * prefill_hidden, axis=1), "tp")
    prefill_normed = (
        prefill_hidden * lax.rsqrt(prefill_squares[:, None] / D + epsilon) * gain_wide
    ).astype(jnp.bfloat16)
    remote = from_behind((decode_queries, decode_keys, decode_values, cursor), "pair", halfway)
    remote_mixed = decode_attention(
        remote[0][0], remote[1][0], remote[2][0], remote[3][0], keys_all[0], values_all[0]
    )
    decode_mixed = from_behind(remote_mixed, "pair", halfway)
    decode_hidden = decode_mixed + decode_residual[0].astype(jnp.float32)
    decode_squares = lax.psum(jnp.sum(decode_hidden * decode_hidden, axis=2), "tp")
    decode_normed = (
        decode_hidden * lax.rsqrt(decode_squares[..., None] / D + epsilon) * gain_wide
    ).astype(jnp.bfloat16)
    return (prefill_normed[None], handed_keys, handed_values, decode_normed[None])


def solution(mesh):
    placed = (
        P(("groups", "pair"), None, "tp", None),
        P(("groups", "pair"), None, "tp", None),
        P(("groups", "pair"), None, "tp", None),
        P(("groups", "pair"), None, "tp", None),
        P(("groups", "pair"), None, "tp", None),
        P(("groups", "pair"), None, "tp"),
        P(("groups", "pair"), None, None, "tp", None),
        P(("groups", "pair"), None, None, "tp", None),
        P(("groups", "pair"), None, None, "tp", None),
        P(("groups", "pair"), None, None, "tp"),
        P(("groups", "pair"), None),
        P("tp"),
    )
    return jax.shard_map(
        local,
        mesh=mesh,
        in_specs=placed,
        out_specs=(
            P(("groups", "pair"), None, "tp"),
            P(("groups", "pair"), None, "tp", None),
            P(("groups", "pair"), None, "tp", None),
            P(("groups", "pair"), None, None, "tp"),
        ),
        check_vma=False,
    )
```

profile of v0, /device:TPU:0, one launch (start us, length us, event | category | flops | bytes accessed | tf_op | source)
XLA Modules:
  0.0 238.9 jit_solution(7475198451881749116)
XLA Ops:
  0.6 4.1 %collective-permute-start.2 = (s32[1,32]{1,0:T(1,128)}, s32[1,32]{1,0:T(1,128)S(1)}, u32[]{:S(2)}, u32[]{:S(2)}) collective-permute-start(s32[1,32]{1,0:T(1,128)} %param.24), channel_id=1, source_target_pairs={{0,8},{4,12},{8,0},{12,4},{1,9},{5,13},{9,1},{13,5},{2,10},{6,14},... | collective-permute-start | bytes 392 | tf_op jit(solution)/shard_map/ppermute | solution.py:15
  5.6 2.9 %collective-permute-start.4 = (bf16[1,2,32,2,128]{4,1,3,2,0:T(2,128)(2,1)S(1)}, bf16[1,2,32,2,128]{4,1,3,2,0:T(2,128)(2,1)S(1)}, u32[]{:S(2)}, u32[]{:S(2)}) collective-permute-start(bf16[1,2,32,2,128]{4,1,3,2,0:T(2,128)(2,1)S(1)} %copy.72), channel_id=1, source_target_pairs={{0,8},{4,12},{8,0},{12,4},{1,9},{5,13},{9,1},{13,5},{2,10},{6,14},... | collective-permute-start | bytes 98312 | tf_op jit(solution)/shard_map/ppermute | solution.py:15
  16.2 2.8 %collective-permute-start.1 = (bf16[1,2048,2,128]{3,1,2,0:T(8,128)(2,1)}, bf16[1,2048,2,128]{3,1,2,0:T(8,128)(2,1)}, u32[]{:S(2)}, u32[]{:S(2)}) collective-permute-start(bf16[1,2048,2,128]{3,1,2,0:T(8,128)(2,1)} %copy_dynamic-update-slice_fusion.2), channel_id=1, source_target_pairs={{0,8},{4,12},{8,0},{12,4},{1,9},{5,13},{9,1},{13,5},{2,10},{6,14},... | collective-permute-start | bytes 3145736 | tf_op jit(solution)/shard_map/ppermute | solution.py:15
  21.0 156.9 %while.13 = (s32[]{:T(128)}, f32[16,512,128]{2,1,0:T(8,128)}, s32[16]{0:T(128)S(1)}, bf16[512,16,128]{2,0,1:T(8,128)(2,1)}, bf16[2048,2,128]{2,0,1:T(8,128)(2,1)...) while((s32[]{:T(128)}, f32[16,512,128]{2,1,0:T(8,128)}, ...), condition=%wide.region_3.4_spmd.clone, body=%wide.region_0.3_spmd.clone.sunk | while | flops 545324032 | bytes 14037870 | solution.py:47
  28.2 2.5 %fusion.75 = f32[16,512,128]{2,1,0:T(8,128)} fusion(f32[16,512,128]{2,1,0:T(8,128)} %get-tuple-element.219, s32[]{:T(128)} %get-tuple-element.218, f32[512,2048]{1,0:T(8,128)S(1)} %get-tuple-element.202, f32[512]{0:T(512)S(1)} %get-tuple-element.203, bf16[2048,2,128]{2,0,1:T(8,128)(2,1)} %get-tuple-element.237, s32[]{:T(128)S(6)} %select_n.65, ...), kind=kOutput, calls=%fused_computation.10.clone.1 | convolution fusion | flops 270598144 | bytes 4985348 | tf_op jit(solution)/shard_map/while/body/eval_jaxpr/dot_general | solution.py:45
  38.0 2.5 %fusion.75 = f32[16,512,128]{2,1,0:T(8,128)} fusion(f32[16,512,128]{2,1,0:T(8,128)} %get-tuple-element.219, s32[]{:T(128)} %get-tuple-element.218, f32[512,2048]{1,0:T(8,128)S(1)} %get-tuple-element.202, f32[512]{0:T(512)S(1)} %get-tuple-element.203, bf16[2048,2,128]{2,0,1:T(8,128)(2,1)} %get-tuple-element.237, s32[]{:T(128)S(6)} %select_n.65, ...), kind=kOutput, calls=%fused_computation.10.clone.1 | convolution fusion | flops 270598144 | bytes 4985348 | tf_op jit(solution)/shard_map/while/body/eval_jaxpr/dot_general | solution.py:45
  47.9 2.6 %fusion.75 = f32[16,512,128]{2,1,0:T(8,128)} fusion(f32[16,512,128]{2,1,0:T(8,128)} %get-tuple-element.219, s32[]{:T(128)} %get-tuple-element.218, f32[512,2048]{1,0:T(8,128)S(1)} %get-tuple-element.202, f32[512]{0:T(512)S(1)} %get-tuple-element.203, bf16[2048,2,128]{2,0,1:T(8,128)(2,1)} %get-tuple-element.237, s32[]{:T(128)S(6)} %select_n.65, ...), kind=kOutput, calls=%fused_computation.10.clone.1 | convolution fusion | flops 270598144 | bytes 4985348 | tf_op jit(solution)/shard_map/while/body/eval_jaxpr/dot_general | solution.py:45
  57.7 2.6 %fusion.75 = f32[16,512,128]{2,1,0:T(8,128)} fusion(f32[16,512,128]{2,1,0:T(8,128)} %get-tuple-element.219, s32[]{:T(128)} %get-tuple-element.218, f32[512,2048]{1,0:T(8,128)S(1)} %get-tuple-element.202, f32[512]{0:T(512)S(1)} %get-tuple-element.203, bf16[2048,2,128]{2,0,1:T(8,128)(2,1)} %get-tuple-element.237, s32[]{:T(128)S(6)} %select_n.65, ...), kind=kOutput, calls=%fused_computation.10.clone.1 | convolution fusion | flops 270598144 | bytes 4985348 | tf_op jit(solution)/shard_map/while/body/eval_jaxpr/dot_general | solution.py:45
  67.5 2.5 %fusion.75 = f32[16,512,128]{2,1,0:T(8,128)} fusion(f32[16,512,128]{2,1,0:T(8,128)} %get-tuple-element.219, s32[]{:T(128)} %get-tuple-element.218, f32[512,2048]{1,0:T(8,128)S(1)} %get-tuple-element.202, f32[512]{0:T(512)S(1)} %get-tuple-element.203, bf16[2048,2,128]{2,0,1:T(8,128)(2,1)} %get-tuple-element.237, s32[]{:T(128)S(6)} %select_n.65, ...), kind=kOutput, calls=%fused_computation.10.clone.1 | convolution fusion | flops 270598144 | bytes 4985348 | tf_op jit(solution)/shard_map/while/body/eval_jaxpr/dot_general | solution.py:45
  77.3 2.6 %fusion.75 = f32[16,512,128]{2,1,0:T(8,128)} fusion(f32[16,512,128]{2,1,0:T(8,128)} %get-tuple-element.219, s32[]{:T(128)} %get-tuple-element.218, f32[512,2048]{1,0:T(8,128)S(1)} %get-tuple-element.202, f32[512]{0:T(512)S(1)} %get-tuple-element.203, bf16[2048,2,128]{2,0,1:T(8,128)(2,1)} %get-tuple-element.237, s32[]{:T(128)S(6)} %select_n.65, ...), kind=kOutput, calls=%fused_computation.10.clone.1 | convolution fusion | flops 270598144 | bytes 4985348 | tf_op jit(solution)/shard_map/while/body/eval_jaxpr/dot_general | solution.py:45
  87.1 2.5 %fusion.75 = f32[16,512,128]{2,1,0:T(8,128)} fusion(f32[16,512,128]{2,1,0:T(8,128)} %get-tuple-element.219, s32[]{:T(128)} %get-tuple-element.218, f32[512,2048]{1,0:T(8,128)S(1)} %get-tuple-element.202, f32[512]{0:T(512)S(1)} %get-tuple-element.203, bf16[2048,2,128]{2,0,1:T(8,128)(2,1)} %get-tuple-element.237, s32[]{:T(128)S(6)} %select_n.65, ...), kind=kOutput, calls=%fused_computation.10.clone.1 | convolution fusion | flops 270598144 | bytes 4985348 | tf_op jit(solution)/shard_map/while/body/eval_jaxpr/dot_general | solution.py:45
  96.9 2.5 %fusion.75 = f32[16,512,128]{2,1,0:T(8,128)} fusion(f32[16,512,128]{2,1,0:T(8,128)} %get-tuple-element.219, s32[]{:T(128)} %get-tuple-element.218, f32[512,2048]{1,0:T(8,128)S(1)} %get-tuple-element.202, f32[512]{0:T(512)S(1)} %get-tuple-element.203, bf16[2048,2,128]{2,0,1:T(8,128)(2,1)} %get-tuple-element.237, s32[]{:T(128)S(6)} %select_n.65, ...), kind=kOutput, calls=%fused_computation.10.clone.1 | convolution fusion | flops 270598144 | bytes 4985348 | tf_op jit(solution)/shard_map/while/body/eval_jaxpr/dot_general | solution.py:45
  106.7 2.5 %fusion.75 = f32[16,512,128]{2,1,0:T(8,128)} fusion(f32[16,512,128]{2,1,0:T(8,128)} %get-tuple-element.219, s32[]{:T(128)} %get-tuple-element.218, f32[512,2048]{1,0:T(8,128)S(1)} %get-tuple-element.202, f32[512]{0:T(512)S(1)} %get-tuple-element.203, bf16[2048,2,128]{2,0,1:T(8,128)(2,1)} %get-tuple-element.237, s32[]{:T(128)S(6)} %select_n.65, ...), kind=kOutput, calls=%fused_computation.10.clone.1 | convolution fusion | flops 270598144 | bytes 4985348 | tf_op jit(solution)/shard_map/while/body/eval_jaxpr/dot_general | solution.py:45
  116.5 2.5 %fusion.75 = f32[16,512,128]{2,1,0:T(8,128)} fusion(f32[16,512,128]{2,1,0:T(8,128)} %get-tuple-element.219, s32[]{:T(128)} %get-tuple-element.218, f32[512,2048]{1,0:T(8,128)S(1)} %get-tuple-element.202, f32[512]{0:T(512)S(1)} %get-tuple-element.203, bf16[2048,2,128]{2,0,1:T(8,128)(2,1)} %get-tuple-element.237, s32[]{:T(128)S(6)} %select_n.65, ...), kind=kOutput, calls=%fused_computation.10.clone.1 | convolution fusion | flops 270598144 | bytes 4985348 | tf_op jit(solution)/shard_map/while/body/eval_jaxpr/dot_general | solution.py:45
  126.3 2.5 %fusion.75 = f32[16,512,128]{2,1,0:T(8,128)} fusion(f32[16,512,128]{2,1,0:T(8,128)} %get-tuple-element.219, s32[]{:T(128)} %get-tuple-element.218, f32[512,2048]{1,0:T(8,128)S(1)} %get-tuple-element.202, f32[512]{0:T(512)S(1)} %get-tuple-element.203, bf16[2048,2,128]{2,0,1:T(8,128)(2,1)} %get-tuple-element.237, s32[]{:T(128)S(6)} %select_n.65, ...), kind=kOutput, calls=%fused_computation.10.clone.1 | convolution fusion | flops 270598144 | bytes 4985348 | tf_op jit(solution)/shard_map/while/body/eval_jaxpr/dot_general | solution.py:45
  136.2 2.5 %fusion.75 = f32[16,512,128]{2,1,0:T(8,128)} fusion(f32[16,512,128]{2,1,0:T(8,128)} %get-tuple-element.219, s32[]{:T(128)} %get-tuple-element.218, f32[512,2048]{1,0:T(8,128)S(1)} %get-tuple-element.202, f32[512]{0:T(512)S(1)} %get-tuple-element.203, bf16[2048,2,128]{2,0,1:T(8,128)(2,1)} %get-tuple-element.237, s32[]{:T(128)S(6)} %select_n.65, ...), kind=kOutput, calls=%fused_computation.10.clone.1 | convolution fusion | flops 270598144 | bytes 4985348 | tf_op jit(solution)/shard_map/while/body/eval_jaxpr/dot_general | solution.py:45
  145.9 2.5 %fusion.75 = f32[16,512,128]{2,1,0:T(8,128)} fusion(f32[16,512,128]{2,1,0:T(8,128)} %get-tuple-element.219, s32[]{:T(128)} %get-tuple-element.218, f32[512,2048]{1,0:T(8,128)S(1)} %get-tuple-element.202, f32[512]{0:T(512)S(1)} %get-tuple-element.203, bf16[2048,2,128]{2,0,1:T(8,128)(2,1)} %get-tuple-element.237, s32[]{:T(128)S(6)} %select_n.65, ...), kind=kOutput, calls=%fused_computation.10.clone.1 | convolution fusion | flops 270598144 | bytes 4985348 | tf_op jit(solution)/shard_map/while/body/eval_jaxpr/dot_general | solution.py:45
  155.7 2.5 %fusion.75 = f32[16,512,128]{2,1,0:T(8,128)} fusion(f32[16,512,128]{2,1,0:T(8,128)} %get-tuple-element.219, s32[]{:T(128)} %get-tuple-element.218, f32[512,2048]{1,0:T(8,128)S(1)} %get-tuple-element.202, f32[512]{0:T(512)S(1)} %get-tuple-element.203, bf16[2048,2,128]{2,0,1:T(8,128)(2,1)} %get-tuple-element.237, s32[]{:T(128)S(6)} %select_n.65, ...), kind=kOutput, calls=%fused_computation.10.clone.1 | convolution fusion | flops 270598144 | bytes 4985348 | tf_op jit(solution)/shard_map/while/body/eval_jaxpr/dot_general | solution.py:45
  165.5 2.5 %fusion.75 = f32[16,512,128]{2,1,0:T(8,128)} fusion(f32[16,512,128]{2,1,0:T(8,128)} %get-tuple-element.219, s32[]{:T(128)} %get-tuple-element.218, f32[512,2048]{1,0:T(8,128)S(1)} %get-tuple-element.202, f32[512]{0:T(512)S(1)} %get-tuple-element.203, bf16[2048,2,128]{2,0,1:T(8,128)(2,1)} %get-tuple-element.237, s32[]{:T(128)S(6)} %select_n.65, ...), kind=kOutput, calls=%fused_computation.10.clone.1 | convolution fusion | flops 270598144 | bytes 4985348 | tf_op jit(solution)/shard_map/while/body/eval_jaxpr/dot_general | solution.py:45
  175.3 2.5 %fusion.75 = f32[16,512,128]{2,1,0:T(8,128)} fusion(f32[16,512,128]{2,1,0:T(8,128)} %get-tuple-element.219, s32[]{:T(128)} %get-tuple-element.218, f32[512,2048]{1,0:T(8,128)S(1)} %get-tuple-element.202, f32[512]{0:T(512)S(1)} %get-tuple-element.203, bf16[2048,2,128]{2,0,1:T(8,128)(2,1)} %get-tuple-element.237, s32[]{:T(128)S(6)} %select_n.65, ...), kind=kOutput, calls=%fused_computation.10.clone.1 | convolution fusion | flops 270598144 | bytes 4985348 | tf_op jit(solution)/shard_map/while/body/eval_jaxpr/dot_general | solution.py:45
  179.6 5.8 %fusion.26 = (f32[2,32,2,8]{1,3,0,2:T(8,128)S(1)}, f32[2,2048,2,32,8]{1,3,4,2,0:T(8,128)}) fusion(pred[32,2048]{1,0:T(8,128)(4,1)S(1)} %iota_compare_fusion.1, bf16[2,32,2,8,128]{4,3,2,1,0:T(8,128)(2,1)S(1)} %bitcast.111, bf16[1,2048,2,128]{3,1,2,0:T(8,128)(2,1)} %copy_dynamic-update-slice_fusion.3), kind=kOutput, calls=%fused_computation.23 | convolution fusion | flops 543161344 | bytes 9768960 | tf_op jit(solution)/shard_map/trkgd,skd->trkgs/dot_general | solution.py:59
  185.5 4.5 %fusion.24 = f32[2,32,2,8]{1,3,0,2:T(8,128)S(1)} fusion(f32[2,2048,2,32,8]{1,3,4,2,0:T(8,128)} %get-tuple-element.154, f32[2,32,2,8]{1,3,0,2:T(8,128)S(1)} %max.7, pred[32,2048]{1,0:T(8,128)(4,1)S(1)} %iota_compare_fusion.1), kind=kLoop, calls=%fused_computation.21 | loop fusion | flops 8387584 | bytes 8462336 | tf_op jit(solution)/shard_map/reduce_sum | solution.py:75
  190.7 5.2 %fusion.46 = f32[2,32,2,8,128]{4,1,3,0,2:T(8,128)S(1)} fusion(f32[2,2048,2,32,8]{1,3,4,2,0:T(8,128)} %get-tuple-element.154, f32[2,32,2,8]{1,3,0,2:T(8,128)S(1)} %max.7, pred[32,2048]{1,0:T(8,128)(4,1)S(1)} %iota_compare_fusion.1, bf16[1,2048,2,128]{3,1,2,0:T(8,128)(2,1)} %copy_dynamic-update-slice_fusion.2, f32[32,2,2,8,128]{4,3,2,1,0:T(8,128)S(1)} %fusion.56, ...), kind=kOutput, calls=%fused_computation.43 | convolution fusion | flops 545521664 | bytes 10559488 | tf_op jit(solution)/shard_map/trkgs,skd->trkgd/dot_general | solution.py:76
  196.3 2.9 %collective-permute-start.6 = (f32[2,32,2048]{2,1,0:T(8,128)S(1)}, f32[2,32,2048]{2,1,0:T(8,128)S(1)}, u32[]{:S(2)}, u32[]{:S(2)}) collective-permute-start(f32[2,32,2048]{2,1,0:T(8,128)S(1)} %reshape.78), channel_id=1, source_target_pairs={{0,8},{4,12},{8,0},{12,4},{1,9},{5,13},{9,1},{13,5},{2,10},{6,14},... | collective-permute-start | bytes 1572872 | tf_op jit(solution)/shard_map/ppermute | solution.py:15
  199.8 2.9 %copy.86 = f32[64,8,16,128]{3,2,1,0:T(8,128)} copy(f32[64,8,16,128]{3,1,2,0:T(8,128)S(1)} %convert_bitcast_fusion) | data formatting | bytes 8388608
  202.6 6.6 %copy.69 = f32[512,16,128]{2,1,0:T(8,128)} copy(f32[512,16,128]{2,0,1:T(8,128)} %bitcast.3) | data formatting | bytes 8388608 | tf_op jit(solution)/shard_map/transpose | solution.py:48
  209.2 4.9 %reshape.77 = f32[1,512,2048]{2,1,0:T(8,128)} reshape(f32[512,16,128]{2,1,0:T(8,128)} %copy.69) | data formatting | bytes 8388608 | tf_op jit(solution)/shard_map/reshape | solution.py:48
  214.1 5.0 %fusion.31 = f32[512]{0:T(512)S(1)} fusion(f32[512,16,128]{2,1,0:T(8,128)} %bitcast.109, f32[16,512,128]{2,1,0:T(8,128)} %get-tuple-element.94), kind=kLoop, calls=%fused_computation.31 | loop fusion | flops 3145216 | bytes 8390656 | tf_op jit(solution)/shard_map/reduce_sum | solution.py:113
  220.9 5.7 %all-reduce = (f32[512]{0:T(512)S(1)}, f32[2,32]{1,0:T(2,128)S(1)}) all-reduce(f32[512]{0:T(512)S(1)} %fusion.31, f32[2,32]{1,0:T(2,128)S(1)} %multiply_reduce_fusion), channel_id=1, replica_groups=mesh['groups'=2,'pair'=4,'tp'=4] {'tp'}, use_global_device_ids=true, to_apply=%region_5.6 | all-reduce | flops 576 | bytes 4608 | tf_op jit(solution)/shard_map/psum | solution.py:113
  227.5 4.1 %fusion.29 = bf16[1,512,2048]{2,1,0:T(8,128)(2,1)} fusion(f32[1,512,2048]{2,1,0:T(8,128)} %reshape.77, bf16[1,512,2048]{2,1,0:T(8,128)(2,1)S(1)} %copy-done, f32[2048]{0:T(1024)S(1)} %convert_element_type.41, f32[512]{0:T(512)S(1)} %add_rsqrt_fusion), kind=kLoop, calls=%fused_computation.28 | loop fusion | flops 5242880 | bytes 8398848 | tf_op jit(solution)/shard_map/convert_element_type | solution.py:116
  231.6 3.6 %copy.80 = bf16[1,2048,2,128]{3,2,1,0:T(2,128)(2,1)} copy(bf16[1,2048,2,128]{3,1,2,0:T(8,128)(2,1)} %collective-permute-done) | data formatting | bytes 2097152
  235.3 3.6 %copy.81 = bf16[1,2048,2,128]{3,2,1,0:T(2,128)(2,1)} copy(bf16[1,2048,2,128]{3,1,2,0:T(8,128)(2,1)} %collective-permute-done.1) | data formatting | bytes 2097152
  (96 shorter events, 70.3 us)
Async XLA Ops:
  0.6 18.5 %copy-start.1 = (bf16[1,512,16,128]{3,2,1,0:T(8,128)(2,1)S(1)}, bf16[1,512,16,128]{3,2,1,0:T(8,128)(2,1)}, u32[]{:S(2)}) copy-start(bf16[1,512,16,128]{3,2,1,0:T(8,128)(2,1)} %param.16) | copy-start | bytes 6291460
  0.6 177.3 %collective-permute-start.2 = (s32[1,32]{1,0:T(1,128)}, s32[1,32]{1,0:T(1,128)S(1)}, u32[]{:S(2)}, u32[]{:S(2)}) collective-permute-start(s32[1,32]{1,0:T(1,128)} %param.24), channel_id=1, source_target_pairs={{0,8},{4,12},{8,0},{12,4},{1,9},{5,13},{9,1},{13,5},{2,10},{6,14},... | collective-permute-start | bytes 392 | tf_op jit(solution)/shard_map/ppermute | solution.py:15
  4.8 173.4 %collective-permute-start.3 = (bf16[1,2,32,16,128]{4,3,2,1,0:T(8,128)(2,1)}, bf16[1,2,32,16,128]{4,3,2,1,0:T(8,128)(2,1)S(1)}, u32[]{:S(2)}, u32[]{:S(2)}) collective-permute-start(bf16[1,2,32,16,128]{4,3,2,1,0:T(8,128)(2,1)} %param.20), channel_id=1, source_target_pairs={{0,8},{4,12},{8,0},{12,4},{1,9},{5,13},{9,1},{13,5},{2,10},{6,14},... | collective-permute-start | bytes 786440 | tf_op jit(solution)/shard_map/ppermute | solution.py:15
  5.6 172.5 %collective-permute-start.4 = (bf16[1,2,32,2,128]{4,1,3,2,0:T(2,128)(2,1)S(1)}, bf16[1,2,32,2,128]{4,1,3,2,0:T(2,128)(2,1)S(1)}, u32[]{:S(2)}, u32[]{:S(2)}) collective-permute-start(bf16[1,2,32,2,128]{4,1,3,2,0:T(2,128)(2,1)S(1)} %copy.72), channel_id=1, source_target_pairs={{0,8},{4,12},{8,0},{12,4},{1,9},{5,13},{9,1},{13,5},{2,10},{6,14},... | collective-permute-start | bytes 98312 | tf_op jit(solution)/shard_map/ppermute | solution.py:15
  12.4 219.3 %collective-permute-start = (bf16[1,2048,2,128]{3,1,2,0:T(8,128)(2,1)}, bf16[1,2048,2,128]{3,1,2,0:T(8,128)(2,1)}, u32[]{:S(2)}, u32[]{:S(2)}) collective-permute-start(bf16[1,2048,2,128]{3,1,2,0:T(8,128)(2,1)} %copy_dynamic-update-slice_fusion.3), channel_id=1, source_target_pairs={{0,8},{4,12},{8,0},{12,4},{1,9},{5,13},{9,1},{13,5},{2,10},{6,14},... | collective-permute-start | bytes 3145736 | tf_op jit(solution)/shard_map/ppermute | solution.py:15
  16.2 219.0 %collective-permute-start.1 = (bf16[1,2048,2,128]{3,1,2,0:T(8,128)(2,1)}, bf16[1,2048,2,128]{3,1,2,0:T(8,128)(2,1)}, u32[]{:S(2)}, u32[]{:S(2)}) collective-permute-start(bf16[1,2048,2,128]{3,1,2,0:T(8,128)(2,1)} %copy_dynamic-update-slice_fusion.2), channel_id=1, source_target_pairs={{0,8},{4,12},{8,0},{12,4},{1,9},{5,13},{9,1},{13,5},{2,10},{6,14},... | collective-permute-start | bytes 3145736 | tf_op jit(solution)/shard_map/ppermute | solution.py:15
  21.0 156.9 %copy-start.3 = (bf16[1,2,32,2,128]{4,3,2,1,0:T(2,128)(2,1)S(1)}, bf16[1,2,32,2,128]{4,3,2,1,0:T(2,128)(2,1)}, u32[]{:S(2)}) copy-start(bf16[1,2,32,2,128]{4,3,2,1,0:T(2,128)(2,1)} %param.22) | copy-start | bytes 98308
  177.9 12.4 %collective-permute-start.5 = (bf16[1,2,32,2,128]{4,1,3,2,0:T(2,128)(2,1)S(1)}, bf16[1,2,32,2,128]{4,1,3,2,0:T(2,128)(2,1)S(1)}, u32[]{:S(2)}, u32[]{:S(2)}) collective-permute-start(bf16[1,2,32,2,128]{4,1,3,2,0:T(2,128)(2,1)S(1)} %copy.76), channel_id=1, source_target_pairs={{0,8},{4,12},{8,0},{12,4},{1,9},{5,13},{9,1},{13,5},{2,10},{6,14},... | collective-permute-start | bytes 98312 | tf_op jit(solution)/shard_map/ppermute | solution.py:15
  190.7 8.6 %copy-start = (bf16[1,512,2048]{2,1,0:T(8,128)(2,1)S(1)}, bf16[1,512,2048]{2,1,0:T(8,128)(2,1)}, u32[]{:S(2)}) copy-start(bf16[1,512,2048]{2,1,0:T(8,128)(2,1)} %param.19) | copy-start | bytes 6291460
  196.3 24.5 %collective-permute-start.6 = (f32[2,32,2048]{2,1,0:T(8,128)S(1)}, f32[2,32,2048]{2,1,0:T(8,128)S(1)}, u32[]{:S(2)}, u32[]{:S(2)}) collective-permute-start(f32[2,32,2048]{2,1,0:T(8,128)S(1)} %reshape.78), channel_id=1, source_target_pairs={{0,8},{4,12},{8,0},{12,4},{1,9},{5,13},{9,1},{13,5},{2,10},{6,14},... | collective-permute-start | bytes 1572872 | tf_op jit(solution)/shard_map/ppermute | solution.py:15
  199.8 2.9 %copy-start.4 = (bf16[2048]{0:T(1024)(128)(2,1)S(1)}, bf16[2048]{0:T(1024)(128)(2,1)}, u32[]{:S(2)}) copy-start(bf16[2048]{0:T(1024)(128)(2,1)} %param.25) | copy-start | bytes 12292
  214.1 6.7 %copy-start.2 = (bf16[1,2,32,2048]{3,2,1,0:T(8,128)(2,1)S(1)}, bf16[1,2,32,2048]{3,2,1,0:T(8,128)(2,1)}, u32[]{:S(2)}) copy-start(bf16[1,2,32,2048]{3,2,1,0:T(8,128)(2,1)} %param.23) | copy-start | bytes 786436
where the time goes:
time: 241 us; the launch traced here: 239 us
  matrix products  86.4 us (36%)
  loops' own time  62.4 us (26%)
  local copies, waits for them, and re-layouts  41.8 us (17%)
  other arithmetic  26.9 us (11%)
  starting transfers between devices  13.1 us (5%)
  blocking collectives  5.73 us (2%)
    another operation x1, loops' own time, prefill_attention(): per_head = lax.map(one_head, jnp.arange(query_heads, dtype=jnp.int32))  62.4 us
    dot_general x16, matrix products, one_head(): jnp.dot(weights, value_head, preferred_element_type=jnp.float32)  40.7 us
    dot_general x16, matrix products, one_head(): lax.dot_general(query, key_head, (((1,), (1,)), ((), ())), preferred_elem...  33.1 us
    unnamed x18, local copies, waits for them, and re-layouts  17 us
    ppermute x7, starting transfers between devices, from_behind(): return lax.ppermute(value, axis, pairs)  13.1 us
    reduce_sum x16, other arithmetic, one_head(): denominator = jnp.sum(scaled, axis=1, keepdims=True)  11.4 us
    dynamic_slice x16, local copies, waits for them, and re-layouts, prefill_attention(): per_head = lax.map(one_head, jnp.arange(query_heads, dtype=jnp.int32))  9.31 us
    transpose x1, local copies, waits for them, and re-layouts, prefill_attention(): jnp.transpose(per_head, (1, 0, 2))  6.58 us
  transfers between devices with their start and end apart: 7, of which 1 were waited for; matrix products, arithmetic and copies ran while one was open for 63% of the time, Pallas kernels for 0%

commit v1 on v0

v1 whole, which is shorter than its diff:
```python
import functools

import jax
import jax.numpy as jnp
from jax import lax
from jax.experimental import pallas as pl
from jax.experimental.pallas import tpu as pltpu
from jax.sharding import PartitionSpec as P

epsilon = 1e-05
log2_e = 1.4426950408889634


def from_behind(value, axis, steps):
    count = lax.axis_size(axis)
    pairs = [(source, (source + steps) % count) for source in range(count)]
    return lax.ppermute(value, axis, pairs)


def sum_over(value, axis):
    count = lax.axis_size(axis)
    if count & (count - 1):
        return lax.psum(value, axis)
    step = 1
    while step < count:
        value = value + lax.ppermute(value, axis, [(i, i ^ step) for i in range(count)])
        step *= 2
    return value


def contract_last(a, b):
    return lax.dot_general(a, b, (((1,), (1,)), ((), ())), preferred_element_type=jnp.float32)


def prefill_kernel(q_ref, k_ref, v_ref, residual_ref, hidden_ref, squares_ref, *, block, past):
    rows = q_ref.shape[1]
    head_size = q_ref.shape[2]
    factor = head_size ** (-0.5) * log2_e

    @pl.when(pl.program_id(0) == 0)
    def _():
        squares_ref[...] = jnp.zeros_like(squares_ref)

    visible = lax.broadcasted_iota(jnp.int32, (block, block), 1) <= lax.broadcasted_iota(
        jnp.int32, (block, block), 0
    )
    for start in range(0, rows, block):
        here = slice(start, start + block)
        before = past + start
        q = q_ref[0, here]
        far = contract_last(q, k_ref[0, :before])
        near = contract_last(q, k_ref[0, before : before + block])
        near = jnp.where(visible, near, -jnp.inf)
        top = jnp.maximum(
            jnp.max(far, axis=1, keepdims=True), jnp.max(near, axis=1, keepdims=True)
        )
        far = jnp.exp2((far - top) * factor)
        near = jnp.exp2((near - top) * factor)
        total = jnp.sum(far, axis=1, keepdims=True) + jnp.sum(near, axis=1, keepdims=True)
        mixed = jnp.dot(
            far.astype(jnp.bfloat16), v_ref[0, :before], preferred_element_type=jnp.float32
        ) + jnp.dot(
            near.astype(jnp.bfloat16),
            v_ref[0, before : before + block],
            preferred_element_type=jnp.float32,
        )
        hidden = mixed / total + residual_ref[here].astype(jnp.float32)
        hidden_ref[here] = hidden
        squares_ref[here] = squares_ref[here] + hidden * hidden


def prefill(queries, keys, values, residual):
    heads, rows, head_size = queries.shape
    key_heads, positions, _ = keys.shape
    per = heads // key_heads
    block = 256 if rows % 256 == 0 else rows
    return pl.pallas_call(
        functools.partial(prefill_kernel, block=block, past=positions - rows),
        grid=(heads,),
        in_specs=[
            pl.BlockSpec((1, rows, head_size), lambda h: (h, 0, 0)),
            pl.BlockSpec((1, positions, head_size), lambda h: (h // per, 0, 0)),
            pl.BlockSpec((1, positions, head_size), lambda h: (h // per, 0, 0)),
            pl.BlockSpec((rows, head_size), lambda h: (0, h)),
        ],
        out_specs=[
            pl.BlockSpec((rows, head_size), lambda h: (0, h)),
            pl.BlockSpec((rows, head_size), lambda h: (0, 0)),
        ],
        out_shape=[
            jax.ShapeDtypeStruct((rows, heads * head_size), jnp.float32),
            jax.ShapeDtypeStruct((rows, head_size), jnp.float32),
        ],
        cost_estimate=pl.CostEstimate(
            flops=8 * heads * rows * positions * head_size,
            transcendentals=heads * rows * positions,
            bytes_accessed=10 * rows * heads * head_size,
        ),
        name="prefill",
    )(queries, keys, values, residual)


def scores_kernel(
    q_ref, old_ref, new_ref, own_ref, cursor_ref, p_old_ref, p_new_ref, p_own_ref, total_ref,
    *, key_heads, steps, blocks_per_head,
):
    heads, rows, head_size = q_ref.shape
    candidates = rows // steps
    factor = head_size ** (-0.5) * log2_e
    key_head = pl.program_id(0) // blocks_per_head
    old_count = old_ref.shape[0]
    new_count = new_ref.shape[0]
    own_count = own_ref.shape[1]
    q = q_ref[...].reshape(heads * rows, head_size)
    limit = jnp.concatenate([cursor_ref[...] * key_heads] * heads, axis=0)

    def far(keys, first, count):
        column = lax.broadcasted_iota(jnp.int32, (1, count), 1)
        column = jnp.where(lax.rem(column, key_heads) == key_head, column + first, 2**30)
        return jnp.where(column < limit, contract_last(q, keys), -jnp.inf)

    old = far(old_ref[...], 0, old_count)
    new = far(new_ref[...], old_count, new_count)
    row = lax.rem(lax.broadcasted_iota(jnp.int32, (heads * rows, own_count), 0), rows)
    column = lax.broadcasted_iota(jnp.int32, (heads * rows, own_count), 1)
    allowed = (lax.rem(row, candidates) == lax.rem(column, candidates)) & (column <= row)
    own = jnp.where(allowed, contract_last(q, own_ref[0]), -jnp.inf)
    top = jnp.maximum(
        jnp.maximum(jnp.max(old, axis=1, keepdims=True), jnp.max(new, axis=1, keepdims=True)),
        jnp.max(own, axis=1, keepdims=True),
    )
    old = jnp.exp2((old - top) * factor)
    new = jnp.exp2((new - top) * factor)
    own = jnp.exp2((own - top) * factor)
    total = (
        jnp.sum(old, axis=1, keepdims=True)
        + jnp.sum(new, axis=1, keepdims=True)
        + jnp.sum(own, axis=1, keepdims=True)
    )
    p_old_ref[...] = old.astype(jnp.bfloat16)
    p_new_ref[...] = new.astype(jnp.bfloat16)
    p_own_ref[...] = own.astype(jnp.bfloat16)
    total_ref[...] = jnp.broadcast_to(total, total_ref.shape)


def decode_scores(queries, old_keys, new_keys, own_keys, cursor, steps):
    heads, rows, head_size = queries.shape
    key_heads, own_count, _ = own_keys.shape
    old_count = old_keys.shape[0]
    new_count = new_keys.shape[0]
    per = heads // key_heads
    take = 4 if per % 4 == 0 else per
    whole = lambda i: (0, 0)
    return pl.pallas_call(
        functools.partial(
            scores_kernel, key_heads=key_heads, steps=steps, blocks_per_head=per // take
        ),
        grid=(heads // take,),
        in_specs=[
            pl.BlockSpec((take, rows, head_size), lambda i: (i, 0, 0)),
            pl.BlockSpec((old_count, head_size), whole),
            pl.BlockSpec((new_count, head_size), whole),
            pl.BlockSpec((1, own_count, head_size), lambda i: (i // (per // take), 0, 0)),
            pl.BlockSpec((rows, 1), whole),
        ],
        out_specs=[
            pl.BlockSpec((take * rows, old_count), lambda i: (i, 0)),
            pl.BlockSpec((take * rows, new_count), lambda i: (i, 0)),
            pl.BlockSpec((take * rows, own_count), lambda i: (i, 0)),
            pl.BlockSpec((take * rows, head_size), lambda i: (i, 0)),
        ],
        out_shape=[
            jax.ShapeDtypeStruct((heads * rows, old_count), jnp.bfloat16),
            jax.ShapeDtypeStruct((heads * rows, new_count), jnp.bfloat16),
            jax.ShapeDtypeStruct((heads * rows, own_count), jnp.bfloat16),
            jax.ShapeDtypeStruct((heads * rows, head_size), jnp.float32),
        ],
        cost_estimate=pl.CostEstimate(
            flops=8 * heads * rows * (old_count + new_count) * head_size,
            transcendentals=heads * rows * (old_count + new_count),
            bytes_accessed=2 * heads * rows * (old_count + new_count),
        ),
        name="decode_scores",
    )(queries, old_keys, new_keys, own_keys, cursor)


def mix_kernel(p_old_ref, p_own_ref, old_ref, own_ref, out_ref):
    out_ref[...] = jnp.dot(
        p_old_ref[...], old_ref[...], preferred_element_type=jnp.float32
    ) + jnp.dot(p_own_ref[...], own_ref[0], preferred_element_type=jnp.float32)


def decode_mix(p_old, p_own, old_values, own_values):
    rows, old_count = p_old.shape
    key_heads, own_count, head_size = own_values.shape
    block = rows // key_heads
    return pl.pallas_call(
        mix_kernel,
        grid=(key_heads,),
        in_specs=[
            pl.BlockSpec((block, old_count), lambda g: (g, 0)),
            pl.BlockSpec((block, own_count), lambda g: (g, 0)),
            pl.BlockSpec((old_count, head_size), lambda g: (0, 0)),
            pl.BlockSpec((1, own_count, head_size), lambda g: (g, 0, 0)),
        ],
        out_specs=pl.BlockSpec((block, head_size), lambda g: (g, 0)),
        out_shape=jax.ShapeDtypeStruct((rows, head_size), jnp.float32),
        cost_estimate=pl.CostEstimate(
            flops=4 * rows * old_count * head_size,
            transcendentals=0,
            bytes_accessed=2 * rows * old_count,
        ),
        name="decode_mix",
    )(p_old, p_own, old_values, own_values)


def finish_kernel(p_new_ref, new_ref, mixed_ref, total_ref, residual_ref, hidden_ref, squares_ref):
    rows = residual_ref.shape[0]
    head_size = mixed_ref.shape[1]
    heads = mixed_ref.shape[0] // rows
    mixed = mixed_ref[...] + jnp.dot(
        p_new_ref[...], new_ref[...], preferred_element_type=jnp.float32
    )
    mixed = mixed / total_ref[...]
    squares = jnp.zeros((rows, head_size), jnp.float32)
    for h in range(heads):
        lanes = slice(h * head_size, (h + 1) * head_size)
        hidden = mixed[h * rows : (h + 1) * rows] + residual_ref[:, lanes].astype(jnp.float32)
        hidden_ref[:, lanes] = hidden
        squares = squares + hidden * hidden
    squares = jnp.broadcast_to(jnp.sum(squares, axis=1, keepdims=True), (rows, 128))
    squares_ref[...] = jnp.transpose(squares)[:8]


def decode_finish(p_new, new_values, mixed, total, residual):
    rows, features = residual.shape
    return pl.pallas_call(
        finish_kernel,
        out_shape=[
            jax.ShapeDtypeStruct((rows, features), jnp.float32),
            jax.ShapeDtypeStruct((8, rows), jnp.float32),
        ],
        cost_estimate=pl.CostEstimate(
            flops=2 * p_new.shape[0] * p_new.shape[1] * new_values.shape[1],
            transcendentals=0,
            bytes_accessed=2 * p_new.shape[0] * p_new.shape[1],
        ),
        name="decode_finish",
    )(p_new, new_values, mixed, total, residual)


def local(
    prompt_keys,
    prompt_values,
    span_queries,
    span_keys,
    span_values,
    prefill_residual,
    decode_queries,
    decode_keys,
    decode_values,
    decode_residual,
    cursor,
    norm_gain,
):
    halfway = lax.axis_size("pair") // 2
    width = norm_gain.shape[0] * lax.axis_size("tp")
    old_keys = from_behind(prompt_keys, "pair", halfway)
    new_keys = from_behind(span_keys, "pair", halfway)
    old_values = from_behind(prompt_values, "pair", halfway)
    new_values = from_behind(span_values, "pair", halfway)
    gain_wide = norm_gain.astype(jnp.float32)

    def normed(hidden, squares):
        scale = lax.rsqrt(squares / width + epsilon)
        return (hidden * scale[..., None] * gain_wide).astype(jnp.bfloat16)

    head_major = lambda x: jnp.transpose(x, (1, 0, 2))
    keys = head_major(jnp.concatenate([prompt_keys[0], span_keys[0]], axis=0))
    values = head_major(jnp.concatenate([prompt_values[0], span_values[0]], axis=0))
    hidden, squares = prefill(head_major(span_queries[0]), keys, values, prefill_residual[0])
    prefill_normed = normed(hidden, lax.psum(jnp.sum(squares, axis=1), "tp"))

    steps, candidates, heads, head_size = decode_queries.shape[1:]
    rows = steps * candidates
    flat = lambda x: x[0].reshape(rows, x.shape[3], head_size)
    mixed_rows = lambda x: x[0].reshape(x.shape[1] * x.shape[2], head_size)
    own_values = head_major(flat(decode_values))
    limits = jnp.concatenate([cursor[0]] * steps)[:, None]
    p_old, p_new, p_own, total = decode_scores(
        head_major(flat(decode_queries)),
        mixed_rows(old_keys),
        mixed_rows(new_keys),
        head_major(flat(decode_keys)),
        limits,
        steps,
    )
    mixed = decode_mix(p_old, p_own, mixed_rows(old_values), own_values)
    hidden, squares = decode_finish(
        p_new, mixed_rows(new_values), mixed, total, decode_residual[0].reshape(rows, -1)
    )
    squares = sum_over(squares, "tp")
    decode_normed = normed(hidden, squares[0]).reshape(decode_residual.shape)
    handed_keys = jnp.concatenate([old_keys, new_keys], axis=1)
    handed_values = jnp.concatenate([old_values, new_values], axis=1)
    return (prefill_normed[None], handed_keys, handed_values, decode_normed)


def solution(mesh):
    whole = P(("groups", "pair"), None, "tp", None)
    step = P(("groups", "pair"), None, None, "tp", None)
    placed = (
        whole,
        whole,
        whole,
        whole,
        whole,
        P(("groups", "pair"), None, "tp"),
        step,
        step,
        step,
        P(("groups", "pair"), None, None, "tp"),
        P(("groups", "pair"), None),
        P("tp"),
    )
    return jax.shard_map(
        local,
        mesh=mesh,
        in_specs=placed,
        out_specs=(
            P(("groups", "pair"), None, "tp"),
            whole,
            whole,
            P(("groups", "pair"), None, None, "tp"),
        ),
        check_vma=False,
    )
```

time: 241 us -> 120 us (0.50)
  matrix products: 86.4 us -> 0 us
  loops' own time: 62.4 us -> 0 us
  Pallas kernels: 0 us -> 50.6 us
  local copies, waits for them, and re-layouts: 41.8 us -> 9.6 us
  waiting for transfers between devices: 1.72 us -> 19.8 us
  starting transfers between devices: 13.1 us -> 9.07 us
  other arithmetic: 26.9 us -> 23.9 us
    dot_general x36 -> x0, matrix products: 86.4 us -> none  [the longest x16 40.7 us: one_head(): jnp.dot(weights, value_head, preferred_element_type=jnp.float32)]
    another operation x1 -> x0, loops' own time: 62.4 us -> none  [prefill_attention(): per_head = lax.map(one_head, jnp.arange(query_heads, dtype=jnp.int32))]
    pallas_call x0 -> x4, Pallas kernels: none -> 50.6 us  [the longest x1 32.1 us: prefill(): pl.pallas_call(functools.partial(prefill_kernel, block=block, past=positi...]
    reduce_sum x20 -> x1, other arithmetic: 21.2 us -> 1.09 us  [local(): prefill_normed = normed(hidden, lax.psum(jnp.sum(squares, axis=1), 'tp'))]
    ppermute x7 -> x4, waiting for transfers between devices: 1.72 us -> 19.8 us  [from_behind(): return lax.ppermute(value, axis, pairs)]
    concatenate x0 -> x2, other arithmetic: none -> 15.9 us  [the longest x1 7.96 us: local(): handed_keys = jnp.concatenate([old_keys, new_keys], axis=1)]
    dynamic_slice x16 -> x0, local copies, waits for them, and re-layouts: 9.31 us -> none  [prefill_attention(): per_head = lax.map(one_head, jnp.arange(query_heads, dtype=jnp.int32))]
    unnamed x18 -> x44, local copies, waits for them, and re-layouts: 17 us -> 8.9 us
  transfers between devices with their start and end apart: 7 -> 6, of which waited for: 1 -> 2; matrix products, arithmetic and copies ran while one was open for 63% -> 25% of each run, Pallas kernels for 0% -> 39%
where the time goes in v1:
time: 120 us
  Pallas kernels  50.6 us (42%)
  other arithmetic  23.9 us (20%)
  waiting for transfers between devices  19.8 us (16%)
  local copies, waits for them, and re-layouts  9.6 us (8%)
  starting transfers between devices  9.07 us (8%)
  blocking collectives  5.93 us (5%)
    pallas_call x1, Pallas kernels, prefill(): pl.pallas_call(functools.partial(prefill_kernel, block=block, past=positi...  32.1 us
    ppermute x4, waiting for transfers between devices, from_behind(): return lax.ppermute(value, axis, pairs)  19.8 us
    pallas_call x1, Pallas kernels, decode_scores(): pl.pallas_call(functools.partial(scores_kernel, key_heads=key_heads, step...  9.91 us
    unnamed x44, local copies, waits for them, and re-layouts  8.9 us
    concatenate x1, other arithmetic, local(): handed_keys = jnp.concatenate([old_keys, new_keys], axis=1)  7.96 us
    concatenate x1, other arithmetic, local(): handed_values = jnp.concatenate([old_values, new_values], axis=1)  7.93 us
    ppermute x4, starting transfers between devices, from_behind(): return lax.ppermute(value, axis, pairs)  7.13 us
    psum x1, blocking collectives, local(): prefill_normed = normed(hidden, lax.psum(jnp.sum(squares, axis=1), 'tp'))  5.93 us
  transfers between devices with their start and end apart: 6, of which 2 were waited for; matrix products, arithmetic and copies ran while one was open for 25% of the time, Pallas kernels for 39%

profile of v1, /device:TPU:0, one launch (start us, length us, event | category | flops | bytes accessed | tf_op | source)
XLA Modules:
  0.0 119.7 jit_solution(4907657094114287072)
XLA Ops:
  0.7 4.1 %collective-permute-start = (bf16[1,1536,2,128]{3,2,1,0:T(2,128)(2,1)}, bf16[1,1536,2,128]{3,2,1,0:T(2,128)(2,1)S(1)}, u32[]{:S(2)}, u32[]{:S(2)}) collective-permute-start(bf16[1,1536,2,128]{3,2,1,0:T(2,128)(2,1)} %param.12), channel_id=1, source_target_pairs={{0,8},{4,12},{8,0},{12,4},{1,9},{5,13},{9,1},{13,5},{2,10},{6,14},... | collective-permute-start | bytes 2359304 | tf_op jit(solution)/shard_map/ppermute | solution.py:17
  4.8 0.1 collective-permute-start.1
  4.9 2.8 %collective-permute-start.2 = (bf16[1,1536,2,128]{3,2,1,0:T(2,128)(2,1)}, bf16[1,1536,2,128]{3,2,1,0:T(2,128)(2,1)S(1)}, u32[]{:S(2)}, u32[]{:S(2)}) collective-permute-start(bf16[1,1536,2,128]{3,2,1,0:T(2,128)(2,1)} %param.13), channel_id=1, source_target_pairs={{0,8},{4,12},{8,0},{12,4},{1,9},{5,13},{9,1},{13,5},{2,10},{6,14},... | collective-permute-start | bytes 2359304 | tf_op jit(solution)/shard_map/ppermute | solution.py:17
  7.7 0.1 collective-permute-start.3
  7.8 1.2 %copy.32 = bf16[1,1536,2,128]{3,1,2,0:T(8,128)(2,1)S(1)} copy(bf16[1,1536,2,128]{3,2,1,0:T(2,128)(2,1)} %param.12) | data formatting | bytes 1572864 | tf_op args[0]
  9.0 1.0 copy.34
  10.0 0.1 copy.31
  10.2 1.9 %copy.30 = bf16[1,512,16,128]{3,1,2,0:T(8,128)(2,1)} copy(bf16[1,512,16,128]{3,2,1,0:T(8,128)(2,1)S(1)} %copy-done.2) | data formatting | bytes 4194304 | tf_op args[2]
  12.1 1.0 maximum_bitcast_fusion.k_ref
  13.1 1.0 maximum_bitcast_fusion.1.v_ref
  14.2 32.1 %prefill.1 = (f32[512,2048]{1,0:T(8,128)}, f32[512,128]{1,0:T(8,128)}) custom-call(bf16[16,512,128]{2,1,0:T(8,128)(2,1)} %bitcast.47, bf16[2,2048,128]{2,1,0:T(8,128)(2,1)} %maximum_bitcast_fusion.k_ref, bf16[2,2048,128]{2,1,0:T(8,128)(2,1)} %maximum_bitcast_fusion.1.v_ref, bf16[512,2048]{1,0:T(8,128)(2,1)} %bitcast.58), custom_call_target="tpu_custom_call" | custom-call | flops 17179869184 | bytes 10485760 | tf_op jit(solution)/shard_map/prefill/pallas_call | solution.py:77
  46.3 1.1 reduce_sum.9
  47.4 5.9 %psum.7 = f32[512]{0:T(512)S(1)} all-reduce(f32[512]{0:T(512)S(1)} %reduce_sum.9), channel_id=1, replica_groups=mesh['groups'=2,'pair'=4,'tp'=4] {'tp'}, use_global_device_ids=true, to_apply=%region_1.0 | all-reduce | flops 512 | bytes 4096 | tf_op jit(solution)/shard_map/psum | solution.py:282
  53.4 3.9 %fusion = bf16[1,512,2048]{2,1,0:T(8,128)(2,1)} fusion(f32[512,2048]{1,0:T(8,128)} %get-tuple-element.12, f32[2048]{0:T(1024)S(1)} %convert_element_type.9, f32[512]{0:T(512)S(1)} %add_rsqrt_fusion), kind=kLoop, calls=%fused_computation.1 | loop fusion | flops 3145728 | bytes 6301696 | tf_op jit(solution)/shard_map/broadcast_in_dim | solution.py:306
  57.3 0.8 copy.21
  58.1 0.1 add_bitcast_fusion
  58.2 0.7 copy.23.cursor_ref
  58.9 0.6 copy.22
  59.5 0.6 copy.24
  60.1 13.8 %collective-permute-done.1 = bf16[1,512,2,128]{3,2,1,0:T(2,128)(2,1)S(1)} collective-permute-done((bf16[1,512,2,128]{3,2,1,0:T(2,128)(2,1)}, bf16[1,512,2,128]{3,2,1,0:T(2,128)(2,1)S(1)}, u32[]{:S(2)}, u32[]{:S(2)}) %collective-permute-start.1) | collective-permute-done | bytes 262176 | tf_op jit(solution)/shard_map/ppermute | solution.py:17
  74.0 0.7 copy-done.11
  74.7 0.3 copy-done.6
  74.9 9.9 %decode_scores.1 = (bf16[1024,3072]{1,0:T(8,128)(2,1)}, bf16[1024,1024]{1,0:T(8,128)(2,1)}, bf16[1024,64]{1,0:T(8,128)(2,1)}, f32[1024,128]{1,0:T(8,128)}) custom-call(bf16[16,64,128]{2,1,0:T(8,128)(2,1)} %bitcast.53, bf16[3072,128]{1,0:T(8,128)(2,1)} %bitcast.51, bf16[1024,128]{1,0:T(8,128)(2,1)} %bitcast.55, bf16[2,64,128]{2,1,0:T(8,128)(2,1)} %bitcast.57, ...), custom_call_target="tpu_custom_call" | custom-call | flops 4294967296 | bytes 8388608 | tf_op jit(solution)/shard_map/decode_scores/pallas_call | solution.py:154
  84.8 6.0 %collective-permute-done.2 = bf16[1,1536,2,128]{3,2,1,0:T(2,128)(2,1)S(1)} collective-permute-done((bf16[1,1536,2,128]{3,2,1,0:T(2,128)(2,1)}, bf16[1,1536,2,128]{3,2,1,0:T(2,128)(2,1)S(1)}, u32[]{:S(2)}, u32[]{:S(2)}) %collective-permute-start.2) | collective-permute-done | bytes 786464 | tf_op jit(solution)/shard_map/ppermute | solution.py:17
  90.8 1.0 copy-done
  91.8 4.9 %decode_mix.1.mixed_ref = f32[1024,128]{1,0:T(8,128)} custom-call(bf16[1024,3072]{1,0:T(8,128)(2,1)} %get-tuple-element.15.p_old_ref, bf16[1024,64]{1,0:T(8,128)(2,1)} %get-tuple-element.16.p_own_ref, bf16[3072,128]{1,0:T(8,128)(2,1)} %bitcast.46, bf16[2,64,128]{2,1,0:T(8,128)(2,1)} %bitcast.56), custom_call_target="tpu_custom_call" | custom-call | flops 1610612736 | bytes 6291456 | tf_op jit(solution)/shard_map/decode_mix/pallas_call | solution.py:197
  96.7 0.7 copy-done.3
  97.4 3.6 %decode_finish.1 = (f32[64,2048]{1,0:T(8,128)}, f32[8,64]{1,0:T(8,128)}) custom-call(bf16[1024,1024]{1,0:T(8,128)(2,1)} %get-tuple-element.14.p_new_ref, bf16[1024,128]{1,0:T(8,128)(2,1)} %bitcast.48, f32[1024,128]{1,0:T(8,128)} %decode_mix.1.mixed_ref, f32[1024,128]{1,0:T(8,128)} %get-tuple-element.17.total_ref, bf16[64,2048]{1,0:T(8,128)(2,1)} %bitcast.52), custom_call_target="tpu_custom_call" | custom-call | flops 268435456 | bytes 2097152 | tf_op jit(solution)/shard_map/decode_finish/pallas_call | solution.py:237
  101.1 8.0 %pad_maximum_fusion = bf16[1,2048,2,128]{3,2,1,0:T(2,128)(2,1)} fusion(bf16[1,512,2,128]{3,2,1,0:T(2,128)(2,1)S(1)} %copy-done.12, bf16[1,1536,2,128]{3,2,1,0:T(2,128)(2,1)S(1)} %copy-done.7), kind=kLoop, calls=%fused_computation.5 | loop fusion | flops 524288 | bytes 2097152 | tf_op jit(solution)/shard_map/concatenate | solution.py:304
  109.1 1.9 %collective-permute-start.5 = (f32[8,64]{1,0:T(8,128)S(1)}, f32[8,64]{1,0:T(8,128)S(1)}, u32[]{:S(2)}, u32[]{:S(2)}) collective-permute-start(f32[8,64]{1,0:T(8,128)S(1)} %add.27), channel_id=1, source_target_pairs={{0,2},{1,3},{2,0},{3,1},{4,6},{5,7},{6,4},{7,5},{8,10},{9,11},{10,... | collective-permute-start | bytes 6152 | tf_op jit(solution)/shard_map/ppermute | solution.py:26
  111.0 7.9 %pad_maximum_fusion.1 = bf16[1,2048,2,128]{3,2,1,0:T(2,128)(2,1)} fusion(bf16[1,512,2,128]{3,2,1,0:T(2,128)(2,1)S(1)} %copy-done.4, bf16[1,1536,2,128]{3,2,1,0:T(2,128)(2,1)S(1)} %copy-done.1), kind=kLoop, calls=%fused_computation.6 | loop fusion | flops 524288 | bytes 2097152 | tf_op jit(solution)/shard_map/concatenate | solution.py:305
  118.9 0.8 multiply_convert_fusion.1
  (43 shorter events, 0.2 us)
Async XLA Ops:
  0.6 9.4 %copy-start.5 = (bf16[1,1536,2,128]{3,2,1,0:T(2,128)(2,1)S(1)}, bf16[1,1536,2,128]{3,2,1,0:T(2,128)(2,1)}, u32[]{:S(2)}) copy-start(bf16[1,1536,2,128]{3,2,1,0:T(2,128)(2,1)} %param.13) | copy-start | bytes 2359300
  0.6 9.5 %copy-start.10 = (bf16[1,512,2,128]{3,2,1,0:T(2,128)(2,1)S(1)}, bf16[1,512,2,128]{3,2,1,0:T(2,128)(2,1)}, u32[]{:S(2)}) copy-start(bf16[1,512,2,128]{3,2,1,0:T(2,128)(2,1)} %param.16) | copy-start | bytes 786436
  0.7 9.6 %copy-start.2 = (bf16[1,512,16,128]{3,2,1,0:T(8,128)(2,1)S(1)}, bf16[1,512,16,128]{3,2,1,0:T(8,128)(2,1)}, u32[]{:S(2)}) copy-start(bf16[1,512,16,128]{3,2,1,0:T(8,128)(2,1)} %param.14) | copy-start | bytes 6291460
  0.7 73.3 %collective-permute-start = (bf16[1,1536,2,128]{3,2,1,0:T(2,128)(2,1)}, bf16[1,1536,2,128]{3,2,1,0:T(2,128)(2,1)S(1)}, u32[]{:S(2)}, u32[]{:S(2)}) collective-permute-start(bf16[1,1536,2,128]{3,2,1,0:T(2,128)(2,1)} %param.12), channel_id=1, source_target_pairs={{0,8},{4,12},{8,0},{12,4},{1,9},{5,13},{9,1},{13,5},{2,10},{6,14},... | collective-permute-start | bytes 2359304 | tf_op jit(solution)/shard_map/ppermute | solution.py:17
  4.8 69.2 %collective-permute-start.1 = (bf16[1,512,2,128]{3,2,1,0:T(2,128)(2,1)}, bf16[1,512,2,128]{3,2,1,0:T(2,128)(2,1)S(1)}, u32[]{:S(2)}, u32[]{:S(2)}) collective-permute-start(bf16[1,512,2,128]{3,2,1,0:T(2,128)(2,1)} %param.15), channel_id=1, source_target_pairs={{0,8},{4,12},{8,0},{12,4},{1,9},{5,13},{9,1},{13,5},{2,10},{6,14},... | collective-permute-start | bytes 786440 | tf_op jit(solution)/shard_map/ppermute | solution.py:17
  4.9 85.9 %collective-permute-start.2 = (bf16[1,1536,2,128]{3,2,1,0:T(2,128)(2,1)}, bf16[1,1536,2,128]{3,2,1,0:T(2,128)(2,1)S(1)}, u32[]{:S(2)}, u32[]{:S(2)}) collective-permute-start(bf16[1,1536,2,128]{3,2,1,0:T(2,128)(2,1)} %param.13), channel_id=1, source_target_pairs={{0,8},{4,12},{8,0},{12,4},{1,9},{5,13},{9,1},{13,5},{2,10},{6,14},... | collective-permute-start | bytes 2359304 | tf_op jit(solution)/shard_map/ppermute | solution.py:17
  7.7 89.0 %collective-permute-start.3 = (bf16[1,512,2,128]{3,2,1,0:T(2,128)(2,1)}, bf16[1,512,2,128]{3,2,1,0:T(2,128)(2,1)S(1)}, u32[]{:S(2)}, u32[]{:S(2)}) collective-permute-start(bf16[1,512,2,128]{3,2,1,0:T(2,128)(2,1)} %param.16), channel_id=1, source_target_pairs={{0,8},{4,12},{8,0},{12,4},{1,9},{5,13},{9,1},{13,5},{2,10},{6,14},... | collective-permute-start | bytes 786440 | tf_op jit(solution)/shard_map/ppermute | solution.py:17
  14.1 39.2 %copy-start.15 = (bf16[2048]{0:T(1024)(128)(2,1)S(1)}, bf16[2048]{0:T(1024)(128)(2,1)}, u32[]{:S(2)}) copy-start(bf16[2048]{0:T(1024)(128)(2,1)} %param.23) | copy-start | bytes 12292
  53.3 4.0 %copy-start.9 = (bf16[1,2,32,16,128]{4,3,2,1,0:T(8,128)(2,1)S(1)}, bf16[1,2,32,16,128]{4,3,2,1,0:T(8,128)(2,1)}, u32[]{:S(2)}) copy-start(bf16[1,2,32,16,128]{4,3,2,1,0:T(8,128)(2,1)} %param.18) | copy-start | bytes 786436
  53.4 4.8 %copy-start.17 = (s32[1,32]{1,0:T(1,128)S(1)}, s32[1,32]{1,0:T(1,128)}, u32[]{:S(2)}) copy-start(s32[1,32]{1,0:T(1,128)} %param.22) | copy-start | bytes 388
  53.4 5.5 %copy-start.13 = (bf16[1,2,32,2,128]{4,3,2,1,0:T(2,128)(2,1)S(1)}, bf16[1,2,32,2,128]{4,3,2,1,0:T(2,128)(2,1)}, u32[]{:S(2)}) copy-start(bf16[1,2,32,2,128]{4,3,2,1,0:T(2,128)(2,1)} %param.19) | copy-start | bytes 98308
  53.4 6.1 %copy-start.14 = (bf16[1,2,32,2,128]{4,3,2,1,0:T(2,128)(2,1)S(1)}, bf16[1,2,32,2,128]{4,3,2,1,0:T(2,128)(2,1)}, u32[]{:S(2)}) copy-start(bf16[1,2,32,2,128]{4,3,2,1,0:T(2,128)(2,1)} %param.20) | copy-start | bytes 98308
  74.0 0.7 copy-start.11
  74.0 1.0 copy-start.6
  90.8 1.0 copy-start
  96.7 4.4 %copy-start.7 = (bf16[1,1536,2,128]{3,2,1,0:T(2,128)(2,1)S(1)}, bf16[1,1536,2,128]{3,2,1,0:T(2,128)(2,1)}, u32[]{:S(2)}) copy-start(bf16[1,1536,2,128]{3,2,1,0:T(2,128)(2,1)} %copy-done.6) | copy-start | bytes 2359300
  96.7 4.4 %copy-start.12 = (bf16[1,512,2,128]{3,2,1,0:T(2,128)(2,1)S(1)}, bf16[1,512,2,128]{3,2,1,0:T(2,128)(2,1)}, u32[]{:S(2)}) copy-start(bf16[1,512,2,128]{3,2,1,0:T(2,128)(2,1)} %copy-done.11) | copy-start | bytes 786436
  96.7 0.7 copy-start.3
  97.4 13.5 %copy-start.1 = (bf16[1,1536,2,128]{3,2,1,0:T(2,128)(2,1)S(1)}, bf16[1,1536,2,128]{3,2,1,0:T(2,128)(2,1)}, u32[]{:S(2)}) copy-start(bf16[1,1536,2,128]{3,2,1,0:T(2,128)(2,1)} %copy-done) | copy-start | bytes 2359300
  101.0 8.1 %copy-start.16 = (f32[8,64]{1,0:T(8,128)S(1)}, f32[8,64]{1,0:T(8,128)}, u32[]{:S(2)}) copy-start(f32[8,64]{1,0:T(8,128)} %get-tuple-element.19) | copy-start | bytes 6148
  101.0 9.9 %copy-start.4 = (bf16[1,512,2,128]{3,2,1,0:T(2,128)(2,1)S(1)}, bf16[1,512,2,128]{3,2,1,0:T(2,128)(2,1)}, u32[]{:S(2)}) copy-start(bf16[1,512,2,128]{3,2,1,0:T(2,128)(2,1)} %copy-done.3) | copy-start | bytes 786436
  101.0 17.9 %copy-start.8 = (f32[64,2048]{1,0:T(8,128)S(1)}, f32[64,2048]{1,0:T(8,128)}, u32[]{:S(2)}) copy-start(f32[64,2048]{1,0:T(8,128)} %get-tuple-element.18) | copy-start | bytes 1572868
  101.0 8.1 %collective-permute-start.4 = (f32[8,64]{1,0:T(8,128)}, f32[8,64]{1,0:T(8,128)S(1)}, u32[]{:S(2)}, u32[]{:S(2)}) collective-permute-start(f32[8,64]{1,0:T(8,128)} %get-tuple-element.19), channel_id=1, source_target_pairs={{0,1},{1,0},{2,3},{3,2},{4,5},{5,4},{6,7},{7,6},{8,9},{9,8},{10,11... | collective-permute-start | bytes 6152 | tf_op jit(solution)/shard_map/ppermute | solution.py:26
  109.1 9.8 %collective-permute-start.5 = (f32[8,64]{1,0:T(8,128)S(1)}, f32[8,64]{1,0:T(8,128)S(1)}, u32[]{:S(2)}, u32[]{:S(2)}) collective-permute-start(f32[8,64]{1,0:T(8,128)S(1)} %add.27), channel_id=1, source_target_pairs={{0,2},{1,3},{2,0},{3,1},{4,6},{5,7},{6,4},{7,5},{8,10},{9,11},{10,... | collective-permute-start | bytes 6152 | tf_op jit(solution)/shard_map/ppermute | solution.py:26

commit v2 on v1

v2 whole, which is shorter than its diff:
```python
import functools

import jax
import jax.numpy as jnp
from jax import lax
from jax.experimental import pallas as pl
from jax.experimental.pallas import tpu as pltpu
from jax.sharding import PartitionSpec as P

epsilon = 1e-05
log2_e = 1.4426950408889634


def from_behind(value, axis, steps):
    count = lax.axis_size(axis)
    pairs = [(source, (source + steps) % count) for source in range(count)]
    return lax.ppermute(value, axis, pairs)


def sum_over(value, axis):
    count = lax.axis_size(axis)
    if count & (count - 1):
        return lax.psum(value, axis)
    step = count // 2
    while step:
        value = value + lax.ppermute(value, axis, [(i, i ^ step) for i in range(count)])
        step //= 2
    return value


def contract_last(a, b):
    return lax.dot_general(a, b, (((1,), (1,)), ((), ())), preferred_element_type=jnp.float32)


def prefill_kernel(q_ref, k_ref, v_ref, residual_ref, hidden_ref, squares_ref, *, block, past):
    rows = q_ref.shape[1]
    head_size = q_ref.shape[2]
    factor = head_size ** (-0.5) * log2_e

    @pl.when(pl.program_id(0) == 0)
    def _():
        squares_ref[...] = jnp.zeros_like(squares_ref)

    visible = lax.broadcasted_iota(jnp.int32, (block, block), 1) <= lax.broadcasted_iota(
        jnp.int32, (block, block), 0
    )
    for start in range(0, rows, block):
        here = slice(start, start + block)
        before = past + start
        q = q_ref[0, here]
        far = contract_last(q, k_ref[0, :before])
        near = contract_last(q, k_ref[0, before : before + block])
        near = jnp.where(visible, near, -jnp.inf)
        top = jnp.maximum(
            jnp.max(far, axis=1, keepdims=True), jnp.max(near, axis=1, keepdims=True)
        )
        far = jnp.exp2((far - top) * factor)
        near = jnp.exp2((near - top) * factor)
        total = jnp.sum(far, axis=1, keepdims=True) + jnp.sum(near, axis=1, keepdims=True)
        mixed = jnp.dot(
            far.astype(jnp.bfloat16), v_ref[0, :before], preferred_element_type=jnp.float32
        ) + jnp.dot(
            near.astype(jnp.bfloat16),
            v_ref[0, before : before + block],
            preferred_element_type=jnp.float32,
        )
        hidden = mixed / total + residual_ref[here].astype(jnp.float32)
        hidden_ref[here] = hidden
        squares_ref[here] = squares_ref[here] + hidden * hidden


def prefill(queries, keys, values, residual):
    heads, rows, head_size = queries.shape
    key_heads, positions, _ = keys.shape
    per = heads // key_heads
    block = 256 if rows % 256 == 0 else rows
    return pl.pallas_call(
        functools.partial(prefill_kernel, block=block, past=positions - rows),
        grid=(heads,),
        in_specs=[
            pl.BlockSpec((1, rows, head_size), lambda h: (h, 0, 0)),
            pl.BlockSpec((1, positions, head_size), lambda h: (h // per, 0, 0)),
            pl.BlockSpec((1, positions, head_size), lambda h: (h // per, 0, 0)),
            pl.BlockSpec((rows, head_size), lambda h: (0, h)),
        ],
        out_specs=[
            pl.BlockSpec((rows, head_size), lambda h: (0, h)),
            pl.BlockSpec((rows, head_size), lambda h: (0, 0)),
        ],
        out_shape=[
            jax.ShapeDtypeStruct((rows, heads * head_size), jnp.float32),
            jax.ShapeDtypeStruct((rows, head_size), jnp.float32),
        ],
        cost_estimate=pl.CostEstimate(
            flops=8 * heads * rows * positions * head_size,
            transcendentals=heads * rows * positions,
            bytes_accessed=10 * rows * heads * head_size,
        ),
        compiler_params=pltpu.CompilerParams(vmem_limit_bytes=32 << 20),
        name="prefill",
    )(queries, keys, values, residual)


def split_heads(rows_ref, wide_ref, out_ref, first):
    key_heads = out_ref.shape[0]
    count = rows_ref.shape[0]
    wide_ref[:count] = rows_ref[...].astype(jnp.float32)
    for g in range(key_heads):
        part = wide_ref[pl.ds(g, count // key_heads, stride=key_heads), :]
        out_ref[g, first : first + count // key_heads] = part.astype(out_ref.dtype)


def scores_kernel(
    q_ref, old_ref, new_ref, own_ref, cursor_ref,
    p_old_ref, p_new_ref, p_own_ref, inverse_ref, handed_ref,
    wide_ref, keys_ref, sems,
    *, steps,
):
    heads, rows, head_size = q_ref.shape
    key_heads, own_count, _ = own_ref.shape
    per = heads // key_heads
    take = 4 if per % 4 == 0 else per
    candidates = rows // steps
    factor = head_size ** (-0.5) * log2_e
    past = old_ref.shape[0]
    copies = [
        pltpu.make_async_copy(old_ref, handed_ref.at[:past], sems.at[0]),
        pltpu.make_async_copy(new_ref, handed_ref.at[past:], sems.at[1]),
    ]
    for copy in copies:
        copy.start()
    split_heads(old_ref, wide_ref, keys_ref, 0)
    split_heads(new_ref, wide_ref, keys_ref, past // key_heads)
    positions = keys_ref.shape[1]
    block = take * rows
    limit = jnp.concatenate([cursor_ref[...]] * take, axis=0)
    within = lax.broadcasted_iota(jnp.int32, (block, positions), 1) < limit
    row = lax.rem(lax.broadcasted_iota(jnp.int32, (block, own_count), 0), rows)
    column = lax.broadcasted_iota(jnp.int32, (block, own_count), 1)
    allowed = (lax.rem(row, candidates) == lax.rem(column, candidates)) & (column <= row)
    for first in range(0, heads, take):
        g = first // per
        here = slice(first * rows, first * rows + block)
        q = q_ref[first : first + take].reshape(block, head_size)
        far = jnp.where(within, contract_last(q, keys_ref[g]), -jnp.inf)
        own = jnp.where(allowed, contract_last(q, own_ref[g]), -jnp.inf)
        top = jnp.maximum(
            jnp.max(far, axis=1, keepdims=True), jnp.max(own, axis=1, keepdims=True)
        )
        far = jnp.exp2((far - top) * factor)
        own = jnp.exp2((own - top) * factor)
        total = jnp.sum(far, axis=1, keepdims=True) + jnp.sum(own, axis=1, keepdims=True)
        far = far.astype(jnp.bfloat16)
        p_old_ref[here] = far[:, : past // key_heads]
        p_new_ref[here] = far[:, past // key_heads :]
        p_own_ref[here] = own.astype(jnp.bfloat16)
        inverse_ref[here] = jnp.broadcast_to(1.0 / total, (block, head_size))
    for copy in copies:
        copy.wait()


HBM = pl.BlockSpec(memory_space=pltpu.HBM)
VMEM = pl.BlockSpec(memory_space=pltpu.VMEM)


def room(mib):
    return pltpu.CompilerParams(vmem_limit_bytes=mib << 20)


def decode_scores(queries, old_keys, new_keys, own_keys, cursor, steps):
    heads, rows, head_size = queries.shape
    key_heads, own_count, _ = own_keys.shape
    past = old_keys.shape[0] // key_heads
    span = new_keys.shape[0] // key_heads
    every = heads * rows
    return pl.pallas_call(
        functools.partial(scores_kernel, steps=steps),
        in_specs=[VMEM] * 5,
        out_specs=[VMEM] * 4 + [HBM],
        out_shape=[
            jax.ShapeDtypeStruct((every, past), jnp.bfloat16),
            jax.ShapeDtypeStruct((every, span), jnp.bfloat16),
            jax.ShapeDtypeStruct((every, own_count), jnp.bfloat16),
            jax.ShapeDtypeStruct((every, head_size), jnp.float32),
            jax.ShapeDtypeStruct((key_heads * (past + span), head_size), jnp.bfloat16),
        ],
        scratch_shapes=[
            pltpu.VMEM(old_keys.shape, jnp.float32),
            pltpu.VMEM((key_heads, past + span, head_size), jnp.bfloat16),
            pltpu.SemaphoreType.DMA((2,)),
        ],
        compiler_params=room(24),
        cost_estimate=pl.CostEstimate(
            flops=8 * every * (past + span) * head_size,
            transcendentals=every * (past + span),
            bytes_accessed=2 * every * (past + span),
        ),
        name="decode_scores",
    )(queries, old_keys, new_keys, own_keys, cursor)


def mix_kernel(
    p_old_ref, p_own_ref, inverse_ref, old_ref, own_ref, residual_ref,
    base_ref, handed_ref,
    wide_ref, values_ref, sem,
):
    rows = residual_ref.shape[0]
    key_heads, _, head_size = own_ref.shape
    heads = p_old_ref.shape[0] // rows
    per = heads // key_heads
    copy = pltpu.make_async_copy(old_ref, handed_ref.at[: old_ref.shape[0]], sem)
    copy.start()
    split_heads(old_ref, wide_ref, values_ref, 0)
    for g in range(key_heads):
        here = slice(g * per * rows, (g + 1) * per * rows)
        mixed = jnp.dot(p_old_ref[here], values_ref[g], preferred_element_type=jnp.float32)
        mixed += jnp.dot(p_own_ref[here], own_ref[g], preferred_element_type=jnp.float32)
        mixed *= inverse_ref[here]
        for h in range(per):
            lanes = slice((g * per + h) * head_size, (g * per + h + 1) * head_size)
            base_ref[:, lanes] = mixed[h * rows : (h + 1) * rows] + residual_ref[:, lanes].astype(
                jnp.float32
            )
    copy.wait()


def decode_mix(p_old, p_own, inverse, old_values, own_values, residual, positions):
    key_heads, _, head_size = own_values.shape
    return pl.pallas_call(
        mix_kernel,
        in_specs=[VMEM] * 6,
        out_specs=[VMEM, HBM],
        out_shape=[
            jax.ShapeDtypeStruct(residual.shape, jnp.float32),
            jax.ShapeDtypeStruct((key_heads * positions, head_size), jnp.bfloat16),
        ],
        scratch_shapes=[
            pltpu.VMEM(old_values.shape, jnp.float32),
            pltpu.VMEM(
                (key_heads, old_values.shape[0] // key_heads, head_size), jnp.bfloat16
            ),
            pltpu.SemaphoreType.DMA(()),
        ],
        compiler_params=room(16),
        cost_estimate=pl.CostEstimate(
            flops=4 * p_old.shape[0] * p_old.shape[1] * head_size,
            transcendentals=0,
            bytes_accessed=2 * p_old.shape[0] * p_old.shape[1],
        ),
        name="decode_mix",
    )(p_old, p_own, inverse, old_values, own_values, residual)


def finish_kernel(
    p_new_ref, inverse_ref, new_ref, base_ref, part_ref,
    hidden_ref, squares_ref, handed_ref,
    wide_ref, values_ref, sem,
):
    rows = base_ref.shape[0]
    key_heads, _, head_size = values_ref.shape
    heads = p_new_ref.shape[0] // rows
    per = heads // key_heads
    past = handed_ref.shape[0] - new_ref.shape[0]
    copy = pltpu.make_async_copy(new_ref, handed_ref.at[past:], sem)
    copy.start()
    split_heads(new_ref, wide_ref, values_ref, 0)
    squares = jnp.zeros((rows, head_size), jnp.float32)
    for g in range(key_heads):
        here = slice(g * per * rows, (g + 1) * per * rows)
        mixed = jnp.dot(p_new_ref[here], values_ref[g], preferred_element_type=jnp.float32)
        mixed *= inverse_ref[here]
        for h in range(per):
            lanes = slice((g * per + h) * head_size, (g * per + h + 1) * head_size)
            hidden = mixed[h * rows : (h + 1) * rows] + base_ref[:, lanes]
            hidden_ref[:, lanes] = hidden
            squares += hidden * hidden
    squares = jnp.broadcast_to(jnp.sum(squares, axis=1, keepdims=True), (rows, 128))
    squares_ref[...] = jnp.transpose(squares)[:8]
    copy.wait()


def decode_finish(p_new, inverse, new_values, base, part, key_heads):
    rows, features = base.shape
    head_size = new_values.shape[1]
    return pl.pallas_call(
        finish_kernel,
        in_specs=[VMEM] * 4 + [HBM],
        out_specs=[VMEM, VMEM, HBM],
        out_shape=[
            jax.ShapeDtypeStruct((rows, features), jnp.float32),
            jax.ShapeDtypeStruct((8, rows), jnp.float32),
            jax.ShapeDtypeStruct(part.shape, part.dtype),
        ],
        scratch_shapes=[
            pltpu.VMEM(new_values.shape, jnp.float32),
            pltpu.VMEM(
                (key_heads, new_values.shape[0] // key_heads, head_size), jnp.bfloat16
            ),
            pltpu.SemaphoreType.DMA(()),
        ],
        input_output_aliases={4: 2},
        compiler_params=room(8),
        cost_estimate=pl.CostEstimate(
            flops=2 * p_new.shape[0] * p_new.shape[1] * head_size,
            transcendentals=0,
            bytes_accessed=2 * p_new.shape[0] * p_new.shape[1],
        ),
        name="decode_finish",
    )(p_new, inverse, new_values, base, part)


def local(
    prompt_keys,
    prompt_values,
    span_queries,
    span_keys,
    span_values,
    prefill_residual,
    decode_queries,
    decode_keys,
    decode_values,
    decode_residual,
    cursor,
    norm_gain,
):
    halfway = lax.axis_size("pair") // 2
    keys_shape = (prompt_keys.shape[1] + span_keys.shape[1],) + prompt_keys.shape[2:]
    width = norm_gain.shape[0] * lax.axis_size("tp")
    old_keys = from_behind(prompt_keys, "pair", halfway)
    new_keys = from_behind(span_keys, "pair", halfway)
    old_values = from_behind(prompt_values, "pair", halfway)
    new_values = from_behind(span_values, "pair", halfway)
    gain_wide = norm_gain.astype(jnp.float32)

    def normed(hidden, squares):
        scale = lax.rsqrt(squares / width + epsilon)
        return (hidden * scale[..., None] * gain_wide).astype(jnp.bfloat16)

    head_major = lambda x: jnp.transpose(x, (1, 0, 2))
    keys = head_major(jnp.concatenate([prompt_keys[0], span_keys[0]], axis=0))
    values = head_major(jnp.concatenate([prompt_values[0], span_values[0]], axis=0))
    hidden, squares = prefill(head_major(span_queries[0]), keys, values, prefill_residual[0])
    prefill_normed = normed(hidden, lax.psum(jnp.sum(squares, axis=1), "tp"))

    steps, candidates, heads, head_size = decode_queries.shape[1:]
    rows = steps * candidates
    flat = lambda x: x[0].reshape(rows, x.shape[3], head_size)
    prefill_normed, decode_queries = lax.optimization_barrier((prefill_normed, decode_queries))
    mixed_rows = lambda x: x[0].reshape(x.shape[1] * x.shape[2], head_size)
    own_values = head_major(flat(decode_values))
    limits = jnp.concatenate([cursor[0]] * steps)[:, None]
    p_old, p_new, p_own, inverse, handed_keys = decode_scores(
        head_major(flat(decode_queries)),
        mixed_rows(old_keys),
        mixed_rows(new_keys),
        head_major(flat(decode_keys)),
        limits,
        steps,
    )
    positions, key_heads, _ = keys_shape
    base, part = decode_mix(
        p_old, p_own, inverse, mixed_rows(old_values), own_values,
        decode_residual[0].reshape(rows, -1), positions,
    )
    hidden, squares, handed_values = decode_finish(
        p_new, inverse, mixed_rows(new_values), base, part, key_heads
    )
    squares = sum_over(squares, "tp")
    decode_normed = normed(hidden, squares[0]).reshape(decode_residual.shape)
    whole = lambda x: x.reshape(1, positions, key_heads, head_size)
    return (prefill_normed[None], whole(handed_keys), whole(handed_values), decode_normed)


def solution(mesh):
    whole = P(("groups", "pair"), None, "tp", None)
    step = P(("groups", "pair"), None, None, "tp", None)
    placed = (
        whole,
        whole,
        whole,
        whole,
        whole,
        P(("groups", "pair"), None, "tp"),
        step,
        step,
        step,
        P(("groups", "pair"), None, None, "tp"),
        P(("groups", "pair"), None),
        P("tp"),
    )
    return jax.shard_map(
        local,
        mesh=mesh,
        in_specs=placed,
        out_specs=(
            P(("groups", "pair"), None, "tp"),
            whole,
            whole,
            P(("groups", "pair"), None, None, "tp"),
        ),
        check_vma=False,
    )
```

time: 120 us -> 102 us (0.85)
  waiting for transfers between devices: 19.8 us -> 39.2 us
  other arithmetic: 23.9 us -> 5.16 us
  Pallas kernels: 50.6 us -> 35.7 us
  local copies, waits for them, and re-layouts: 9.6 us -> 6.51 us
    ppermute x4, waiting for transfers between devices: 19.8 us -> 36 us  [from_behind(): return lax.ppermute(value, axis, pairs)]
    concatenate x2 -> x0, other arithmetic: 15.9 us -> none  [the longest x1 7.96 us: local(): handed_keys = jnp.concatenate([old_keys, new_keys], axis=1)]
    pallas_call x3, Pallas kernels: 18.4 us -> 5.17 us  [the longest x1 3.25 us: decode_scores(): pl.pallas_call(functools.partial(scores_kernel, steps=steps), in_specs=[V...]
    convert_element_type x1 -> x2, other arithmetic: 0.82 us -> 4.77 us  [normed(): return (hidden * scale[..., None] * gain_wide).astype(jnp.bfloat16)]
    broadcast_in_dim x1 -> x0, other arithmetic: 3.95 us -> none  [local(): return (prefill_normed[None], handed_keys, handed_values, decode_normed)]
    ppermute x2, waiting for transfers between devices: 0.01 us -> 3.23 us  [sum_over(): lax.ppermute(value, axis, [(i, i ^ step) for i in range(count)])]
    unnamed x44 -> x29, local copies, waits for them, and re-layouts: 8.9 us -> 6.34 us
    transpose x2, other arithmetic: 2.07 us -> 0.14 us  [local(): head_major = lambda x: jnp.transpose(x, (1, 0, 2))]
  transfers between devices with their start and end apart: 6 -> 6, of which waited for: 2 -> 5; matrix products, arithmetic and copies ran while one was open for 25% -> 7% of each run, Pallas kernels for 39% -> 34%
where the time goes in v2:
time: 102 us
  waiting for transfers between devices  39.2 us (38%)
  Pallas kernels  35.7 us (35%)
  starting transfers between devices  8.74 us (9%)
  local copies, waits for them, and re-layouts  6.51 us (6%)
  blocking collectives  5.75 us (6%)
  other arithmetic  5.16 us (5%)
    ppermute x4, waiting for transfers between devices, from_behind(): return lax.ppermute(value, axis, pairs)  36 us
    pallas_call x1, Pallas kernels, prefill(): pl.pallas_call(functools.partial(prefill_kernel, block=block, past=positi...  30.6 us
    ppermute x4, starting transfers between devices, from_behind(): return lax.ppermute(value, axis, pairs)  7.13 us
    unnamed x29, local copies, waits for them, and re-layouts  6.34 us
    psum x1, blocking collectives, local(): prefill_normed = normed(hidden, lax.psum(jnp.sum(squares, axis=1), 'tp'))  5.75 us
    convert_element_type x2, other arithmetic, normed(): return (hidden * scale[..., None] * gain_wide).astype(jnp.bfloat16)  4.77 us
    pallas_call x1, Pallas kernels, decode_scores(): pl.pallas_call(functools.partial(scores_kernel, steps=steps), in_specs=[V...  3.25 us
    ppermute x2, waiting for transfers between devices, sum_over(): lax.ppermute(value, axis, [(i, i ^ step) for i in range(count)])  3.23 us
  transfers between devices with their start and end apart: 6, of which 5 were waited for; matrix products, arithmetic and copies ran while one was open for 7% of the time, Pallas kernels for 34%

profile of v2, /device:TPU:0, one launch (start us, length us, event | category | flops | bytes accessed | tf_op | source)
XLA Modules:
  0.0 102.0 jit_solution(7348466842438460233)
XLA Ops:
  0.7 4.1 %collective-permute-start = (bf16[1,1536,2,128]{3,2,1,0:T(2,128)(2,1)}, bf16[1,1536,2,128]{3,2,1,0:T(2,128)(2,1)S(1)}, u32[]{:S(2)}, u32[]{:S(2)}) collective-permute-start(bf16[1,1536,2,128]{3,2,1,0:T(2,128)(2,1)} %param.12), channel_id=1, source_target_pairs={{0,8},{4,12},{8,0},{12,4},{1,9},{5,13},{9,1},{13,5},{2,10},{6,14},... | collective-permute-start | bytes 2359304 | tf_op jit(solution)/shard_map/ppermute | solution.py:17
  4.8 0.1 collective-permute-start.1
  4.9 2.8 %collective-permute-start.3 = (bf16[1,1536,2,128]{3,2,1,0:T(2,128)(2,1)}, bf16[1,1536,2,128]{3,2,1,0:T(2,128)(2,1)S(1)}, u32[]{:S(2)}, u32[]{:S(2)}) collective-permute-start(bf16[1,1536,2,128]{3,2,1,0:T(2,128)(2,1)} %param.13), channel_id=1, source_target_pairs={{0,8},{4,12},{8,0},{12,4},{1,9},{5,13},{9,1},{13,5},{2,10},{6,14},... | collective-permute-start | bytes 2359304 | tf_op jit(solution)/shard_map/ppermute | solution.py:17
  7.7 0.1 collective-permute-start.2
  7.8 1.2 %copy.33 = bf16[1,1536,2,128]{3,1,2,0:T(8,128)(2,1)S(1)} copy(bf16[1,1536,2,128]{3,2,1,0:T(2,128)(2,1)} %param.12) | data formatting | bytes 1572864 | tf_op args[0]
  9.0 1.0 copy.35
  10.0 0.1 copy.32
  10.2 0.5 copy.31
  10.8 0.0 copy-start.2
  10.8 0.1 maximum_bitcast_fusion.k_ref
  10.9 0.1 maximum_bitcast_fusion.1.v_ref
  10.9 1.4 %copy-done.2 = bf16[1,512,2048]{2,1,0:T(8,128)(2,1)S(1)} copy-done((bf16[1,512,2048]{2,1,0:T(8,128)(2,1)S(1)}, bf16[1,512,2048]{2,1,0:T(8,128)(2,1)}, u32[]{:S(2)}) %copy-start.2) | copy-done | bytes 2097176
  12.4 30.6 %prefill.1 = (f32[512,2048]{1,0:T(8,128)S(1)}, f32[512,128]{1,0:T(8,128)S(1)}) custom-call(bf16[16,512,128]{2,1,0:T(8,128)(2,1)S(1)} %bitcast.45, bf16[2,2048,128]{2,1,0:T(8,128)(2,1)S(1)} %maximum_bitcast_fusion.k_ref, bf16[2,2048,128]{2,1,0:T(8,128)(2,1)S(1)} %maximum_bitcast_fusion.1.v_ref, bf16[512,2048]{1,0:T(8,128)(2,1)S(1)} %bitcast.52), custom_call_target="tpu_custom_call" | custom-call | flops 17179869184 | bytes 10485760 | tf_op jit(solution)/shard_map/prefill/pallas_call | solution.py:77
  43.0 1.9 %copy-done = f32[512,2048]{1,0:T(8,128)} copy-done((f32[512,2048]{1,0:T(8,128)}, f32[512,2048]{1,0:T(8,128)S(1)}, u32[]{:S(2)}) %copy-start) | copy-done | bytes 4194328
  44.9 0.1 reduce_sum.9
  45.0 5.8 %psum.7 = f32[512]{0:T(512)S(1)} all-reduce(f32[512]{0:T(512)S(1)} %reduce_sum.9), channel_id=1, replica_groups=mesh['groups'=2,'pair'=4,'tp'=4] {'tp'}, use_global_device_ids=true, to_apply=%region_1.0 | all-reduce | flops 512 | bytes 4096 | tf_op jit(solution)/shard_map/psum | solution.py:343
  50.8 0.0 copy-start.7
  50.9 0.0 copy-start.8
  50.9 3.9 %multiply_convert_fusion = bf16[512,2048]{1,0:T(8,128)(2,1)} fusion(f32[512,2048]{1,0:T(8,128)} %copy-done, f32[2048]{0:T(1024)S(1)} %convert_element_type.9, f32[512]{0:T(512)S(1)} %add_rsqrt_fusion), kind=kLoop, calls=%fused_computation | loop fusion | flops 3145728 | bytes 6301696 | tf_op jit(solution)/shard_map/convert_element_type | solution.py:337
  54.8 0.1 copy.22
  54.9 0.1 add_bitcast_fusion
  55.0 0.1 copy.24.cursor_ref
  55.1 18.8 %collective-permute-done.1 = bf16[1,512,2,128]{3,2,1,0:T(2,128)(2,1)S(1)} collective-permute-done((bf16[1,512,2,128]{3,2,1,0:T(2,128)(2,1)}, bf16[1,512,2,128]{3,2,1,0:T(2,128)(2,1)S(1)}, u32[]{:S(2)}, u32[]{:S(2)}) %collective-permute-start.1) | collective-permute-done | bytes 262176 | tf_op jit(solution)/shard_map/ppermute | solution.py:17
  74.0 3.3 %decode_scores.1 = (bf16[1024,1536]{1,0:T(8,128)(2,1)S(1)}, bf16[1024,512]{1,0:T(8,128)(2,1)S(1)}, bf16[1024,64]{1,0:T(8,128)(2,1)S(1)}, f32[1024,128]{1,0:T(8,128)S(1)}, bf16[4096,128]{1,0:T(8,128)(2,1)}) custom-call(bf16[16,64,128]{2,1,0:T(8,128)(2,1)S(1)} %bitcast.48, bf16[3072,128]{1,0:T(8,128)(2,1)S(1)} %bitcast.53, bf16[1024,128]{1,0:T(8,128)(2,1)S(1)} %bitcast.54, ...), custom_call_target="tpu_custom_call" | custom-call | flops 2147483648 | bytes 4194304 | tf_op jit(solution)/shard_map/decode_scores/pallas_call | solution.py:176
  77.2 13.6 %collective-permute-done.3 = bf16[1,1536,2,128]{3,2,1,0:T(2,128)(2,1)S(1)} collective-permute-done((bf16[1,1536,2,128]{3,2,1,0:T(2,128)(2,1)}, bf16[1,1536,2,128]{3,2,1,0:T(2,128)(2,1)S(1)}, u32[]{:S(2)}, u32[]{:S(2)}) %collective-permute-start.3) | collective-permute-done | bytes 786464 | tf_op jit(solution)/shard_map/ppermute | solution.py:17
  90.8 1.2 %decode_mix.1 = (f32[64,2048]{1,0:T(8,128)S(1)}, bf16[4096,128]{1,0:T(8,128)(2,1)}) custom-call(bf16[1024,1536]{1,0:T(8,128)(2,1)S(1)} %get-tuple-element.25.p_old_ref, bf16[1024,64]{1,0:T(8,128)(2,1)S(1)} %get-tuple-element.26.p_own_ref, f32[1024,128]{1,0:T(8,128)S(1)} %get-tuple-element.24.inverse_ref, bf16[3072,128]{1,0:T(8,128)(2,1)S(1)} %bitcast.46, ...), custom_call_target="tpu_custom_call" | custom-call | flops 805306368 | bytes 3145728 | tf_op jit(solution)/shard_map/decode_mix/pallas_call | solution.py:229
  92.0 3.6 %collective-permute-done.2 = bf16[1,512,2,128]{3,2,1,0:T(2,128)(2,1)S(1)} collective-permute-done((bf16[1,512,2,128]{3,2,1,0:T(2,128)(2,1)}, bf16[1,512,2,128]{3,2,1,0:T(2,128)(2,1)S(1)}, u32[]{:S(2)}, u32[]{:S(2)}) %collective-permute-start.2) | collective-permute-done | bytes 262176 | tf_op jit(solution)/shard_map/ppermute | solution.py:17
  95.6 0.7 decode_finish.1
  96.3 1.6 %collective-permute-start.4 = (f32[8,64]{1,0:T(8,128)S(1)}, f32[8,64]{1,0:T(8,128)S(1)}, u32[]{:S(2)}, u32[]{:S(2)}) collective-permute-start(f32[8,64]{1,0:T(8,128)S(1)} %get-tuple-element.31), channel_id=1, source_target_pairs={{0,2},{1,3},{2,0},{3,1},{4,6},{5,7},{6,4},{7,5},{8,10},{9,11},{10,... | collective-permute-start | bytes 6152 | tf_op jit(solution)/shard_map/ppermute | solution.py:26
  97.9 2.1 %collective-permute-done.4 = f32[8,64]{1,0:T(8,128)S(1)} collective-permute-done((f32[8,64]{1,0:T(8,128)S(1)}, f32[8,64]{1,0:T(8,128)S(1)}, u32[]{:S(2)}, u32[]{:S(2)}) %collective-permute-start.4) | collective-permute-done | bytes 2080 | tf_op jit(solution)/shard_map/ppermute | solution.py:26
  100.0 1.2 %collective-permute-done.5 = f32[8,64]{1,0:T(8,128)S(1)} collective-permute-done((f32[8,64]{1,0:T(8,128)S(1)}, f32[8,64]{1,0:T(8,128)S(1)}, u32[]{:S(2)}, u32[]{:S(2)}) %collective-permute-start.5) | collective-permute-done | bytes 2080 | tf_op jit(solution)/shard_map/ppermute | solution.py:26
  101.1 0.8 multiply_convert_fusion.1
  (27 shorter events, 0.1 us)
Async XLA Ops:
  0.6 9.4 %copy-start.4 = (bf16[1,1536,2,128]{3,2,1,0:T(2,128)(2,1)S(1)}, bf16[1,1536,2,128]{3,2,1,0:T(2,128)(2,1)}, u32[]{:S(2)}) copy-start(bf16[1,1536,2,128]{3,2,1,0:T(2,128)(2,1)} %param.13) | copy-start | bytes 2359300
  0.6 9.5 %copy-start.6 = (bf16[1,512,2,128]{3,2,1,0:T(2,128)(2,1)S(1)}, bf16[1,512,2,128]{3,2,1,0:T(2,128)(2,1)}, u32[]{:S(2)}) copy-start(bf16[1,512,2,128]{3,2,1,0:T(2,128)(2,1)} %param.16) | copy-start | bytes 786436
  0.7 9.6 %copy-start.3 = (bf16[1,512,16,128]{3,2,1,0:T(8,128)(2,1)S(1)}, bf16[1,512,16,128]{3,2,1,0:T(8,128)(2,1)}, u32[]{:S(2)}) copy-start(bf16[1,512,16,128]{3,2,1,0:T(8,128)(2,1)} %param.14) | copy-start | bytes 6291460
  0.7 73.3 %collective-permute-start = (bf16[1,1536,2,128]{3,2,1,0:T(2,128)(2,1)}, bf16[1,1536,2,128]{3,2,1,0:T(2,128)(2,1)S(1)}, u32[]{:S(2)}, u32[]{:S(2)}) collective-permute-start(bf16[1,1536,2,128]{3,2,1,0:T(2,128)(2,1)} %param.12), channel_id=1, source_target_pairs={{0,8},{4,12},{8,0},{12,4},{1,9},{5,13},{9,1},{13,5},{2,10},{6,14},... | collective-permute-start | bytes 2359304 | tf_op jit(solution)/shard_map/ppermute | solution.py:17
  4.8 69.2 %collective-permute-start.1 = (bf16[1,512,2,128]{3,2,1,0:T(2,128)(2,1)}, bf16[1,512,2,128]{3,2,1,0:T(2,128)(2,1)S(1)}, u32[]{:S(2)}, u32[]{:S(2)}) collective-permute-start(bf16[1,512,2,128]{3,2,1,0:T(2,128)(2,1)} %param.15), channel_id=1, source_target_pairs={{0,8},{4,12},{8,0},{12,4},{1,9},{5,13},{9,1},{13,5},{2,10},{6,14},... | collective-permute-start | bytes 786440 | tf_op jit(solution)/shard_map/ppermute | solution.py:17
  4.9 85.9 %collective-permute-start.3 = (bf16[1,1536,2,128]{3,2,1,0:T(2,128)(2,1)}, bf16[1,1536,2,128]{3,2,1,0:T(2,128)(2,1)S(1)}, u32[]{:S(2)}, u32[]{:S(2)}) collective-permute-start(bf16[1,1536,2,128]{3,2,1,0:T(2,128)(2,1)} %param.13), channel_id=1, source_target_pairs={{0,8},{4,12},{8,0},{12,4},{1,9},{5,13},{9,1},{13,5},{2,10},{6,14},... | collective-permute-start | bytes 2359304 | tf_op jit(solution)/shard_map/ppermute | solution.py:17
  7.7 87.9 %collective-permute-start.2 = (bf16[1,512,2,128]{3,2,1,0:T(2,128)(2,1)}, bf16[1,512,2,128]{3,2,1,0:T(2,128)(2,1)S(1)}, u32[]{:S(2)}, u32[]{:S(2)}) collective-permute-start(bf16[1,512,2,128]{3,2,1,0:T(2,128)(2,1)} %param.16), channel_id=1, source_target_pairs={{0,8},{4,12},{8,0},{12,4},{1,9},{5,13},{9,1},{13,5},{2,10},{6,14},... | collective-permute-start | bytes 786440 | tf_op jit(solution)/shard_map/ppermute | solution.py:17
  10.8 1.6 %copy-start.2 = (bf16[1,512,2048]{2,1,0:T(8,128)(2,1)S(1)}, bf16[1,512,2048]{2,1,0:T(8,128)(2,1)}, u32[]{:S(2)}) copy-start(bf16[1,512,2048]{2,1,0:T(8,128)(2,1)} %param.17) | copy-start | bytes 6291460
  12.4 38.5 %copy-start.9 = (bf16[2048]{0:T(1024)(128)(2,1)S(1)}, bf16[2048]{0:T(1024)(128)(2,1)}, u32[]{:S(2)}) copy-start(bf16[2048]{0:T(1024)(128)(2,1)} %param.23) | copy-start | bytes 12292
  42.9 2.0 %copy-start = (f32[512,2048]{1,0:T(8,128)}, f32[512,2048]{1,0:T(8,128)S(1)}, u32[]{:S(2)}) copy-start(f32[512,2048]{1,0:T(8,128)S(1)} %get-tuple-element.18) | copy-start | bytes 12582916
  50.8 4.0 %copy-start.5 = (bf16[1,2,32,16,128]{4,3,2,1,0:T(8,128)(2,1)S(1)}, bf16[1,2,32,16,128]{4,3,2,1,0:T(8,128)(2,1)}, u32[]{:S(2)}) copy-start(bf16[1,2,32,16,128]{4,3,2,1,0:T(8,128)(2,1)} %param.18) | copy-start | bytes 786436
  50.8 4.1 %copy-start.10 = (s32[1,32]{1,0:T(1,128)S(1)}, s32[1,32]{1,0:T(1,128)}, u32[]{:S(2)}) copy-start(s32[1,32]{1,0:T(1,128)} %param.22) | copy-start | bytes 388
  50.8 4.2 %copy-start.7 = (bf16[1,2,32,2,128]{4,3,2,1,0:T(2,128)(2,1)S(1)}, bf16[1,2,32,2,128]{4,3,2,1,0:T(2,128)(2,1)}, u32[]{:S(2)}) copy-start(bf16[1,2,32,2,128]{4,3,2,1,0:T(2,128)(2,1)} %param.19) | copy-start | bytes 98308
  50.9 4.2 %copy-start.8 = (bf16[1,2,32,2,128]{4,3,2,1,0:T(2,128)(2,1)S(1)}, bf16[1,2,32,2,128]{4,3,2,1,0:T(2,128)(2,1)}, u32[]{:S(2)}) copy-start(bf16[1,2,32,2,128]{4,3,2,1,0:T(2,128)(2,1)} %param.20) | copy-start | bytes 98308
  74.0 16.9 %copy-start.1 = (bf16[1,2,32,2048]{3,2,1,0:T(8,128)(2,1)S(1)}, bf16[1,2,32,2048]{3,2,1,0:T(8,128)(2,1)}, u32[]{:S(2)}) copy-start(bf16[1,2,32,2048]{3,2,1,0:T(8,128)(2,1)} %param.21) | copy-start | bytes 786436
  96.3 3.7 %collective-permute-start.4 = (f32[8,64]{1,0:T(8,128)S(1)}, f32[8,64]{1,0:T(8,128)S(1)}, u32[]{:S(2)}, u32[]{:S(2)}) collective-permute-start(f32[8,64]{1,0:T(8,128)S(1)} %get-tuple-element.31), channel_id=1, source_target_pairs={{0,2},{1,3},{2,0},{3,1},{4,6},{5,7},{6,4},{7,5},{8,10},{9,11},{10,... | collective-permute-start | bytes 6152 | tf_op jit(solution)/shard_map/ppermute | solution.py:26
  100.0 1.2 %collective-permute-start.5 = (f32[8,64]{1,0:T(8,128)S(1)}, f32[8,64]{1,0:T(8,128)S(1)}, u32[]{:S(2)}, u32[]{:S(2)}) collective-permute-start(f32[8,64]{1,0:T(8,128)S(1)} %add.27), channel_id=1, source_target_pairs={{0,1},{1,0},{2,3},{3,2},{4,5},{5,4},{6,7},{7,6},{8,9},{9,8},{10,11... | collective-permute-start | bytes 6152 | tf_op jit(solution)/shard_map/ppermute | solution.py:26

commit v3 on v2

--- a/solution.py
+++ b/solution.py
@@ -21,11 +21,11 @@
     count = lax.axis_size(axis)
     if count & (count - 1):
         return lax.psum(value, axis)
-    step = count // 2
-    while step:
-        value = value + lax.ppermute(value, axis, [(i, i ^ step) for i in range(count)])
-        step //= 2
-    return value
+    others = [
+        lax.ppermute(value, axis, [(i, i ^ step) for i in range(count)])
+        for step in (3, 2, 1)
+    ]
+    return functools.reduce(jnp.add, others, value)
 
 
 def contract_last(a, b):
@@ -252,17 +252,14 @@
 
 
 def finish_kernel(
-    p_new_ref, inverse_ref, new_ref, base_ref, part_ref,
-    hidden_ref, squares_ref, handed_ref,
-    wide_ref, values_ref, sem,
+    p_new_ref, inverse_ref, new_ref, base_ref,
+    hidden_ref, squares_ref,
+    wide_ref, values_ref,
 ):
     rows = base_ref.shape[0]
     key_heads, _, head_size = values_ref.shape
     heads = p_new_ref.shape[0] // rows
     per = heads // key_heads
-    past = handed_ref.shape[0] - new_ref.shape[0]
-    copy = pltpu.make_async_copy(new_ref, handed_ref.at[past:], sem)
-    copy.start()
     split_heads(new_ref, wide_ref, values_ref, 0)
     squares = jnp.zeros((rows, head_size), jnp.float32)
     for g in range(key_heads):
@@ -276,29 +273,25 @@
             squares += hidden * hidden
     squares = jnp.broadcast_to(jnp.sum(squares, axis=1, keepdims=True), (rows, 128))
     squares_ref[...] = jnp.transpose(squares)[:8]
-    copy.wait()
-
-
-def decode_finish(p_new, inverse, new_values, base, part, key_heads):
+
+
+def decode_finish(p_new, inverse, new_values, base, key_heads):
     rows, features = base.shape
     head_size = new_values.shape[1]
     return pl.pallas_call(
         finish_kernel,
-        in_specs=[VMEM] * 4 + [HBM],
-        out_specs=[VMEM, VMEM, HBM],
+        in_specs=[VMEM] * 4,
+        out_specs=[VMEM] * 2,
         out_shape=[
             jax.ShapeDtypeStruct((rows, features), jnp.float32),
             jax.ShapeDtypeStruct((8, rows), jnp.float32),
-            jax.ShapeDtypeStruct(part.shape, part.dtype),
         ],
         scratch_shapes=[
             pltpu.VMEM(new_values.shape, jnp.float32),
             pltpu.VMEM(
                 (key_heads, new_values.shape[0] // key_heads, head_size), jnp.bfloat16
             ),
-            pltpu.SemaphoreType.DMA(()),
-        ],
-        input_output_aliases={4: 2},
+        ],
         compiler_params=room(8),
         cost_estimate=pl.CostEstimate(
             flops=2 * p_new.shape[0] * p_new.shape[1] * head_size,
@@ -306,7 +299,31 @@
             bytes_accessed=2 * p_new.shape[0] * p_new.shape[1],
         ),
         name="decode_finish",
-    )(p_new, inverse, new_values, base, part)
+    )(p_new, inverse, new_values, base)
+
+
+def append_kernel(new_ref, part_ref, after_ref, handed_ref, sem):
+    copy = pltpu.make_async_copy(
+        new_ref, handed_ref.at[handed_ref.shape[0] - new_ref.shape[0] :], sem
+    )
+    copy.start()
+    copy.wait()
+
+
+def append(part, new, after):
+    return pl.pallas_call(
+        append_kernel,
+        in_specs=[VMEM, HBM, VMEM],
+        out_specs=HBM,
+        out_shape=jax.ShapeDtypeStruct(part.shape, part.dtype),
+        scratch_shapes=[pltpu.SemaphoreType.DMA(())],
+        input_output_aliases={1: 0},
+        compiler_params=room(2),
+        cost_estimate=pl.CostEstimate(
+            flops=1000000, transcendentals=0, bytes_accessed=4 * new.size
+        ),
+        name="append",
+    )(new, part, after)
 
 
 def local(
@@ -362,9 +379,9 @@
         p_old, p_own, inverse, mixed_rows(old_values), own_values,
         decode_residual[0].reshape(rows, -1), positions,
     )
-    hidden, squares, handed_values = decode_finish(
-        p_new, inverse, mixed_rows(new_values), base, part, key_heads
-    )
+    new_rows = mixed_rows(new_values)
+    hidden, squares = decode_finish(p_new, inverse, new_rows, base, key_heads)
+    handed_values = append(part, new_rows, squares)
     squares = sum_over(squares, "tp")
     decode_normed = normed(hidden, squares[0]).reshape(decode_residual.shape)
     whole = lambda x: x.reshape(1, positions, key_heads, head_size)

time: 102 us -> 101 us (level)
  waiting for transfers between devices: 39.2 us -> 37.1 us
    ppermute x2 -> x3, waiting for transfers between devices: 3.23 us -> 1.18 us  [sum_over(): lax.ppermute(value, axis, [(i, i ^ step) for i in range(count)])]
  transfers between devices with their start and end apart: 6 -> 7, of which waited for: 5 -> 5; matrix products, arithmetic and copies ran while one was open for 7% -> 7% of each run, Pallas kernels for 34% -> 35%
where the time goes in v3:
time: 101 us
  waiting for transfers between devices  37.1 us (37%)
  Pallas kernels  36.4 us (36%)
  starting transfers between devices  9 us (9%)
  local copies, waits for them, and re-layouts  6.52 us (6%)
  blocking collectives  5.75 us (6%)
  other arithmetic  5.15 us (5%)
    ppermute x4, waiting for transfers between devices, from_behind(): return lax.ppermute(value, axis, pairs)  36 us
    pallas_call x1, Pallas kernels, prefill(): pl.pallas_call(functools.partial(prefill_kernel, block=block, past=positi...  30.6 us
    ppermute x4, starting transfers between devices, from_behind(): return lax.ppermute(value, axis, pairs)  7.13 us
    unnamed x29, local copies, waits for them, and re-layouts  6.36 us
    psum x1, blocking collectives, local(): prefill_normed = normed(hidden, lax.psum(jnp.sum(squares, axis=1), 'tp'))  5.75 us
    convert_element_type x2, other arithmetic, normed(): return (hidden * scale[..., None] * gain_wide).astype(jnp.bfloat16)  4.77 us
    pallas_call x1, Pallas kernels, decode_scores(): pl.pallas_call(functools.partial(scores_kernel, steps=steps), in_specs=[V...  3.25 us
  transfers between devices with their start and end apart: 7, of which 5 were waited for; matrix products, arithmetic and copies ran while one was open for 7% of the time, Pallas kernels for 35%

profile of v3, /device:TPU:0, one launch (start us, length us, event | category | flops | bytes accessed | tf_op | source)
XLA Modules:
  0.0 100.8 jit_solution(15546803568714201739)
XLA Ops:
  0.7 4.1 %collective-permute-start = (bf16[1,1536,2,128]{3,2,1,0:T(2,128)(2,1)}, bf16[1,1536,2,128]{3,2,1,0:T(2,128)(2,1)S(1)}, u32[]{:S(2)}, u32[]{:S(2)}) collective-permute-start(bf16[1,1536,2,128]{3,2,1,0:T(2,128)(2,1)} %param.12), channel_id=1, source_target_pairs={{0,8},{4,12},{8,0},{12,4},{1,9},{5,13},{9,1},{13,5},{2,10},{6,14},... | collective-permute-start | bytes 2359304 | tf_op jit(solution)/shard_map/ppermute | solution.py:17
  4.8 0.1 collective-permute-start.1
  4.9 2.8 %collective-permute-start.3 = (bf16[1,1536,2,128]{3,2,1,0:T(2,128)(2,1)}, bf16[1,1536,2,128]{3,2,1,0:T(2,128)(2,1)S(1)}, u32[]{:S(2)}, u32[]{:S(2)}) collective-permute-start(bf16[1,1536,2,128]{3,2,1,0:T(2,128)(2,1)} %param.13), channel_id=1, source_target_pairs={{0,8},{4,12},{8,0},{12,4},{1,9},{5,13},{9,1},{13,5},{2,10},{6,14},... | collective-permute-start | bytes 2359304 | tf_op jit(solution)/shard_map/ppermute | solution.py:17
  7.7 0.1 collective-permute-start.2
  7.8 1.2 %copy.33 = bf16[1,1536,2,128]{3,1,2,0:T(8,128)(2,1)S(1)} copy(bf16[1,1536,2,128]{3,2,1,0:T(2,128)(2,1)} %param.12) | data formatting | bytes 1572864 | tf_op args[0]
  9.0 1.0 copy.35
  10.0 0.1 copy.32
  10.2 0.5 copy.31
  10.8 0.1 maximum_bitcast_fusion.k_ref
  10.9 0.1 maximum_bitcast_fusion.1.v_ref
  10.9 1.4 %copy-done.2 = bf16[1,512,2048]{2,1,0:T(8,128)(2,1)S(1)} copy-done((bf16[1,512,2048]{2,1,0:T(8,128)(2,1)S(1)}, bf16[1,512,2048]{2,1,0:T(8,128)(2,1)}, u32[]{:S(2)}) %copy-start.2) | copy-done | bytes 2097176
  12.4 30.6 %prefill.1 = (f32[512,2048]{1,0:T(8,128)S(1)}, f32[512,128]{1,0:T(8,128)S(1)}) custom-call(bf16[16,512,128]{2,1,0:T(8,128)(2,1)S(1)} %bitcast.45, bf16[2,2048,128]{2,1,0:T(8,128)(2,1)S(1)} %maximum_bitcast_fusion.k_ref, bf16[2,2048,128]{2,1,0:T(8,128)(2,1)S(1)} %maximum_bitcast_fusion.1.v_ref, bf16[512,2048]{1,0:T(8,128)(2,1)S(1)} %bitcast.53), custom_call_target="tpu_custom_call" | custom-call | flops 17179869184 | bytes 10485760 | tf_op jit(solution)/shard_map/prefill/pallas_call | solution.py:77
  43.0 2.0 %copy-done = f32[512,2048]{1,0:T(8,128)} copy-done((f32[512,2048]{1,0:T(8,128)}, f32[512,2048]{1,0:T(8,128)S(1)}, u32[]{:S(2)}) %copy-start) | copy-done | bytes 4194328
  44.9 0.1 reduce_sum.9
  45.1 5.8 %psum.7 = f32[512]{0:T(512)S(1)} all-reduce(f32[512]{0:T(512)S(1)} %reduce_sum.9), channel_id=1, replica_groups=mesh['groups'=2,'pair'=4,'tp'=4] {'tp'}, use_global_device_ids=true, to_apply=%region_1.0 | all-reduce | flops 512 | bytes 4096 | tf_op jit(solution)/shard_map/psum | solution.py:360
  50.9 3.9 %multiply_convert_fusion = bf16[512,2048]{1,0:T(8,128)(2,1)} fusion(f32[512,2048]{1,0:T(8,128)} %copy-done, f32[2048]{0:T(1024)S(1)} %convert_element_type.9, f32[512]{0:T(512)S(1)} %add_rsqrt_fusion), kind=kLoop, calls=%fused_computation | loop fusion | flops 3145728 | bytes 6301696 | tf_op jit(solution)/shard_map/convert_element_type | solution.py:354
  54.8 0.1 copy.22
  54.9 0.1 add_bitcast_fusion
  55.0 0.1 copy.24.cursor_ref
  55.1 18.8 %collective-permute-done.1 = bf16[1,512,2,128]{3,2,1,0:T(2,128)(2,1)S(1)} collective-permute-done((bf16[1,512,2,128]{3,2,1,0:T(2,128)(2,1)}, bf16[1,512,2,128]{3,2,1,0:T(2,128)(2,1)S(1)}, u32[]{:S(2)}, u32[]{:S(2)}) %collective-permute-start.1) | collective-permute-done | bytes 262176 | tf_op jit(solution)/shard_map/ppermute | solution.py:17
  74.0 3.3 %decode_scores.1 = (bf16[1024,1536]{1,0:T(8,128)(2,1)S(1)}, bf16[1024,512]{1,0:T(8,128)(2,1)S(1)}, bf16[1024,64]{1,0:T(8,128)(2,1)S(1)}, f32[1024,128]{1,0:T(8,128)S(1)}, bf16[4096,128]{1,0:T(8,128)(2,1)}) custom-call(bf16[16,64,128]{2,1,0:T(8,128)(2,1)S(1)} %bitcast.50, bf16[3072,128]{1,0:T(8,128)(2,1)S(1)} %bitcast.54, bf16[1024,128]{1,0:T(8,128)(2,1)S(1)} %bitcast.55, ...), custom_call_target="tpu_custom_call" | custom-call | flops 2147483648 | bytes 4194304 | tf_op jit(solution)/shard_map/decode_scores/pallas_call | solution.py:176
  77.2 13.6 %collective-permute-done.3 = bf16[1,1536,2,128]{3,2,1,0:T(2,128)(2,1)S(1)} collective-permute-done((bf16[1,1536,2,128]{3,2,1,0:T(2,128)(2,1)}, bf16[1,1536,2,128]{3,2,1,0:T(2,128)(2,1)S(1)}, u32[]{:S(2)}, u32[]{:S(2)}) %collective-permute-start.3) | collective-permute-done | bytes 786464 | tf_op jit(solution)/shard_map/ppermute | solution.py:17
  90.8 1.2 %decode_mix.1 = (f32[64,2048]{1,0:T(8,128)S(1)}, bf16[4096,128]{1,0:T(8,128)(2,1)}) custom-call(bf16[1024,1536]{1,0:T(8,128)(2,1)S(1)} %get-tuple-element.22.p_old_ref, bf16[1024,64]{1,0:T(8,128)(2,1)S(1)} %get-tuple-element.23.p_own_ref, f32[1024,128]{1,0:T(8,128)S(1)} %get-tuple-element.24.inverse_ref, bf16[3072,128]{1,0:T(8,128)(2,1)S(1)} %bitcast.48, ...), custom_call_target="tpu_custom_call" | custom-call | flops 805306368 | bytes 3145728 | tf_op jit(solution)/shard_map/decode_mix/pallas_call | solution.py:229
  92.0 3.6 %collective-permute-done.2 = bf16[1,512,2,128]{3,2,1,0:T(2,128)(2,1)S(1)} collective-permute-done((bf16[1,512,2,128]{3,2,1,0:T(2,128)(2,1)}, bf16[1,512,2,128]{3,2,1,0:T(2,128)(2,1)S(1)}, u32[]{:S(2)}, u32[]{:S(2)}) %collective-permute-start.2) | collective-permute-done | bytes 262176 | tf_op jit(solution)/shard_map/ppermute | solution.py:17
  95.6 0.6 decode_finish.1
  96.2 0.2 collective-permute-start.4
  96.4 1.4 %collective-permute-start.5 = (f32[8,64]{1,0:T(8,128)S(1)}, f32[8,64]{1,0:T(8,128)S(1)}, u32[]{:S(2)}, u32[]{:S(2)}) collective-permute-start(f32[8,64]{1,0:T(8,128)S(1)} %get-tuple-element.28.after_ref), channel_id=1, source_target_pairs={{0,2},{1,3},{2,0},{3,1},{4,6},{5,7},{6,4},{7,5},{8,10},{9,11},{10,... | collective-permute-start | bytes 6152 | tf_op jit(solution)/shard_map/ppermute | solution.py:25
  97.8 0.3 collective-permute-start.6
  98.1 0.7 append.1
  98.8 0.5 collective-permute-done.4
  99.2 0.7 collective-permute-done.5
  100.0 0.8 multiply_convert_fusion.1
  (29 shorter events, 0.1 us)
Async XLA Ops:
  0.6 9.4 %copy-start.4 = (bf16[1,1536,2,128]{3,2,1,0:T(2,128)(2,1)S(1)}, bf16[1,1536,2,128]{3,2,1,0:T(2,128)(2,1)}, u32[]{:S(2)}) copy-start(bf16[1,1536,2,128]{3,2,1,0:T(2,128)(2,1)} %param.13) | copy-start | bytes 2359300
  0.6 9.5 %copy-start.6 = (bf16[1,512,2,128]{3,2,1,0:T(2,128)(2,1)S(1)}, bf16[1,512,2,128]{3,2,1,0:T(2,128)(2,1)}, u32[]{:S(2)}) copy-start(bf16[1,512,2,128]{3,2,1,0:T(2,128)(2,1)} %param.16) | copy-start | bytes 786436
  0.7 9.6 %copy-start.3 = (bf16[1,512,16,128]{3,2,1,0:T(8,128)(2,1)S(1)}, bf16[1,512,16,128]{3,2,1,0:T(8,128)(2,1)}, u32[]{:S(2)}) copy-start(bf16[1,512,16,128]{3,2,1,0:T(8,128)(2,1)} %param.14) | copy-start | bytes 6291460
  0.7 73.3 %collective-permute-start = (bf16[1,1536,2,128]{3,2,1,0:T(2,128)(2,1)}, bf16[1,1536,2,128]{3,2,1,0:T(2,128)(2,1)S(1)}, u32[]{:S(2)}, u32[]{:S(2)}) collective-permute-start(bf16[1,1536,2,128]{3,2,1,0:T(2,128)(2,1)} %param.12), channel_id=1, source_target_pairs={{0,8},{4,12},{8,0},{12,4},{1,9},{5,13},{9,1},{13,5},{2,10},{6,14},... | collective-permute-start | bytes 2359304 | tf_op jit(solution)/shard_map/ppermute | solution.py:17
  4.8 69.2 %collective-permute-start.1 = (bf16[1,512,2,128]{3,2,1,0:T(2,128)(2,1)}, bf16[1,512,2,128]{3,2,1,0:T(2,128)(2,1)S(1)}, u32[]{:S(2)}, u32[]{:S(2)}) collective-permute-start(bf16[1,512,2,128]{3,2,1,0:T(2,128)(2,1)} %param.15), channel_id=1, source_target_pairs={{0,8},{4,12},{8,0},{12,4},{1,9},{5,13},{9,1},{13,5},{2,10},{6,14},... | collective-permute-start | bytes 786440 | tf_op jit(solution)/shard_map/ppermute | solution.py:17
  4.9 85.9 %collective-permute-start.3 = (bf16[1,1536,2,128]{3,2,1,0:T(2,128)(2,1)}, bf16[1,1536,2,128]{3,2,1,0:T(2,128)(2,1)S(1)}, u32[]{:S(2)}, u32[]{:S(2)}) collective-permute-start(bf16[1,1536,2,128]{3,2,1,0:T(2,128)(2,1)} %param.13), channel_id=1, source_target_pairs={{0,8},{4,12},{8,0},{12,4},{1,9},{5,13},{9,1},{13,5},{2,10},{6,14},... | collective-permute-start | bytes 2359304 | tf_op jit(solution)/shard_map/ppermute | solution.py:17
  7.7 87.9 %collective-permute-start.2 = (bf16[1,512,2,128]{3,2,1,0:T(2,128)(2,1)}, bf16[1,512,2,128]{3,2,1,0:T(2,128)(2,1)S(1)}, u32[]{:S(2)}, u32[]{:S(2)}) collective-permute-start(bf16[1,512,2,128]{3,2,1,0:T(2,128)(2,1)} %param.16), channel_id=1, source_target_pairs={{0,8},{4,12},{8,0},{12,4},{1,9},{5,13},{9,1},{13,5},{2,10},{6,14},... | collective-permute-start | bytes 786440 | tf_op jit(solution)/shard_map/ppermute | solution.py:17
  10.8 1.6 %copy-start.2 = (bf16[1,512,2048]{2,1,0:T(8,128)(2,1)S(1)}, bf16[1,512,2048]{2,1,0:T(8,128)(2,1)}, u32[]{:S(2)}) copy-start(bf16[1,512,2048]{2,1,0:T(8,128)(2,1)} %param.17) | copy-start | bytes 6291460
  12.4 38.5 %copy-start.9 = (bf16[2048]{0:T(1024)(128)(2,1)S(1)}, bf16[2048]{0:T(1024)(128)(2,1)}, u32[]{:S(2)}) copy-start(bf16[2048]{0:T(1024)(128)(2,1)} %param.23) | copy-start | bytes 12292
  42.9 2.0 %copy-start = (f32[512,2048]{1,0:T(8,128)}, f32[512,2048]{1,0:T(8,128)S(1)}, u32[]{:S(2)}) copy-start(f32[512,2048]{1,0:T(8,128)S(1)} %get-tuple-element.17) | copy-start | bytes 12582916
  50.8 4.0 %copy-start.5 = (bf16[1,2,32,16,128]{4,3,2,1,0:T(8,128)(2,1)S(1)}, bf16[1,2,32,16,128]{4,3,2,1,0:T(8,128)(2,1)}, u32[]{:S(2)}) copy-start(bf16[1,2,32,16,128]{4,3,2,1,0:T(8,128)(2,1)} %param.18) | copy-start | bytes 786436
  50.8 4.1 %copy-start.10 = (s32[1,32]{1,0:T(1,128)S(1)}, s32[1,32]{1,0:T(1,128)}, u32[]{:S(2)}) copy-start(s32[1,32]{1,0:T(1,128)} %param.22) | copy-start | bytes 388
  50.9 4.2 %copy-start.7 = (bf16[1,2,32,2,128]{4,3,2,1,0:T(2,128)(2,1)S(1)}, bf16[1,2,32,2,128]{4,3,2,1,0:T(2,128)(2,1)}, u32[]{:S(2)}) copy-start(bf16[1,2,32,2,128]{4,3,2,1,0:T(2,128)(2,1)} %param.19) | copy-start | bytes 98308
  50.9 4.2 %copy-start.8 = (bf16[1,2,32,2,128]{4,3,2,1,0:T(2,128)(2,1)S(1)}, bf16[1,2,32,2,128]{4,3,2,1,0:T(2,128)(2,1)}, u32[]{:S(2)}) copy-start(bf16[1,2,32,2,128]{4,3,2,1,0:T(2,128)(2,1)} %param.20) | copy-start | bytes 98308
  74.0 16.9 %copy-start.1 = (bf16[1,2,32,2048]{3,2,1,0:T(8,128)(2,1)S(1)}, bf16[1,2,32,2048]{3,2,1,0:T(8,128)(2,1)}, u32[]{:S(2)}) copy-start(bf16[1,2,32,2048]{3,2,1,0:T(8,128)(2,1)} %param.21) | copy-start | bytes 786436
  96.2 3.0 %collective-permute-start.4 = (f32[8,64]{1,0:T(8,128)S(1)}, f32[8,64]{1,0:T(8,128)S(1)}, u32[]{:S(2)}, u32[]{:S(2)}) collective-permute-start(f32[8,64]{1,0:T(8,128)S(1)} %get-tuple-element.28.after_ref), channel_id=1, source_target_pairs={{0,3},{1,2},{2,1},{3,0},{4,7},{5,6},{6,5},{7,4},{8,11},{9,10},{10,... | collective-permute-start | bytes 6152 | tf_op jit(solution)/shard_map/ppermute | solution.py:25
  96.4 3.6 %collective-permute-start.5 = (f32[8,64]{1,0:T(8,128)S(1)}, f32[8,64]{1,0:T(8,128)S(1)}, u32[]{:S(2)}, u32[]{:S(2)}) collective-permute-start(f32[8,64]{1,0:T(8,128)S(1)} %get-tuple-element.28.after_ref), channel_id=1, source_target_pairs={{0,2},{1,3},{2,0},{3,1},{4,6},{5,7},{6,4},{7,5},{8,10},{9,11},{10,... | collective-permute-start | bytes 6152 | tf_op jit(solution)/shard_map/ppermute | solution.py:25
  97.8 2.2 %collective-permute-start.6 = (f32[8,64]{1,0:T(8,128)S(1)}, f32[8,64]{1,0:T(8,128)S(1)}, u32[]{:S(2)}, u32[]{:S(2)}) collective-permute-start(f32[8,64]{1,0:T(8,128)S(1)} %get-tuple-element.28.after_ref), channel_id=1, source_target_pairs={{0,1},{1,0},{2,3},{3,2},{4,5},{5,4},{6,7},{7,6},{8,9},{9,8},{10,11... | collective-permute-start | bytes 6152 | tf_op jit(solution)/shard_map/ppermute | solution.py:25

commit v4 on v3

--- a/solution.py
+++ b/solution.py
@@ -9,6 +9,7 @@
 
 epsilon = 1e-05
 log2_e = 1.4426950408889634
+late_rows = 128
 
 
 def from_behind(value, axis, steps):
@@ -114,7 +115,7 @@
     q_ref, old_ref, new_ref, own_ref, cursor_ref,
     p_old_ref, p_new_ref, p_own_ref, inverse_ref, handed_ref,
     wide_ref, keys_ref, sems,
-    *, steps,
+    *, steps, early, late,
 ):
     heads, rows, head_size = q_ref.shape
     key_heads, own_count, _ = own_ref.shape
@@ -151,8 +152,12 @@
         own = jnp.exp2((own - top) * factor)
         total = jnp.sum(far, axis=1, keepdims=True) + jnp.sum(own, axis=1, keepdims=True)
         far = far.astype(jnp.bfloat16)
-        p_old_ref[here] = far[:, : past // key_heads]
-        p_new_ref[here] = far[:, past // key_heads :]
+        for p_ref, chunks in ((p_old_ref, early), (p_new_ref, late)):
+            first_column = 0
+            for start, stop in chunks:
+                columns = slice(first_column, first_column + stop - start)
+                p_ref[here, columns] = far[:, start:stop]
+                first_column = columns.stop
         p_own_ref[here] = own.astype(jnp.bfloat16)
         inverse_ref[here] = jnp.broadcast_to(1.0 / total, (block, head_size))
     for copy in copies:
@@ -163,23 +168,45 @@
 VMEM = pl.BlockSpec(memory_space=pltpu.VMEM)
 
 
+def length(chunks):
+    return sum(stop - start for start, stop in chunks)
+
+
+def copies_of(refs, chunks, handed_ref, sems):
+    copies = []
+    for i, (ref, (start, stop)) in enumerate(zip(refs, chunks)):
+        per = ref.shape[0] // (stop - start)
+        copies.append(
+            pltpu.make_async_copy(ref, handed_ref.at[start * per : stop * per], sems.at[i])
+        )
+        copies[-1].start()
+    return copies
+
+
+def split_all(refs, chunks, wide_ref, out_ref):
+    first = 0
+    for ref, (start, stop) in zip(refs, chunks):
+        split_heads(ref, wide_ref, out_ref, first)
+        first += stop - start
+
+
 def room(mib):
     return pltpu.CompilerParams(vmem_limit_bytes=mib << 20)
 
 
-def decode_scores(queries, old_keys, new_keys, own_keys, cursor, steps):
+def decode_scores(queries, old_keys, new_keys, own_keys, cursor, steps, early, late):
     heads, rows, head_size = queries.shape
     key_heads, own_count, _ = own_keys.shape
     past = old_keys.shape[0] // key_heads
     span = new_keys.shape[0] // key_heads
     every = heads * rows
     return pl.pallas_call(
-        functools.partial(scores_kernel, steps=steps),
+        functools.partial(scores_kernel, steps=steps, early=early, late=late),
         in_specs=[VMEM] * 5,
         out_specs=[VMEM] * 4 + [HBM],
         out_shape=[
-            jax.ShapeDtypeStruct((every, past), jnp.bfloat16),
-            jax.ShapeDtypeStruct((every, span), jnp.bfloat16),
+            jax.ShapeDtypeStruct((every, length(early)), jnp.bfloat16),
+            jax.ShapeDtypeStruct((every, length(late)), jnp.bfloat16),
             jax.ShapeDtypeStruct((every, own_count), jnp.bfloat16),
             jax.ShapeDtypeStruct((every, head_size), jnp.float32),
             jax.ShapeDtypeStruct((key_heads * (past + span), head_size), jnp.bfloat16),
@@ -199,18 +226,16 @@
     )(queries, old_keys, new_keys, own_keys, cursor)
 
 
-def mix_kernel(
-    p_old_ref, p_own_ref, inverse_ref, old_ref, own_ref, residual_ref,
-    base_ref, handed_ref,
-    wide_ref, values_ref, sem,
-):
+def mix_kernel(*refs, early):
+    p_old_ref, p_own_ref, inverse_ref, own_ref, residual_ref = refs[:5]
+    chunk_refs = refs[5 : 5 + len(early)]
+    base_ref, handed_ref, wide_ref, values_ref, sems = refs[5 + len(early) :]
     rows = residual_ref.shape[0]
     key_heads, _, head_size = own_ref.shape
     heads = p_old_ref.shape[0] // rows
     per = heads // key_heads
-    copy = pltpu.make_async_copy(old_ref, handed_ref.at[: old_ref.shape[0]], sem)
-    copy.start()
-    split_heads(old_ref, wide_ref, values_ref, 0)
+    copies = copies_of(chunk_refs, early, handed_ref, sems)
+    split_all(chunk_refs, early, wide_ref, values_ref)
     for g in range(key_heads):
         here = slice(g * per * rows, (g + 1) * per * rows)
         mixed = jnp.dot(p_old_ref[here], values_ref[g], preferred_element_type=jnp.float32)
@@ -221,25 +246,25 @@
             base_ref[:, lanes] = mixed[h * rows : (h + 1) * rows] + residual_ref[:, lanes].astype(
                 jnp.float32
             )
-    copy.wait()
-
-
-def decode_mix(p_old, p_own, inverse, old_values, own_values, residual, positions):
+    for copy in copies:
+        copy.wait()
+
+
+def decode_mix(p_old, p_own, inverse, own_values, residual, chunk_values, early, positions):
     key_heads, _, head_size = own_values.shape
+    most = max(x.shape[0] for x in chunk_values)
     return pl.pallas_call(
-        mix_kernel,
-        in_specs=[VMEM] * 6,
+        functools.partial(mix_kernel, early=early),
+        in_specs=[VMEM] * (5 + len(early)),
         out_specs=[VMEM, HBM],
         out_shape=[
             jax.ShapeDtypeStruct(residual.shape, jnp.float32),
             jax.ShapeDtypeStruct((key_heads * positions, head_size), jnp.bfloat16),
         ],
         scratch_shapes=[
-            pltpu.VMEM(old_values.shape, jnp.float32),
-            pltpu.VMEM(
-                (key_heads, old_values.shape[0] // key_heads, head_size), jnp.bfloat16
-            ),
-            pltpu.SemaphoreType.DMA(()),
+            pltpu.VMEM((most, head_size), jnp.float32),
+            pltpu.VMEM((key_heads, length(early), head_size), jnp.bfloat16),
+            pltpu.SemaphoreType.DMA((len(early),)),
         ],
         compiler_params=room(16),
         cost_estimate=pl.CostEstimate(
@@ -248,19 +273,18 @@
             bytes_accessed=2 * p_old.shape[0] * p_old.shape[1],
         ),
         name="decode_mix",
-    )(p_old, p_own, inverse, old_values, own_values, residual)
-
-
-def finish_kernel(
-    p_new_ref, inverse_ref, new_ref, base_ref,
-    hidden_ref, squares_ref,
-    wide_ref, values_ref,
-):
+    )(p_old, p_own, inverse, own_values, residual, *chunk_values)
+
+
+def finish_kernel(*refs, late):
+    p_new_ref, inverse_ref, base_ref = refs[:3]
+    chunk_refs = refs[3 : 3 + len(late)]
+    hidden_ref, squares_ref, wide_ref, values_ref = refs[3 + len(late) :]
     rows = base_ref.shape[0]
     key_heads, _, head_size = values_ref.shape
     heads = p_new_ref.shape[0] // rows
     per = heads // key_heads
-    split_heads(new_ref, wide_ref, values_ref, 0)
+    split_all(chunk_refs, late, wide_ref, values_ref)
     squares = jnp.zeros((rows, head_size), jnp.float32)
     for g in range(key_heads):
         here = slice(g * per * rows, (g + 1) * per * rows)
@@ -275,22 +299,21 @@
     squares_ref[...] = jnp.transpose(squares)[:8]
 
 
-def decode_finish(p_new, inverse, new_values, base, key_heads):
+def decode_finish(p_new, inverse, base, chunk_values, late):
     rows, features = base.shape
-    head_size = new_values.shape[1]
+    most, head_size = max(x.shape for x in chunk_values)
+    key_heads = sum(x.shape[0] for x in chunk_values) // length(late)
     return pl.pallas_call(
-        finish_kernel,
-        in_specs=[VMEM] * 4,
+        functools.partial(finish_kernel, late=late),
+        in_specs=[VMEM] * (3 + len(late)),
         out_specs=[VMEM] * 2,
         out_shape=[
             jax.ShapeDtypeStruct((rows, features), jnp.float32),
             jax.ShapeDtypeStruct((8, rows), jnp.float32),
         ],
         scratch_shapes=[
-            pltpu.VMEM(new_values.shape, jnp.float32),
-            pltpu.VMEM(
-                (key_heads, new_values.shape[0] // key_heads, head_size), jnp.bfloat16
-            ),
+            pltpu.VMEM((most, head_size), jnp.float32),
+            pltpu.VMEM((key_heads, length(late), head_size), jnp.bfloat16),
         ],
         compiler_params=room(8),
         cost_estimate=pl.CostEstimate(
@@ -299,31 +322,31 @@
             bytes_accessed=2 * p_new.shape[0] * p_new.shape[1],
         ),
         name="decode_finish",
-    )(p_new, inverse, new_values, base)
-
-
-def append_kernel(new_ref, part_ref, after_ref, handed_ref, sem):
-    copy = pltpu.make_async_copy(
-        new_ref, handed_ref.at[handed_ref.shape[0] - new_ref.shape[0] :], sem
-    )
-    copy.start()
-    copy.wait()
-
-
-def append(part, new, after):
+    )(p_new, inverse, base, *chunk_values)
+
+
+def append_kernel(*refs, late):
+    *chunk_refs, _, _, handed_ref, sems = refs
+    for copy in copies_of(chunk_refs, late, handed_ref, sems):
+        copy.wait()
+
+
+def append(part, chunk_values, late, after):
     return pl.pallas_call(
-        append_kernel,
-        in_specs=[VMEM, HBM, VMEM],
+        functools.partial(append_kernel, late=late),
+        in_specs=[VMEM] * len(late) + [HBM, VMEM],
         out_specs=HBM,
         out_shape=jax.ShapeDtypeStruct(part.shape, part.dtype),
-        scratch_shapes=[pltpu.SemaphoreType.DMA(())],
-        input_output_aliases={1: 0},
+        scratch_shapes=[pltpu.SemaphoreType.DMA((len(late),))],
+        input_output_aliases={len(late): 0},
         compiler_params=room(2),
         cost_estimate=pl.CostEstimate(
-            flops=1000000, transcendentals=0, bytes_accessed=4 * new.size
+            flops=1000000,
+            transcendentals=0,
+            bytes_accessed=4 * sum(x.size for x in chunk_values),
         ),
         name="append",
-    )(new, part, after)
+    )(*chunk_values, part, after)
 
 
 def local(
@@ -345,8 +368,23 @@
     width = norm_gain.shape[0] * lax.axis_size("tp")
     old_keys = from_behind(prompt_keys, "pair", halfway)
     new_keys = from_behind(span_keys, "pair", halfway)
-    old_values = from_behind(prompt_values, "pair", halfway)
-    new_values = from_behind(span_values, "pair", halfway)
+    past, span = prompt_values.shape[1], span_values.shape[1]
+    late_past, late_span = min(late_rows, past), min(late_rows, span)
+    early = ((0, past - late_past), (past, past + span - late_span))
+    late = ((past - late_past, past), (past + span - late_span, past + span))
+    early, late = [[(a, b) for a, b in chunks if b > a] for chunks in (early, late)]
+
+    def received(chunk):
+        start, stop = chunk
+        if start < past:
+            rows = prompt_values[:, start:stop]
+        else:
+            rows = span_values[:, start - past : stop - past]
+        rows = from_behind(rows, "pair", halfway)[0]
+        return rows.reshape(-1, rows.shape[-1])
+
+    early_values = [received(chunk) for chunk in early]
+    late_values = [received(chunk) for chunk in late]
     gain_wide = norm_gain.astype(jnp.float32)
 
     def normed(hidden, squares):
@@ -373,15 +411,16 @@
         head_major(flat(decode_keys)),
         limits,
         steps,
+        early,
+        late,
     )
     positions, key_heads, _ = keys_shape
     base, part = decode_mix(
-        p_old, p_own, inverse, mixed_rows(old_values), own_values,
-        decode_residual[0].reshape(rows, -1), positions,
+        p_old, p_own, inverse, own_values, decode_residual[0].reshape(rows, -1),
+        early_values, early, positions,
     )
-    new_rows = mixed_rows(new_values)
-    hidden, squares = decode_finish(p_new, inverse, new_rows, base, key_heads)
-    handed_values = append(part, new_rows, squares)
+    hidden, squares = decode_finish(p_new, inverse, base, late_values, late)
+    handed_values = append(part, late_values, late, squares)
     squares = sum_over(squares, "tp")
     decode_normed = normed(hidden, squares[0]).reshape(decode_residual.shape)
     whole = lambda x: x.reshape(1, positions, key_heads, head_size)

time: 101 us -> 101 us (level)
  waiting for transfers between devices: 37.1 us -> 31 us
  starting transfers between devices: 9 us -> 11.9 us
  local copies, waits for them, and re-layouts: 6.52 us -> 9.34 us
    ppermute x4 -> x6, waiting for transfers between devices: 36 us -> 29.8 us  [from_behind(): return lax.ppermute(value, axis, pairs)]
    slice x0 -> x4, local copies, waits for them, and re-layouts: none -> 4.9 us  [the longest x2 3.12 us: received(): rows = prompt_values[:, start:stop]]
    ppermute x4 -> x6, starting transfers between devices: 7.13 us -> 10 us  [from_behind(): return lax.ppermute(value, axis, pairs)]
    unnamed x29 -> x33, local copies, waits for them, and re-layouts: 6.36 us -> 4.27 us
  transfers between devices with their start and end apart: 7 -> 9, of which waited for: 5 -> 5; matrix products, arithmetic and copies ran while one was open for 7% -> 10% of each run, Pallas kernels for 35% -> 36%
where the time goes in v4:
time: 101 us
  Pallas kernels  36.4 us (36%)
  waiting for transfers between devices  31 us (31%)
  starting transfers between devices  11.9 us (12%)
  local copies, waits for them, and re-layouts  9.34 us (9%)
  blocking collectives  5.96 us (6%)
  other arithmetic  5.15 us (5%)
    pallas_call x1, Pallas kernels, prefill(): pl.pallas_call(functools.partial(prefill_kernel, block=block, past=positi...  30.6 us
    ppermute x6, waiting for transfers between devices, from_behind(): return lax.ppermute(value, axis, pairs)  29.8 us
    ppermute x6, starting transfers between devices, from_behind(): return lax.ppermute(value, axis, pairs)  10 us
    psum x1, blocking collectives, local(): prefill_normed = normed(hidden, lax.psum(jnp.sum(squares, axis=1), 'tp'))  5.96 us
    convert_element_type x2, other arithmetic, normed(): return (hidden * scale[..., None] * gain_wide).astype(jnp.bfloat16)  4.77 us
    unnamed x33, local copies, waits for them, and re-layouts  4.27 us
    pallas_call x1, Pallas kernels, decode_scores(): pl.pallas_call(functools.partial(scores_kernel, steps=steps, early=early,...  3.3 us
    slice x2, local copies, waits for them, and re-layouts, received(): rows = prompt_values[:, start:stop]  3.12 us
  transfers between devices with their start and end apart: 9, of which 5 were waited for; matrix products, arithmetic and copies ran while one was open for 10% of the time, Pallas kernels for 36%

profile of v4, /device:TPU:0, one launch (start us, length us, event | category | flops | bytes accessed | tf_op | source)
XLA Modules:
  0.0 100.6 jit_solution(1464804230356879470)
XLA Ops:
  0.7 4.1 %collective-permute-start = (bf16[1,1536,2,128]{3,2,1,0:T(2,128)(2,1)}, bf16[1,1536,2,128]{3,2,1,0:T(2,128)(2,1)S(1)}, u32[]{:S(2)}, u32[]{:S(2)}) collective-permute-start(bf16[1,1536,2,128]{3,2,1,0:T(2,128)(2,1)} %param.12), channel_id=1, source_target_pairs={{0,8},{4,12},{8,0},{12,4},{1,9},{5,13},{9,1},{13,5},{2,10},{6,14},... | collective-permute-start | bytes 2359304 | tf_op jit(solution)/shard_map/ppermute | solution.py:18
  4.8 0.1 collective-permute-start.1
  4.9 2.2 %slice.17 = bf16[1,1408,2,128]{3,2,1,0:T(2,128)(2,1)} slice(bf16[1,1536,2,128]{3,2,1,0:T(2,128)(2,1)} %param.13), slice={[0:1], [0:1408], [0:2], [0:128]} | slice | bytes 1441792 | tf_op jit(solution)/shard_map/slice | solution.py:380
  7.1 2.8 %collective-permute-start.4 = (bf16[1,1408,2,128]{3,2,1,0:T(2,128)(2,1)}, bf16[1,1408,2,128]{3,2,1,0:T(2,128)(2,1)S(1)}, u32[]{:S(2)}, u32[]{:S(2)}) collective-permute-start(bf16[1,1408,2,128]{3,2,1,0:T(2,128)(2,1)} %slice.17), channel_id=1, source_target_pairs={{0,8},{4,12},{8,0},{12,4},{1,9},{5,13},{9,1},{13,5},{2,10},{6,14},... | collective-permute-start | bytes 2162696 | tf_op jit(solution)/shard_map/ppermute | solution.py:18
  10.0 1.7 %slice.18 = bf16[1,384,2,128]{3,2,1,0:T(2,128)(2,1)} slice(bf16[1,512,2,128]{3,2,1,0:T(2,128)(2,1)} %param.16), slice={[0:1], [0:384], [0:2], [0:128]} | slice | bytes 393216 | tf_op jit(solution)/shard_map/slice | solution.py:382
  11.7 0.1 collective-permute-start.5
  11.8 0.9 slice.15
  12.7 2.9 %collective-permute-start.2 = (bf16[1,128,2,128]{3,2,1,0:T(2,128)(2,1)S(1)}, bf16[1,128,2,128]{3,2,1,0:T(2,128)(2,1)S(1)}, u32[]{:S(2)}, u32[]{:S(2)}) collective-permute-start(bf16[1,128,2,128]{3,2,1,0:T(2,128)(2,1)S(1)} %slice.15), channel_id=1, source_target_pairs={{0,8},{4,12},{8,0},{12,4},{1,9},{5,13},{9,1},{13,5},{2,10},{6,14},... | collective-permute-start | bytes 196616 | tf_op jit(solution)/shard_map/ppermute | solution.py:18
  15.6 0.1 copy.33
  15.8 0.1 copy.32
  15.9 0.5 copy.31
  16.6 1.4 %copy-done.2 = bf16[1,512,2048]{2,1,0:T(8,128)(2,1)S(1)} copy-done((bf16[1,512,2048]{2,1,0:T(8,128)(2,1)S(1)}, bf16[1,512,2048]{2,1,0:T(8,128)(2,1)}, u32[]{:S(2)}) %copy-start.2) | copy-done | bytes 2097176
  18.1 30.6 %prefill.1 = (f32[512,2048]{1,0:T(8,128)S(1)}, f32[512,128]{1,0:T(8,128)S(1)}) custom-call(bf16[16,512,128]{2,1,0:T(8,128)(2,1)S(1)} %bitcast.47, bf16[2,2048,128]{2,1,0:T(8,128)(2,1)S(1)} %maximum_bitcast_fusion.k_ref, bf16[2,2048,128]{2,1,0:T(8,128)(2,1)S(1)} %maximum_bitcast_fusion.1.v_ref, bf16[512,2048]{1,0:T(8,128)(2,1)S(1)} %bitcast.58), custom_call_target="tpu_custom_call" | custom-call | flops 17179869184 | bytes 10485760 | tf_op jit(solution)/shard_map/prefill/pallas_call | solution.py:78
  48.7 1.9 %copy-done = f32[512,2048]{1,0:T(8,128)} copy-done((f32[512,2048]{1,0:T(8,128)}, f32[512,2048]{1,0:T(8,128)S(1)}, u32[]{:S(2)}) %copy-start) | copy-done | bytes 4194328
  50.6 0.1 reduce_sum.9
  50.8 6.0 %psum.7 = f32[512]{0:T(512)S(1)} all-reduce(f32[512]{0:T(512)S(1)} %reduce_sum.9), channel_id=1, replica_groups=mesh['groups'=2,'pair'=4,'tp'=4] {'tp'}, use_global_device_ids=true, to_apply=%region_1.0 | all-reduce | flops 512 | bytes 4096 | tf_op jit(solution)/shard_map/psum | solution.py:398
  56.8 3.9 %multiply_convert_fusion = bf16[512,2048]{1,0:T(8,128)(2,1)} fusion(f32[512,2048]{1,0:T(8,128)} %copy-done, f32[2048]{0:T(1024)S(1)} %convert_element_type.9, f32[512]{0:T(512)S(1)} %add_rsqrt_fusion), kind=kLoop, calls=%fused_computation | loop fusion | flops 3145728 | bytes 6301696 | tf_op jit(solution)/shard_map/convert_element_type | solution.py:392
  60.9 0.1 add_bitcast_fusion
  61.0 0.1 copy.24.cursor_ref
  61.1 11.4 %collective-permute-done.1 = bf16[1,512,2,128]{3,2,1,0:T(2,128)(2,1)S(1)} collective-permute-done((bf16[1,512,2,128]{3,2,1,0:T(2,128)(2,1)}, bf16[1,512,2,128]{3,2,1,0:T(2,128)(2,1)S(1)}, u32[]{:S(2)}, u32[]{:S(2)}) %collective-permute-start.1) | collective-permute-done | bytes 262176 | tf_op jit(solution)/shard_map/ppermute | solution.py:18
  72.6 3.3 %decode_scores.1 = (bf16[1024,1792]{1,0:T(8,128)(2,1)S(1)}, bf16[1024,256]{1,0:T(8,128)(2,1)S(1)}, bf16[1024,64]{1,0:T(8,128)(2,1)S(1)}, f32[1024,128]{1,0:T(8,128)S(1)}, bf16[4096,128]{1,0:T(8,128)(2,1)}) custom-call(bf16[16,64,128]{2,1,0:T(8,128)(2,1)S(1)} %bitcast.50, bf16[3072,128]{1,0:T(8,128)(2,1)S(1)} %bitcast.59, bf16[1024,128]{1,0:T(8,128)(2,1)S(1)} %bitcast.60, ...), custom_call_target="tpu_custom_call" | custom-call | flops 2147483648 | bytes 4194304 | tf_op jit(solution)/shard_map/decode_scores/pallas_call | solution.py:203
  75.9 17.7 %collective-permute-done.5 = bf16[1,384,2,128]{3,2,1,0:T(2,128)(2,1)S(1)} collective-permute-done((bf16[1,384,2,128]{3,2,1,0:T(2,128)(2,1)}, bf16[1,384,2,128]{3,2,1,0:T(2,128)(2,1)S(1)}, u32[]{:S(2)}, u32[]{:S(2)}) %collective-permute-start.5) | collective-permute-done | bytes 196640 | tf_op jit(solution)/shard_map/ppermute | solution.py:18
  93.6 1.3 %decode_mix.1 = (f32[64,2048]{1,0:T(8,128)S(1)}, bf16[4096,128]{1,0:T(8,128)(2,1)}) custom-call(bf16[1024,1792]{1,0:T(8,128)(2,1)S(1)} %get-tuple-element.22.refs_0_, bf16[1024,64]{1,0:T(8,128)(2,1)S(1)} %get-tuple-element.23.refs_1_, f32[1024,128]{1,0:T(8,128)S(1)} %get-tuple-element.24.refs_2_.refs_1_, bf16[2,64,128]{2,1,0:T(8,128)(2,1)S(1)} %bitcast.56, ...), custom_call_target="tpu_custom_call" | custom-call | flops 939524096 | bytes 3670016 | tf_op jit(solution)/shard_map/decode_mix/pallas_call | solution.py:256
  95.0 0.6 collective-permute-done.3
  95.6 0.5 decode_finish.1
  96.0 0.2 collective-permute-start.6
  96.2 1.5 %collective-permute-start.7 = (f32[8,64]{1,0:T(8,128)S(1)}, f32[8,64]{1,0:T(8,128)S(1)}, u32[]{:S(2)}, u32[]{:S(2)}) collective-permute-start(f32[8,64]{1,0:T(8,128)S(1)} %get-tuple-element.28.refs_3_), channel_id=1, source_target_pairs={{0,2},{1,3},{2,0},{3,1},{4,6},{5,7},{6,4},{7,5},{8,10},{9,11},{10,... | collective-permute-start | bytes 6152 | tf_op jit(solution)/shard_map/ppermute | solution.py:26
  97.7 0.3 collective-permute-start.8
  97.9 0.7 append.1
  98.6 0.5 collective-permute-done.6
  99.1 0.7 collective-permute-done.7
  99.8 0.8 multiply_convert_fusion.1
  (41 shorter events, 0.4 us)
Async XLA Ops:
  0.6 15.0 %copy-start.6 = (bf16[1,1536,2,128]{3,2,1,0:T(2,128)(2,1)S(1)}, bf16[1,1536,2,128]{3,2,1,0:T(2,128)(2,1)}, u32[]{:S(2)}) copy-start(bf16[1,1536,2,128]{3,2,1,0:T(2,128)(2,1)} %param.12) | copy-start | bytes 2359300
  0.6 15.1 %copy-start.8 = (bf16[1,512,2,128]{3,2,1,0:T(2,128)(2,1)S(1)}, bf16[1,512,2,128]{3,2,1,0:T(2,128)(2,1)}, u32[]{:S(2)}) copy-start(bf16[1,512,2,128]{3,2,1,0:T(2,128)(2,1)} %param.15) | copy-start | bytes 786436
  0.7 15.1 %copy-start.3 = (bf16[1,1536,2,128]{3,2,1,0:T(2,128)(2,1)S(1)}, bf16[1,1536,2,128]{3,2,1,0:T(2,128)(2,1)}, u32[]{:S(2)}) copy-start(bf16[1,1536,2,128]{3,2,1,0:T(2,128)(2,1)} %param.13) | copy-start | bytes 2359300
  0.7 71.9 %collective-permute-start = (bf16[1,1536,2,128]{3,2,1,0:T(2,128)(2,1)}, bf16[1,1536,2,128]{3,2,1,0:T(2,128)(2,1)S(1)}, u32[]{:S(2)}, u32[]{:S(2)}) collective-permute-start(bf16[1,1536,2,128]{3,2,1,0:T(2,128)(2,1)} %param.12), channel_id=1, source_target_pairs={{0,8},{4,12},{8,0},{12,4},{1,9},{5,13},{9,1},{13,5},{2,10},{6,14},... | collective-permute-start | bytes 2359304 | tf_op jit(solution)/shard_map/ppermute | solution.py:18
  4.8 67.8 %collective-permute-start.1 = (bf16[1,512,2,128]{3,2,1,0:T(2,128)(2,1)}, bf16[1,512,2,128]{3,2,1,0:T(2,128)(2,1)S(1)}, u32[]{:S(2)}, u32[]{:S(2)}) collective-permute-start(bf16[1,512,2,128]{3,2,1,0:T(2,128)(2,1)} %param.15), channel_id=1, source_target_pairs={{0,8},{4,12},{8,0},{12,4},{1,9},{5,13},{9,1},{13,5},{2,10},{6,14},... | collective-permute-start | bytes 786440 | tf_op jit(solution)/shard_map/ppermute | solution.py:18
  7.1 8.8 %copy-start.5 = (bf16[1,512,2,128]{3,2,1,0:T(2,128)(2,1)S(1)}, bf16[1,512,2,128]{3,2,1,0:T(2,128)(2,1)}, u32[]{:S(2)}) copy-start(bf16[1,512,2,128]{3,2,1,0:T(2,128)(2,1)} %param.16) | copy-start | bytes 786436
  7.1 86.5 %collective-permute-start.4 = (bf16[1,1408,2,128]{3,2,1,0:T(2,128)(2,1)}, bf16[1,1408,2,128]{3,2,1,0:T(2,128)(2,1)S(1)}, u32[]{:S(2)}, u32[]{:S(2)}) collective-permute-start(bf16[1,1408,2,128]{3,2,1,0:T(2,128)(2,1)} %slice.17), channel_id=1, source_target_pairs={{0,8},{4,12},{8,0},{12,4},{1,9},{5,13},{9,1},{13,5},{2,10},{6,14},... | collective-permute-start | bytes 2162696 | tf_op jit(solution)/shard_map/ppermute | solution.py:18
  11.7 81.9 %collective-permute-start.5 = (bf16[1,384,2,128]{3,2,1,0:T(2,128)(2,1)}, bf16[1,384,2,128]{3,2,1,0:T(2,128)(2,1)S(1)}, u32[]{:S(2)}, u32[]{:S(2)}) collective-permute-start(bf16[1,384,2,128]{3,2,1,0:T(2,128)(2,1)} %slice.18), channel_id=1, source_target_pairs={{0,8},{4,12},{8,0},{12,4},{1,9},{5,13},{9,1},{13,5},{2,10},{6,14},... | collective-permute-start | bytes 589832 | tf_op jit(solution)/shard_map/ppermute | solution.py:18
  12.7 3.3 %copy-start.4 = (bf16[1,512,16,128]{3,2,1,0:T(8,128)(2,1)S(1)}, bf16[1,512,16,128]{3,2,1,0:T(8,128)(2,1)}, u32[]{:S(2)}) copy-start(bf16[1,512,16,128]{3,2,1,0:T(8,128)(2,1)} %param.14) | copy-start | bytes 6291460
  12.7 82.3 %collective-permute-start.2 = (bf16[1,128,2,128]{3,2,1,0:T(2,128)(2,1)S(1)}, bf16[1,128,2,128]{3,2,1,0:T(2,128)(2,1)S(1)}, u32[]{:S(2)}, u32[]{:S(2)}) collective-permute-start(bf16[1,128,2,128]{3,2,1,0:T(2,128)(2,1)S(1)} %slice.15), channel_id=1, source_target_pairs={{0,8},{4,12},{8,0},{12,4},{1,9},{5,13},{9,1},{13,5},{2,10},{6,14},... | collective-permute-start | bytes 196616 | tf_op jit(solution)/shard_map/ppermute | solution.py:18
  16.5 1.6 %copy-start.2 = (bf16[1,512,2048]{2,1,0:T(8,128)(2,1)S(1)}, bf16[1,512,2048]{2,1,0:T(8,128)(2,1)}, u32[]{:S(2)}) copy-start(bf16[1,512,2048]{2,1,0:T(8,128)(2,1)} %param.17) | copy-start | bytes 6291460
  18.1 38.7 %copy-start.11 = (bf16[2048]{0:T(1024)(128)(2,1)S(1)}, bf16[2048]{0:T(1024)(128)(2,1)}, u32[]{:S(2)}) copy-start(bf16[2048]{0:T(1024)(128)(2,1)} %param.23) | copy-start | bytes 12292
  48.7 1.9 %copy-start = (f32[512,2048]{1,0:T(8,128)}, f32[512,2048]{1,0:T(8,128)S(1)}, u32[]{:S(2)}) copy-start(f32[512,2048]{1,0:T(8,128)S(1)} %get-tuple-element.17) | copy-start | bytes 12582916
  56.7 4.1 %copy-start.7 = (bf16[1,2,32,16,128]{4,3,2,1,0:T(8,128)(2,1)S(1)}, bf16[1,2,32,16,128]{4,3,2,1,0:T(8,128)(2,1)}, u32[]{:S(2)}) copy-start(bf16[1,2,32,16,128]{4,3,2,1,0:T(8,128)(2,1)} %param.18) | copy-start | bytes 786436
  56.8 4.1 %copy-start.12 = (s32[1,32]{1,0:T(1,128)S(1)}, s32[1,32]{1,0:T(1,128)}, u32[]{:S(2)}) copy-start(s32[1,32]{1,0:T(1,128)} %param.22) | copy-start | bytes 388
  56.8 4.3 %copy-start.9 = (bf16[1,2,32,2,128]{4,3,2,1,0:T(2,128)(2,1)S(1)}, bf16[1,2,32,2,128]{4,3,2,1,0:T(2,128)(2,1)}, u32[]{:S(2)}) copy-start(bf16[1,2,32,2,128]{4,3,2,1,0:T(2,128)(2,1)} %param.19) | copy-start | bytes 98308
  56.8 4.3 %copy-start.10 = (bf16[1,2,32,2,128]{4,3,2,1,0:T(2,128)(2,1)S(1)}, bf16[1,2,32,2,128]{4,3,2,1,0:T(2,128)(2,1)}, u32[]{:S(2)}) copy-start(bf16[1,2,32,2,128]{4,3,2,1,0:T(2,128)(2,1)} %param.20) | copy-start | bytes 98308
  72.5 23.0 %collective-permute-start.3 = (bf16[1,128,2,128]{3,2,1,0:T(2,128)(2,1)S(1)}, bf16[1,128,2,128]{3,2,1,0:T(2,128)(2,1)S(1)}, u32[]{:S(2)}, u32[]{:S(2)}) collective-permute-start(bf16[1,128,2,128]{3,2,1,0:T(2,128)(2,1)S(1)} %slice.16), channel_id=1, source_target_pairs={{0,8},{4,12},{8,0},{12,4},{1,9},{5,13},{9,1},{13,5},{2,10},{6,14},... | collective-permute-start | bytes 196616 | tf_op jit(solution)/shard_map/ppermute | solution.py:18
  72.6 21.1 %copy-start.1 = (bf16[1,2,32,2048]{3,2,1,0:T(8,128)(2,1)S(1)}, bf16[1,2,32,2048]{3,2,1,0:T(8,128)(2,1)}, u32[]{:S(2)}) copy-start(bf16[1,2,32,2048]{3,2,1,0:T(8,128)(2,1)} %param.21) | copy-start | bytes 786436
  96.0 3.0 %collective-permute-start.6 = (f32[8,64]{1,0:T(8,128)S(1)}, f32[8,64]{1,0:T(8,128)S(1)}, u32[]{:S(2)}, u32[]{:S(2)}) collective-permute-start(f32[8,64]{1,0:T(8,128)S(1)} %get-tuple-element.28.refs_3_), channel_id=1, source_target_pairs={{0,3},{1,2},{2,1},{3,0},{4,7},{5,6},{6,5},{7,4},{8,11},{9,10},{10,... | collective-permute-start | bytes 6152 | tf_op jit(solution)/shard_map/ppermute | solution.py:26
  96.2 3.6 %collective-permute-start.7 = (f32[8,64]{1,0:T(8,128)S(1)}, f32[8,64]{1,0:T(8,128)S(1)}, u32[]{:S(2)}, u32[]{:S(2)}) collective-permute-start(f32[8,64]{1,0:T(8,128)S(1)} %get-tuple-element.28.refs_3_), channel_id=1, source_target_pairs={{0,2},{1,3},{2,0},{3,1},{4,6},{5,7},{6,4},{7,5},{8,10},{9,11},{10,... | collective-permute-start | bytes 6152 | tf_op jit(solution)/shard_map/ppermute | solution.py:26
  97.7 2.1 %collective-permute-start.8 = (f32[8,64]{1,0:T(8,128)S(1)}, f32[8,64]{1,0:T(8,128)S(1)}, u32[]{:S(2)}, u32[]{:S(2)}) collective-permute-start(f32[8,64]{1,0:T(8,128)S(1)} %get-tuple-element.28.refs_3_), channel_id=1, source_target_pairs={{0,1},{1,0},{2,3},{3,2},{4,5},{5,4},{6,7},{7,6},{8,9},{9,8},{10,11... | collective-permute-start | bytes 6152 | tf_op jit(solution)/shard_map/ppermute | solution.py:26

commit v5 on v4

--- a/solution.py
+++ b/solution.py
@@ -24,7 +24,7 @@
         return lax.psum(value, axis)
     others = [
         lax.ppermute(value, axis, [(i, i ^ step) for i in range(count)])
-        for step in (3, 2, 1)
+        for step in range(count - 1, 0, -1)
     ]
     return functools.reduce(jnp.add, others, value)
 

time: 101 us -> 101 us (level)
  no operation moved by 1% of the time
where the time goes in v5:
time: 101 us
  Pallas kernels  36.4 us (36%)
  waiting for transfers between devices  31 us (31%)
  starting transfers between devices  11.9 us (12%)
  local copies, waits for them, and re-layouts  9.34 us (9%)
  blocking collectives  5.96 us (6%)
  other arithmetic  5.15 us (5%)
    pallas_call x1, Pallas kernels, prefill(): pl.pallas_call(functools.partial(prefill_kernel, block=block, past=positi...  30.6 us
    ppermute x6, waiting for transfers between devices, from_behind(): return lax.ppermute(value, axis, pairs)  29.8 us
    ppermute x6, starting transfers between devices, from_behind(): return lax.ppermute(value, axis, pairs)  10 us
    psum x1, blocking collectives, local(): prefill_normed = normed(hidden, lax.psum(jnp.sum(squares, axis=1), 'tp'))  5.96 us
    convert_element_type x2, other arithmetic, normed(): return (hidden * scale[..., None] * gain_wide).astype(jnp.bfloat16)  4.77 us
    unnamed x33, local copies, waits for them, and re-layouts  4.27 us
    pallas_call x1, Pallas kernels, decode_scores(): pl.pallas_call(functools.partial(scores_kernel, steps=steps, early=early,...  3.3 us
    slice x2, local copies, waits for them, and re-layouts, received(): rows = prompt_values[:, start:stop]  3.12 us
  transfers between devices with their start and end apart: 9, of which 5 were waited for; matrix products, arithmetic and copies ran while one was open for 10% of the time, Pallas kernels for 36%

profile of v5, /device:TPU:0, one launch (start us, length us, event | category | flops | bytes accessed | tf_op | source)
XLA Modules:
  0.0 100.6 jit_solution(1464804230356879470)
XLA Ops:
  0.7 4.1 %collective-permute-start = (bf16[1,1536,2,128]{3,2,1,0:T(2,128)(2,1)}, bf16[1,1536,2,128]{3,2,1,0:T(2,128)(2,1)S(1)}, u32[]{:S(2)}, u32[]{:S(2)}) collective-permute-start(bf16[1,1536,2,128]{3,2,1,0:T(2,128)(2,1)} %param.12), channel_id=1, source_target_pairs={{0,8},{4,12},{8,0},{12,4},{1,9},{5,13},{9,1},{13,5},{2,10},{6,14},... | collective-permute-start | bytes 2359304 | tf_op jit(solution)/shard_map/ppermute | solution.py:18
  4.8 0.1 collective-permute-start.1
  4.9 2.2 %slice.17 = bf16[1,1408,2,128]{3,2,1,0:T(2,128)(2,1)} slice(bf16[1,1536,2,128]{3,2,1,0:T(2,128)(2,1)} %param.13), slice={[0:1], [0:1408], [0:2], [0:128]} | slice | bytes 1441792 | tf_op jit(solution)/shard_map/slice | solution.py:380
  7.1 2.8 %collective-permute-start.4 = (bf16[1,1408,2,128]{3,2,1,0:T(2,128)(2,1)}, bf16[1,1408,2,128]{3,2,1,0:T(2,128)(2,1)S(1)}, u32[]{:S(2)}, u32[]{:S(2)}) collective-permute-start(bf16[1,1408,2,128]{3,2,1,0:T(2,128)(2,1)} %slice.17), channel_id=1, source_target_pairs={{0,8},{4,12},{8,0},{12,4},{1,9},{5,13},{9,1},{13,5},{2,10},{6,14},... | collective-permute-start | bytes 2162696 | tf_op jit(solution)/shard_map/ppermute | solution.py:18
  10.0 1.7 %slice.18 = bf16[1,384,2,128]{3,2,1,0:T(2,128)(2,1)} slice(bf16[1,512,2,128]{3,2,1,0:T(2,128)(2,1)} %param.16), slice={[0:1], [0:384], [0:2], [0:128]} | slice | bytes 393216 | tf_op jit(solution)/shard_map/slice | solution.py:382
  11.7 0.1 collective-permute-start.5
  11.8 0.9 slice.15
  12.7 2.9 %collective-permute-start.2 = (bf16[1,128,2,128]{3,2,1,0:T(2,128)(2,1)S(1)}, bf16[1,128,2,128]{3,2,1,0:T(2,128)(2,1)S(1)}, u32[]{:S(2)}, u32[]{:S(2)}) collective-permute-start(bf16[1,128,2,128]{3,2,1,0:T(2,128)(2,1)S(1)} %slice.15), channel_id=1, source_target_pairs={{0,8},{4,12},{8,0},{12,4},{1,9},{5,13},{9,1},{13,5},{2,10},{6,14},... | collective-permute-start | bytes 196616 | tf_op jit(solution)/shard_map/ppermute | solution.py:18
  15.6 0.1 copy.33
  15.8 0.1 copy.32
  15.9 0.5 copy.31
  16.6 1.4 %copy-done.2 = bf16[1,512,2048]{2,1,0:T(8,128)(2,1)S(1)} copy-done((bf16[1,512,2048]{2,1,0:T(8,128)(2,1)S(1)}, bf16[1,512,2048]{2,1,0:T(8,128)(2,1)}, u32[]{:S(2)}) %copy-start.2) | copy-done | bytes 2097176
  18.1 30.6 %prefill.1 = (f32[512,2048]{1,0:T(8,128)S(1)}, f32[512,128]{1,0:T(8,128)S(1)}) custom-call(bf16[16,512,128]{2,1,0:T(8,128)(2,1)S(1)} %bitcast.47, bf16[2,2048,128]{2,1,0:T(8,128)(2,1)S(1)} %maximum_bitcast_fusion.k_ref, bf16[2,2048,128]{2,1,0:T(8,128)(2,1)S(1)} %maximum_bitcast_fusion.1.v_ref, bf16[512,2048]{1,0:T(8,128)(2,1)S(1)} %bitcast.58), custom_call_target="tpu_custom_call" | custom-call | flops 17179869184 | bytes 10485760 | tf_op jit(solution)/shard_map/prefill/pallas_call | solution.py:78
  48.7 1.9 %copy-done = f32[512,2048]{1,0:T(8,128)} copy-done((f32[512,2048]{1,0:T(8,128)}, f32[512,2048]{1,0:T(8,128)S(1)}, u32[]{:S(2)}) %copy-start) | copy-done | bytes 4194328
  50.6 0.1 reduce_sum.9
  50.8 6.0 %psum.7 = f32[512]{0:T(512)S(1)} all-reduce(f32[512]{0:T(512)S(1)} %reduce_sum.9), channel_id=1, replica_groups=mesh['groups'=2,'pair'=4,'tp'=4] {'tp'}, use_global_device_ids=true, to_apply=%region_1.0 | all-reduce | flops 512 | bytes 4096 | tf_op jit(solution)/shard_map/psum | solution.py:398
  56.8 3.9 %multiply_convert_fusion = bf16[512,2048]{1,0:T(8,128)(2,1)} fusion(f32[512,2048]{1,0:T(8,128)} %copy-done, f32[2048]{0:T(1024)S(1)} %convert_element_type.9, f32[512]{0:T(512)S(1)} %add_rsqrt_fusion), kind=kLoop, calls=%fused_computation | loop fusion | flops 3145728 | bytes 6301696 | tf_op jit(solution)/shard_map/convert_element_type | solution.py:392
  60.9 0.1 add_bitcast_fusion
  61.0 0.1 copy.24.cursor_ref
  61.1 11.4 %collective-permute-done.1 = bf16[1,512,2,128]{3,2,1,0:T(2,128)(2,1)S(1)} collective-permute-done((bf16[1,512,2,128]{3,2,1,0:T(2,128)(2,1)}, bf16[1,512,2,128]{3,2,1,0:T(2,128)(2,1)S(1)}, u32[]{:S(2)}, u32[]{:S(2)}) %collective-permute-start.1) | collective-permute-done | bytes 262176 | tf_op jit(solution)/shard_map/ppermute | solution.py:18
  72.6 3.3 %decode_scores.1 = (bf16[1024,1792]{1,0:T(8,128)(2,1)S(1)}, bf16[1024,256]{1,0:T(8,128)(2,1)S(1)}, bf16[1024,64]{1,0:T(8,128)(2,1)S(1)}, f32[1024,128]{1,0:T(8,128)S(1)}, bf16[4096,128]{1,0:T(8,128)(2,1)}) custom-call(bf16[16,64,128]{2,1,0:T(8,128)(2,1)S(1)} %bitcast.50, bf16[3072,128]{1,0:T(8,128)(2,1)S(1)} %bitcast.59, bf16[1024,128]{1,0:T(8,128)(2,1)S(1)} %bitcast.60, ...), custom_call_target="tpu_custom_call" | custom-call | flops 2147483648 | bytes 4194304 | tf_op jit(solution)/shard_map/decode_scores/pallas_call | solution.py:203
  75.9 17.7 %collective-permute-done.5 = bf16[1,384,2,128]{3,2,1,0:T(2,128)(2,1)S(1)} collective-permute-done((bf16[1,384,2,128]{3,2,1,0:T(2,128)(2,1)}, bf16[1,384,2,128]{3,2,1,0:T(2,128)(2,1)S(1)}, u32[]{:S(2)}, u32[]{:S(2)}) %collective-permute-start.5) | collective-permute-done | bytes 196640 | tf_op jit(solution)/shard_map/ppermute | solution.py:18
  93.6 1.3 %decode_mix.1 = (f32[64,2048]{1,0:T(8,128)S(1)}, bf16[4096,128]{1,0:T(8,128)(2,1)}) custom-call(bf16[1024,1792]{1,0:T(8,128)(2,1)S(1)} %get-tuple-element.22.refs_0_, bf16[1024,64]{1,0:T(8,128)(2,1)S(1)} %get-tuple-element.23.refs_1_, f32[1024,128]{1,0:T(8,128)S(1)} %get-tuple-element.24.refs_2_.refs_1_, bf16[2,64,128]{2,1,0:T(8,128)(2,1)S(1)} %bitcast.56, ...), custom_call_target="tpu_custom_call" | custom-call | flops 939524096 | bytes 3670016 | tf_op jit(solution)/shard_map/decode_mix/pallas_call | solution.py:256
  95.0 0.6 collective-permute-done.3
  95.6 0.5 decode_finish.1
  96.0 0.2 collective-permute-start.6
  96.2 1.5 %collective-permute-start.7 = (f32[8,64]{1,0:T(8,128)S(1)}, f32[8,64]{1,0:T(8,128)S(1)}, u32[]{:S(2)}, u32[]{:S(2)}) collective-permute-start(f32[8,64]{1,0:T(8,128)S(1)} %get-tuple-element.28.refs_3_), channel_id=1, source_target_pairs={{0,2},{1,3},{2,0},{3,1},{4,6},{5,7},{6,4},{7,5},{8,10},{9,11},{10,... | collective-permute-start | bytes 6152 | tf_op jit(solution)/shard_map/ppermute | solution.py:26
  97.7 0.3 collective-permute-start.8
  97.9 0.7 append.1
  98.6 0.5 collective-permute-done.6
  99.1 0.7 collective-permute-done.7
  99.8 0.8 multiply_convert_fusion.1
  (41 shorter events, 0.4 us)
Async XLA Ops:
  0.6 15.0 %copy-start.6 = (bf16[1,1536,2,128]{3,2,1,0:T(2,128)(2,1)S(1)}, bf16[1,1536,2,128]{3,2,1,0:T(2,128)(2,1)}, u32[]{:S(2)}) copy-start(bf16[1,1536,2,128]{3,2,1,0:T(2,128)(2,1)} %param.12) | copy-start | bytes 2359300
  0.6 15.1 %copy-start.8 = (bf16[1,512,2,128]{3,2,1,0:T(2,128)(2,1)S(1)}, bf16[1,512,2,128]{3,2,1,0:T(2,128)(2,1)}, u32[]{:S(2)}) copy-start(bf16[1,512,2,128]{3,2,1,0:T(2,128)(2,1)} %param.15) | copy-start | bytes 786436
  0.7 15.1 %copy-start.3 = (bf16[1,1536,2,128]{3,2,1,0:T(2,128)(2,1)S(1)}, bf16[1,1536,2,128]{3,2,1,0:T(2,128)(2,1)}, u32[]{:S(2)}) copy-start(bf16[1,1536,2,128]{3,2,1,0:T(2,128)(2,1)} %param.13) | copy-start | bytes 2359300
  0.7 71.9 %collective-permute-start = (bf16[1,1536,2,128]{3,2,1,0:T(2,128)(2,1)}, bf16[1,1536,2,128]{3,2,1,0:T(2,128)(2,1)S(1)}, u32[]{:S(2)}, u32[]{:S(2)}) collective-permute-start(bf16[1,1536,2,128]{3,2,1,0:T(2,128)(2,1)} %param.12), channel_id=1, source_target_pairs={{0,8},{4,12},{8,0},{12,4},{1,9},{5,13},{9,1},{13,5},{2,10},{6,14},... | collective-permute-start | bytes 2359304 | tf_op jit(solution)/shard_map/ppermute | solution.py:18
  4.8 67.8 %collective-permute-start.1 = (bf16[1,512,2,128]{3,2,1,0:T(2,128)(2,1)}, bf16[1,512,2,128]{3,2,1,0:T(2,128)(2,1)S(1)}, u32[]{:S(2)}, u32[]{:S(2)}) collective-permute-start(bf16[1,512,2,128]{3,2,1,0:T(2,128)(2,1)} %param.15), channel_id=1, source_target_pairs={{0,8},{4,12},{8,0},{12,4},{1,9},{5,13},{9,1},{13,5},{2,10},{6,14},... | collective-permute-start | bytes 786440 | tf_op jit(solution)/shard_map/ppermute | solution.py:18
  7.1 8.8 %copy-start.5 = (bf16[1,512,2,128]{3,2,1,0:T(2,128)(2,1)S(1)}, bf16[1,512,2,128]{3,2,1,0:T(2,128)(2,1)}, u32[]{:S(2)}) copy-start(bf16[1,512,2,128]{3,2,1,0:T(2,128)(2,1)} %param.16) | copy-start | bytes 786436
  7.1 86.5 %collective-permute-start.4 = (bf16[1,1408,2,128]{3,2,1,0:T(2,128)(2,1)}, bf16[1,1408,2,128]{3,2,1,0:T(2,128)(2,1)S(1)}, u32[]{:S(2)}, u32[]{:S(2)}) collective-permute-start(bf16[1,1408,2,128]{3,2,1,0:T(2,128)(2,1)} %slice.17), channel_id=1, source_target_pairs={{0,8},{4,12},{8,0},{12,4},{1,9},{5,13},{9,1},{13,5},{2,10},{6,14},... | collective-permute-start | bytes 2162696 | tf_op jit(solution)/shard_map/ppermute | solution.py:18
  11.7 81.9 %collective-permute-start.5 = (bf16[1,384,2,128]{3,2,1,0:T(2,128)(2,1)}, bf16[1,384,2,128]{3,2,1,0:T(2,128)(2,1)S(1)}, u32[]{:S(2)}, u32[]{:S(2)}) collective-permute-start(bf16[1,384,2,128]{3,2,1,0:T(2,128)(2,1)} %slice.18), channel_id=1, source_target_pairs={{0,8},{4,12},{8,0},{12,4},{1,9},{5,13},{9,1},{13,5},{2,10},{6,14},... | collective-permute-start | bytes 589832 | tf_op jit(solution)/shard_map/ppermute | solution.py:18
  12.7 3.3 %copy-start.4 = (bf16[1,512,16,128]{3,2,1,0:T(8,128)(2,1)S(1)}, bf16[1,512,16,128]{3,2,1,0:T(8,128)(2,1)}, u32[]{:S(2)}) copy-start(bf16[1,512,16,128]{3,2,1,0:T(8,128)(2,1)} %param.14) | copy-start | bytes 6291460
  12.7 82.3 %collective-permute-start.2 = (bf16[1,128,2,128]{3,2,1,0:T(2,128)(2,1)S(1)}, bf16[1,128,2,128]{3,2,1,0:T(2,128)(2,1)S(1)}, u32[]{:S(2)}, u32[]{:S(2)}) collective-permute-start(bf16[1,128,2,128]{3,2,1,0:T(2,128)(2,1)S(1)} %slice.15), channel_id=1, source_target_pairs={{0,8},{4,12},{8,0},{12,4},{1,9},{5,13},{9,1},{13,5},{2,10},{6,14},... | collective-permute-start | bytes 196616 | tf_op jit(solution)/shard_map/ppermute | solution.py:18
  16.5 1.6 %copy-start.2 = (bf16[1,512,2048]{2,1,0:T(8,128)(2,1)S(1)}, bf16[1,512,2048]{2,1,0:T(8,128)(2,1)}, u32[]{:S(2)}) copy-start(bf16[1,512,2048]{2,1,0:T(8,128)(2,1)} %param.17) | copy-start | bytes 6291460
  18.1 38.7 %copy-start.11 = (bf16[2048]{0:T(1024)(128)(2,1)S(1)}, bf16[2048]{0:T(1024)(128)(2,1)}, u32[]{:S(2)}) copy-start(bf16[2048]{0:T(1024)(128)(2,1)} %param.23) | copy-start | bytes 12292
  48.7 1.9 %copy-start = (f32[512,2048]{1,0:T(8,128)}, f32[512,2048]{1,0:T(8,128)S(1)}, u32[]{:S(2)}) copy-start(f32[512,2048]{1,0:T(8,128)S(1)} %get-tuple-element.17) | copy-start | bytes 12582916
  56.7 4.1 %copy-start.7 = (bf16[1,2,32,16,128]{4,3,2,1,0:T(8,128)(2,1)S(1)}, bf16[1,2,32,16,128]{4,3,2,1,0:T(8,128)(2,1)}, u32[]{:S(2)}) copy-start(bf16[1,2,32,16,128]{4,3,2,1,0:T(8,128)(2,1)} %param.18) | copy-start | bytes 786436
  56.8 4.1 %copy-start.12 = (s32[1,32]{1,0:T(1,128)S(1)}, s32[1,32]{1,0:T(1,128)}, u32[]{:S(2)}) copy-start(s32[1,32]{1,0:T(1,128)} %param.22) | copy-start | bytes 388
  56.8 4.3 %copy-start.9 = (bf16[1,2,32,2,128]{4,3,2,1,0:T(2,128)(2,1)S(1)}, bf16[1,2,32,2,128]{4,3,2,1,0:T(2,128)(2,1)}, u32[]{:S(2)}) copy-start(bf16[1,2,32,2,128]{4,3,2,1,0:T(2,128)(2,1)} %param.19) | copy-start | bytes 98308
  56.8 4.3 %copy-start.10 = (bf16[1,2,32,2,128]{4,3,2,1,0:T(2,128)(2,1)S(1)}, bf16[1,2,32,2,128]{4,3,2,1,0:T(2,128)(2,1)}, u32[]{:S(2)}) copy-start(bf16[1,2,32,2,128]{4,3,2,1,0:T(2,128)(2,1)} %param.20) | copy-start | bytes 98308
  72.5 23.0 %collective-permute-start.3 = (bf16[1,128,2,128]{3,2,1,0:T(2,128)(2,1)S(1)}, bf16[1,128,2,128]{3,2,1,0:T(2,128)(2,1)S(1)}, u32[]{:S(2)}, u32[]{:S(2)}) collective-permute-start(bf16[1,128,2,128]{3,2,1,0:T(2,128)(2,1)S(1)} %slice.16), channel_id=1, source_target_pairs={{0,8},{4,12},{8,0},{12,4},{1,9},{5,13},{9,1},{13,5},{2,10},{6,14},... | collective-permute-start | bytes 196616 | tf_op jit(solution)/shard_map/ppermute | solution.py:18
  72.6 21.1 %copy-start.1 = (bf16[1,2,32,2048]{3,2,1,0:T(8,128)(2,1)S(1)}, bf16[1,2,32,2048]{3,2,1,0:T(8,128)(2,1)}, u32[]{:S(2)}) copy-start(bf16[1,2,32,2048]{3,2,1,0:T(8,128)(2,1)} %param.21) | copy-start | bytes 786436
  96.0 3.0 %collective-permute-start.6 = (f32[8,64]{1,0:T(8,128)S(1)}, f32[8,64]{1,0:T(8,128)S(1)}, u32[]{:S(2)}, u32[]{:S(2)}) collective-permute-start(f32[8,64]{1,0:T(8,128)S(1)} %get-tuple-element.28.refs_3_), channel_id=1, source_target_pairs={{0,3},{1,2},{2,1},{3,0},{4,7},{5,6},{6,5},{7,4},{8,11},{9,10},{10,... | collective-permute-start | bytes 6152 | tf_op jit(solution)/shard_map/ppermute | solution.py:26
  96.2 3.6 %collective-permute-start.7 = (f32[8,64]{1,0:T(8,128)S(1)}, f32[8,64]{1,0:T(8,128)S(1)}, u32[]{:S(2)}, u32[]{:S(2)}) collective-permute-start(f32[8,64]{1,0:T(8,128)S(1)} %get-tuple-element.28.refs_3_), channel_id=1, source_target_pairs={{0,2},{1,3},{2,0},{3,1},{4,6},{5,7},{6,4},{7,5},{8,10},{9,11},{10,... | collective-permute-start | bytes 6152 | tf_op jit(solution)/shard_map/ppermute | solution.py:26
  97.7 2.1 %collective-permute-start.8 = (f32[8,64]{1,0:T(8,128)S(1)}, f32[8,64]{1,0:T(8,128)S(1)}, u32[]{:S(2)}, u32[]{:S(2)}) collective-permute-start(f32[8,64]{1,0:T(8,128)S(1)} %get-tuple-element.28.refs_3_), channel_id=1, source_target_pairs={{0,1},{1,0},{2,3},{3,2},{4,5},{5,4},{6,7},{7,6},{8,9},{9,8},{10,11... | collective-permute-start | bytes 6152 | tf_op jit(solution)/shard_map/ppermute | solution.py:26

commit v6 on v5

--- a/solution.py
+++ b/solution.py
@@ -151,15 +151,15 @@
         far = jnp.exp2((far - top) * factor)
         own = jnp.exp2((own - top) * factor)
         total = jnp.sum(far, axis=1, keepdims=True) + jnp.sum(own, axis=1, keepdims=True)
-        far = far.astype(jnp.bfloat16)
-        for p_ref, chunks in ((p_old_ref, early), (p_new_ref, late)):
+        inverse = 1.0 / total
+        for p_ref, chunks, factor_of in ((p_old_ref, early, 1.0), (p_new_ref, late, inverse)):
             first_column = 0
             for start, stop in chunks:
                 columns = slice(first_column, first_column + stop - start)
-                p_ref[here, columns] = far[:, start:stop]
+                p_ref[here, columns] = (far[:, start:stop] * factor_of).astype(jnp.bfloat16)
                 first_column = columns.stop
         p_own_ref[here] = own.astype(jnp.bfloat16)
-        inverse_ref[here] = jnp.broadcast_to(1.0 / total, (block, head_size))
+        inverse_ref[here] = jnp.broadcast_to(inverse, (block, head_size))
     for copy in copies:
         copy.wait()
 
@@ -277,9 +277,9 @@
 
 
 def finish_kernel(*refs, late):
-    p_new_ref, inverse_ref, base_ref = refs[:3]
-    chunk_refs = refs[3 : 3 + len(late)]
-    hidden_ref, squares_ref, wide_ref, values_ref = refs[3 + len(late) :]
+    p_new_ref, base_ref = refs[:2]
+    chunk_refs = refs[2 : 2 + len(late)]
+    hidden_ref, squares_ref, wide_ref, values_ref = refs[2 + len(late) :]
     rows = base_ref.shape[0]
     key_heads, _, head_size = values_ref.shape
     heads = p_new_ref.shape[0] // rows
@@ -289,7 +289,6 @@
     for g in range(key_heads):
         here = slice(g * per * rows, (g + 1) * per * rows)
         mixed = jnp.dot(p_new_ref[here], values_ref[g], preferred_element_type=jnp.float32)
-        mixed *= inverse_ref[here]
         for h in range(per):
             lanes = slice((g * per + h) * head_size, (g * per + h + 1) * head_size)
             hidden = mixed[h * rows : (h + 1) * rows] + base_ref[:, lanes]
@@ -299,13 +298,13 @@
     squares_ref[...] = jnp.transpose(squares)[:8]
 
 
-def decode_finish(p_new, inverse, base, chunk_values, late):
+def decode_finish(p_new, base, chunk_values, late):
     rows, features = base.shape
     most, head_size = max(x.shape for x in chunk_values)
     key_heads = sum(x.shape[0] for x in chunk_values) // length(late)
     return pl.pallas_call(
         functools.partial(finish_kernel, late=late),
-        in_specs=[VMEM] * (3 + len(late)),
+        in_specs=[VMEM] * (2 + len(late)),
         out_specs=[VMEM] * 2,
         out_shape=[
             jax.ShapeDtypeStruct((rows, features), jnp.float32),
@@ -322,7 +321,7 @@
             bytes_accessed=2 * p_new.shape[0] * p_new.shape[1],
         ),
         name="decode_finish",
-    )(p_new, inverse, base, *chunk_values)
+    )(p_new, base, *chunk_values)
 
 
 def append_kernel(*refs, late):
@@ -419,7 +418,7 @@
         p_old, p_own, inverse, own_values, decode_residual[0].reshape(rows, -1),
         early_values, early, positions,
     )
-    hidden, squares = decode_finish(p_new, inverse, base, late_values, late)
+    hidden, squares = decode_finish(p_new, base, late_values, late)
     handed_values = append(part, late_values, late, squares)
     squares = sum_over(squares, "tp")
     decode_normed = normed(hidden, squares[0]).reshape(decode_residual.shape)

time: 101 us -> 101 us (level)
  no operation moved by 1% of the time
where the time goes in v6:
time: 101 us
  Pallas kernels  36.4 us (36%)
  waiting for transfers between devices  31 us (31%)
  starting transfers between devices  11.9 us (12%)
  local copies, waits for them, and re-layouts  9.34 us (9%)
  blocking collectives  5.96 us (6%)
  other arithmetic  5.15 us (5%)
    pallas_call x1, Pallas kernels, prefill(): pl.pallas_call(functools.partial(prefill_kernel, block=block, past=positi...  30.6 us
    ppermute x6, waiting for transfers between devices, from_behind(): return lax.ppermute(value, axis, pairs)  29.7 us
    ppermute x6, starting transfers between devices, from_behind(): return lax.ppermute(value, axis, pairs)  10 us
    psum x1, blocking collectives, local(): prefill_normed = normed(hidden, lax.psum(jnp.sum(squares, axis=1), 'tp'))  5.96 us
    convert_element_type x2, other arithmetic, normed(): return (hidden * scale[..., None] * gain_wide).astype(jnp.bfloat16)  4.77 us
    unnamed x33, local copies, waits for them, and re-layouts  4.27 us
    pallas_call x1, Pallas kernels, decode_scores(): pl.pallas_call(functools.partial(scores_kernel, steps=steps, early=early,...  3.34 us
    slice x2, local copies, waits for them, and re-layouts, received(): rows = prompt_values[:, start:stop]  3.12 us
  transfers between devices with their start and end apart: 9, of which 5 were waited for; matrix products, arithmetic and copies ran while one was open for 10% of the time, Pallas kernels for 36%

profile of v6, /device:TPU:0, one launch (start us, length us, event | category | flops | bytes accessed | tf_op | source)
XLA Modules:
  0.0 100.6 jit_solution(11146786397500423339)
XLA Ops:
  0.7 4.1 %collective-permute-start = (bf16[1,1536,2,128]{3,2,1,0:T(2,128)(2,1)}, bf16[1,1536,2,128]{3,2,1,0:T(2,128)(2,1)S(1)}, u32[]{:S(2)}, u32[]{:S(2)}) collective-permute-start(bf16[1,1536,2,128]{3,2,1,0:T(2,128)(2,1)} %param.12), channel_id=1, source_target_pairs={{0,8},{4,12},{8,0},{12,4},{1,9},{5,13},{9,1},{13,5},{2,10},{6,14},... | collective-permute-start | bytes 2359304 | tf_op jit(solution)/shard_map/ppermute | solution.py:18
  4.8 0.1 collective-permute-start.1
  4.9 2.2 %slice.17 = bf16[1,1408,2,128]{3,2,1,0:T(2,128)(2,1)} slice(bf16[1,1536,2,128]{3,2,1,0:T(2,128)(2,1)} %param.13), slice={[0:1], [0:1408], [0:2], [0:128]} | slice | bytes 1441792 | tf_op jit(solution)/shard_map/slice | solution.py:379
  7.1 2.8 %collective-permute-start.4 = (bf16[1,1408,2,128]{3,2,1,0:T(2,128)(2,1)}, bf16[1,1408,2,128]{3,2,1,0:T(2,128)(2,1)S(1)}, u32[]{:S(2)}, u32[]{:S(2)}) collective-permute-start(bf16[1,1408,2,128]{3,2,1,0:T(2,128)(2,1)} %slice.17), channel_id=1, source_target_pairs={{0,8},{4,12},{8,0},{12,4},{1,9},{5,13},{9,1},{13,5},{2,10},{6,14},... | collective-permute-start | bytes 2162696 | tf_op jit(solution)/shard_map/ppermute | solution.py:18
  10.0 1.7 %slice.18 = bf16[1,384,2,128]{3,2,1,0:T(2,128)(2,1)} slice(bf16[1,512,2,128]{3,2,1,0:T(2,128)(2,1)} %param.16), slice={[0:1], [0:384], [0:2], [0:128]} | slice | bytes 393216 | tf_op jit(solution)/shard_map/slice | solution.py:381
  11.7 0.1 collective-permute-start.5
  11.8 0.9 slice.15
  12.7 2.9 %collective-permute-start.2 = (bf16[1,128,2,128]{3,2,1,0:T(2,128)(2,1)S(1)}, bf16[1,128,2,128]{3,2,1,0:T(2,128)(2,1)S(1)}, u32[]{:S(2)}, u32[]{:S(2)}) collective-permute-start(bf16[1,128,2,128]{3,2,1,0:T(2,128)(2,1)S(1)} %slice.15), channel_id=1, source_target_pairs={{0,8},{4,12},{8,0},{12,4},{1,9},{5,13},{9,1},{13,5},{2,10},{6,14},... | collective-permute-start | bytes 196616 | tf_op jit(solution)/shard_map/ppermute | solution.py:18
  15.6 0.1 copy.33
  15.8 0.1 copy.32
  15.9 0.5 copy.31
  16.6 1.4 %copy-done.2 = bf16[1,512,2048]{2,1,0:T(8,128)(2,1)S(1)} copy-done((bf16[1,512,2048]{2,1,0:T(8,128)(2,1)S(1)}, bf16[1,512,2048]{2,1,0:T(8,128)(2,1)}, u32[]{:S(2)}) %copy-start.2) | copy-done | bytes 2097176
  18.1 30.6 %prefill.1 = (f32[512,2048]{1,0:T(8,128)S(1)}, f32[512,128]{1,0:T(8,128)S(1)}) custom-call(bf16[16,512,128]{2,1,0:T(8,128)(2,1)S(1)} %bitcast.47, bf16[2,2048,128]{2,1,0:T(8,128)(2,1)S(1)} %maximum_bitcast_fusion.k_ref, bf16[2,2048,128]{2,1,0:T(8,128)(2,1)S(1)} %maximum_bitcast_fusion.1.v_ref, bf16[512,2048]{1,0:T(8,128)(2,1)S(1)} %bitcast.58), custom_call_target="tpu_custom_call" | custom-call | flops 17179869184 | bytes 10485760 | tf_op jit(solution)/shard_map/prefill/pallas_call | solution.py:78
  48.7 1.9 %copy-done = f32[512,2048]{1,0:T(8,128)} copy-done((f32[512,2048]{1,0:T(8,128)}, f32[512,2048]{1,0:T(8,128)S(1)}, u32[]{:S(2)}) %copy-start) | copy-done | bytes 4194328
  50.6 0.1 reduce_sum.9
  50.8 6.0 %psum.7 = f32[512]{0:T(512)S(1)} all-reduce(f32[512]{0:T(512)S(1)} %reduce_sum.9), channel_id=1, replica_groups=mesh['groups'=2,'pair'=4,'tp'=4] {'tp'}, use_global_device_ids=true, to_apply=%region_1.0 | all-reduce | flops 512 | bytes 4096 | tf_op jit(solution)/shard_map/psum | solution.py:397
  56.8 3.9 %multiply_convert_fusion = bf16[512,2048]{1,0:T(8,128)(2,1)} fusion(f32[512,2048]{1,0:T(8,128)} %copy-done, f32[2048]{0:T(1024)S(1)} %convert_element_type.9, f32[512]{0:T(512)S(1)} %add_rsqrt_fusion), kind=kLoop, calls=%fused_computation | loop fusion | flops 3145728 | bytes 6301696 | tf_op jit(solution)/shard_map/convert_element_type | solution.py:391
  60.9 0.1 add_bitcast_fusion
  61.0 0.1 copy.24.cursor_ref
  61.1 11.4 %collective-permute-done.1 = bf16[1,512,2,128]{3,2,1,0:T(2,128)(2,1)S(1)} collective-permute-done((bf16[1,512,2,128]{3,2,1,0:T(2,128)(2,1)}, bf16[1,512,2,128]{3,2,1,0:T(2,128)(2,1)S(1)}, u32[]{:S(2)}, u32[]{:S(2)}) %collective-permute-start.1) | collective-permute-done | bytes 262176 | tf_op jit(solution)/shard_map/ppermute | solution.py:18
  72.6 3.3 %decode_scores.1 = (bf16[1024,1792]{1,0:T(8,128)(2,1)S(1)}, bf16[1024,256]{1,0:T(8,128)(2,1)S(1)}, bf16[1024,64]{1,0:T(8,128)(2,1)S(1)}, f32[1024,128]{1,0:T(8,128)S(1)}, bf16[4096,128]{1,0:T(8,128)(2,1)}) custom-call(bf16[16,64,128]{2,1,0:T(8,128)(2,1)S(1)} %bitcast.54, bf16[3072,128]{1,0:T(8,128)(2,1)S(1)} %bitcast.59, bf16[1024,128]{1,0:T(8,128)(2,1)S(1)} %bitcast.60, ...), custom_call_target="tpu_custom_call" | custom-call | flops 2147483648 | bytes 4194304 | tf_op jit(solution)/shard_map/decode_scores/pallas_call | solution.py:203
  75.9 17.7 %collective-permute-done.5 = bf16[1,384,2,128]{3,2,1,0:T(2,128)(2,1)S(1)} collective-permute-done((bf16[1,384,2,128]{3,2,1,0:T(2,128)(2,1)}, bf16[1,384,2,128]{3,2,1,0:T(2,128)(2,1)S(1)}, u32[]{:S(2)}, u32[]{:S(2)}) %collective-permute-start.5) | collective-permute-done | bytes 196640 | tf_op jit(solution)/shard_map/ppermute | solution.py:18
  93.6 1.3 %decode_mix.1 = (f32[64,2048]{1,0:T(8,128)S(1)}, bf16[4096,128]{1,0:T(8,128)(2,1)}) custom-call(bf16[1024,1792]{1,0:T(8,128)(2,1)S(1)} %get-tuple-element.22.refs_0_, bf16[1024,64]{1,0:T(8,128)(2,1)S(1)} %get-tuple-element.23.refs_1_, f32[1024,128]{1,0:T(8,128)S(1)} %get-tuple-element.24.refs_2_, bf16[2,64,128]{2,1,0:T(8,128)(2,1)S(1)} %bitcast.56, ...), custom_call_target="tpu_custom_call" | custom-call | flops 939524096 | bytes 3670016 | tf_op jit(solution)/shard_map/decode_mix/pallas_call | solution.py:256
  95.0 0.6 collective-permute-done.3
  95.6 0.5 decode_finish.1
  96.0 0.2 collective-permute-start.6
  96.2 1.5 %collective-permute-start.7 = (f32[8,64]{1,0:T(8,128)S(1)}, f32[8,64]{1,0:T(8,128)S(1)}, u32[]{:S(2)}, u32[]{:S(2)}) collective-permute-start(f32[8,64]{1,0:T(8,128)S(1)} %get-tuple-element.28.refs_3_), channel_id=1, source_target_pairs={{0,2},{1,3},{2,0},{3,1},{4,6},{5,7},{6,4},{7,5},{8,10},{9,11},{10,... | collective-permute-start | bytes 6152 | tf_op jit(solution)/shard_map/ppermute | solution.py:26
  97.6 0.3 collective-permute-start.8
  97.9 0.7 append.1
  98.6 0.5 collective-permute-done.6
  99.1 0.7 collective-permute-done.7
  99.8 0.8 multiply_convert_fusion.1
  (41 shorter events, 0.4 us)
Async XLA Ops:
  0.6 15.0 %copy-start.6 = (bf16[1,1536,2,128]{3,2,1,0:T(2,128)(2,1)S(1)}, bf16[1,1536,2,128]{3,2,1,0:T(2,128)(2,1)}, u32[]{:S(2)}) copy-start(bf16[1,1536,2,128]{3,2,1,0:T(2,128)(2,1)} %param.12) | copy-start | bytes 2359300
  0.6 15.1 %copy-start.8 = (bf16[1,512,2,128]{3,2,1,0:T(2,128)(2,1)S(1)}, bf16[1,512,2,128]{3,2,1,0:T(2,128)(2,1)}, u32[]{:S(2)}) copy-start(bf16[1,512,2,128]{3,2,1,0:T(2,128)(2,1)} %param.15) | copy-start | bytes 786436
  0.7 15.1 %copy-start.3 = (bf16[1,1536,2,128]{3,2,1,0:T(2,128)(2,1)S(1)}, bf16[1,1536,2,128]{3,2,1,0:T(2,128)(2,1)}, u32[]{:S(2)}) copy-start(bf16[1,1536,2,128]{3,2,1,0:T(2,128)(2,1)} %param.13) | copy-start | bytes 2359300
  0.7 71.9 %collective-permute-start = (bf16[1,1536,2,128]{3,2,1,0:T(2,128)(2,1)}, bf16[1,1536,2,128]{3,2,1,0:T(2,128)(2,1)S(1)}, u32[]{:S(2)}, u32[]{:S(2)}) collective-permute-start(bf16[1,1536,2,128]{3,2,1,0:T(2,128)(2,1)} %param.12), channel_id=1, source_target_pairs={{0,8},{4,12},{8,0},{12,4},{1,9},{5,13},{9,1},{13,5},{2,10},{6,14},... | collective-permute-start | bytes 2359304 | tf_op jit(solution)/shard_map/ppermute | solution.py:18
  4.8 67.8 %collective-permute-start.1 = (bf16[1,512,2,128]{3,2,1,0:T(2,128)(2,1)}, bf16[1,512,2,128]{3,2,1,0:T(2,128)(2,1)S(1)}, u32[]{:S(2)}, u32[]{:S(2)}) collective-permute-start(bf16[1,512,2,128]{3,2,1,0:T(2,128)(2,1)} %param.15), channel_id=1, source_target_pairs={{0,8},{4,12},{8,0},{12,4},{1,9},{5,13},{9,1},{13,5},{2,10},{6,14},... | collective-permute-start | bytes 786440 | tf_op jit(solution)/shard_map/ppermute | solution.py:18
  7.1 8.8 %copy-start.5 = (bf16[1,512,2,128]{3,2,1,0:T(2,128)(2,1)S(1)}, bf16[1,512,2,128]{3,2,1,0:T(2,128)(2,1)}, u32[]{:S(2)}) copy-start(bf16[1,512,2,128]{3,2,1,0:T(2,128)(2,1)} %param.16) | copy-start | bytes 786436
  7.1 86.5 %collective-permute-start.4 = (bf16[1,1408,2,128]{3,2,1,0:T(2,128)(2,1)}, bf16[1,1408,2,128]{3,2,1,0:T(2,128)(2,1)S(1)}, u32[]{:S(2)}, u32[]{:S(2)}) collective-permute-start(bf16[1,1408,2,128]{3,2,1,0:T(2,128)(2,1)} %slice.17), channel_id=1, source_target_pairs={{0,8},{4,12},{8,0},{12,4},{1,9},{5,13},{9,1},{13,5},{2,10},{6,14},... | collective-permute-start | bytes 2162696 | tf_op jit(solution)/shard_map/ppermute | solution.py:18
  11.7 81.9 %collective-permute-start.5 = (bf16[1,384,2,128]{3,2,1,0:T(2,128)(2,1)}, bf16[1,384,2,128]{3,2,1,0:T(2,128)(2,1)S(1)}, u32[]{:S(2)}, u32[]{:S(2)}) collective-permute-start(bf16[1,384,2,128]{3,2,1,0:T(2,128)(2,1)} %slice.18), channel_id=1, source_target_pairs={{0,8},{4,12},{8,0},{12,4},{1,9},{5,13},{9,1},{13,5},{2,10},{6,14},... | collective-permute-start | bytes 589832 | tf_op jit(solution)/shard_map/ppermute | solution.py:18
  12.7 3.3 %copy-start.4 = (bf16[1,512,16,128]{3,2,1,0:T(8,128)(2,1)S(1)}, bf16[1,512,16,128]{3,2,1,0:T(8,128)(2,1)}, u32[]{:S(2)}) copy-start(bf16[1,512,16,128]{3,2,1,0:T(8,128)(2,1)} %param.14) | copy-start | bytes 6291460
  12.7 82.3 %collective-permute-start.2 = (bf16[1,128,2,128]{3,2,1,0:T(2,128)(2,1)S(1)}, bf16[1,128,2,128]{3,2,1,0:T(2,128)(2,1)S(1)}, u32[]{:S(2)}, u32[]{:S(2)}) collective-permute-start(bf16[1,128,2,128]{3,2,1,0:T(2,128)(2,1)S(1)} %slice.15), channel_id=1, source_target_pairs={{0,8},{4,12},{8,0},{12,4},{1,9},{5,13},{9,1},{13,5},{2,10},{6,14},... | collective-permute-start | bytes 196616 | tf_op jit(solution)/shard_map/ppermute | solution.py:18
  16.5 1.6 %copy-start.2 = (bf16[1,512,2048]{2,1,0:T(8,128)(2,1)S(1)}, bf16[1,512,2048]{2,1,0:T(8,128)(2,1)}, u32[]{:S(2)}) copy-start(bf16[1,512,2048]{2,1,0:T(8,128)(2,1)} %param.17) | copy-start | bytes 6291460
  18.1 38.7 %copy-start.11 = (bf16[2048]{0:T(1024)(128)(2,1)S(1)}, bf16[2048]{0:T(1024)(128)(2,1)}, u32[]{:S(2)}) copy-start(bf16[2048]{0:T(1024)(128)(2,1)} %param.23) | copy-start | bytes 12292
  48.7 1.9 %copy-start = (f32[512,2048]{1,0:T(8,128)}, f32[512,2048]{1,0:T(8,128)S(1)}, u32[]{:S(2)}) copy-start(f32[512,2048]{1,0:T(8,128)S(1)} %get-tuple-element.17) | copy-start | bytes 12582916
  56.7 4.1 %copy-start.7 = (bf16[1,2,32,16,128]{4,3,2,1,0:T(8,128)(2,1)S(1)}, bf16[1,2,32,16,128]{4,3,2,1,0:T(8,128)(2,1)}, u32[]{:S(2)}) copy-start(bf16[1,2,32,16,128]{4,3,2,1,0:T(8,128)(2,1)} %param.18) | copy-start | bytes 786436
  56.8 4.1 %copy-start.12 = (s32[1,32]{1,0:T(1,128)S(1)}, s32[1,32]{1,0:T(1,128)}, u32[]{:S(2)}) copy-start(s32[1,32]{1,0:T(1,128)} %param.22) | copy-start | bytes 388
  56.8 4.3 %copy-start.9 = (bf16[1,2,32,2,128]{4,3,2,1,0:T(2,128)(2,1)S(1)}, bf16[1,2,32,2,128]{4,3,2,1,0:T(2,128)(2,1)}, u32[]{:S(2)}) copy-start(bf16[1,2,32,2,128]{4,3,2,1,0:T(2,128)(2,1)} %param.19) | copy-start | bytes 98308
  56.8 4.3 %copy-start.10 = (bf16[1,2,32,2,128]{4,3,2,1,0:T(2,128)(2,1)S(1)}, bf16[1,2,32,2,128]{4,3,2,1,0:T(2,128)(2,1)}, u32[]{:S(2)}) copy-start(bf16[1,2,32,2,128]{4,3,2,1,0:T(2,128)(2,1)} %param.20) | copy-start | bytes 98308
  72.5 23.0 %collective-permute-start.3 = (bf16[1,128,2,128]{3,2,1,0:T(2,128)(2,1)S(1)}, bf16[1,128,2,128]{3,2,1,0:T(2,128)(2,1)S(1)}, u32[]{:S(2)}, u32[]{:S(2)}) collective-permute-start(bf16[1,128,2,128]{3,2,1,0:T(2,128)(2,1)S(1)} %slice.16), channel_id=1, source_target_pairs={{0,8},{4,12},{8,0},{12,4},{1,9},{5,13},{9,1},{13,5},{2,10},{6,14},... | collective-permute-start | bytes 196616 | tf_op jit(solution)/shard_map/ppermute | solution.py:18
  72.6 21.1 %copy-start.1 = (bf16[1,2,32,2048]{3,2,1,0:T(8,128)(2,1)S(1)}, bf16[1,2,32,2048]{3,2,1,0:T(8,128)(2,1)}, u32[]{:S(2)}) copy-start(bf16[1,2,32,2048]{3,2,1,0:T(8,128)(2,1)} %param.21) | copy-start | bytes 786436
  96.0 3.0 %collective-permute-start.6 = (f32[8,64]{1,0:T(8,128)S(1)}, f32[8,64]{1,0:T(8,128)S(1)}, u32[]{:S(2)}, u32[]{:S(2)}) collective-permute-start(f32[8,64]{1,0:T(8,128)S(1)} %get-tuple-element.28.refs_3_), channel_id=1, source_target_pairs={{0,3},{1,2},{2,1},{3,0},{4,7},{5,6},{6,5},{7,4},{8,11},{9,10},{10,... | collective-permute-start | bytes 6152 | tf_op jit(solution)/shard_map/ppermute | solution.py:26
  96.2 3.6 %collective-permute-start.7 = (f32[8,64]{1,0:T(8,128)S(1)}, f32[8,64]{1,0:T(8,128)S(1)}, u32[]{:S(2)}, u32[]{:S(2)}) collective-permute-start(f32[8,64]{1,0:T(8,128)S(1)} %get-tuple-element.28.refs_3_), channel_id=1, source_target_pairs={{0,2},{1,3},{2,0},{3,1},{4,6},{5,7},{6,4},{7,5},{8,10},{9,11},{10,... | collective-permute-start | bytes 6152 | tf_op jit(solution)/shard_map/ppermute | solution.py:26
  97.6 2.1 %collective-permute-start.8 = (f32[8,64]{1,0:T(8,128)S(1)}, f32[8,64]{1,0:T(8,128)S(1)}, u32[]{:S(2)}, u32[]{:S(2)}) collective-permute-start(f32[8,64]{1,0:T(8,128)S(1)} %get-tuple-element.28.refs_3_), channel_id=1, source_target_pairs={{0,1},{1,0},{2,3},{3,2},{4,5},{5,4},{6,7},{7,6},{8,9},{9,8},{10,11... | collective-permute-start | bytes 6152 | tf_op jit(solution)/shard_map/ppermute | solution.py:26
